TPU v7x, 32 devices: a whole 2x2x4 slice. The times are simulated.
32 devices in a mesh: gx: 4 (over y, x), gy: 4 (over z), gz: 2 (over core).
Axes of the slice: x: 2, y: 2, z: 4, core: 2. Of those that a mesh axis runs over, the one named last changes fastest.
Arguments:
- element_load: float32 [36, 36, 18, 128], P('gx', 'gy', 'gz'), may hold values from -90 to 90
- local_matrix: float32 [4, 4, 2, 729, 729], P('gx', 'gy', 'gz'), may hold values from -10 to 61, as said below
- dirichlet_inverse: float32 [4, 4, 2, 343, 343], P('gx', 'gy', 'gz'), as said below
- neumann_inverse: float32 [4, 4, 2, 729, 729], P('gx', 'gy', 'gz'), as said below
- coarse_basis: float32 [4, 4, 2, 20, 729], P('gx', 'gy', 'gz'), as said below
Outputs:
- solution: float32 [36, 36, 18, 128], P('gx', 'gy', 'gz')
- residual: float32 [36, 36, 18, 128], P('gx', 'gy', 'gz')
Inputs may be any that keep to these rules, and one draw needn't show every extreme that they name: `local_matrix`: block (a, b, c) is the symmetric positive definite stiffness matrix of subdomain (a, b, c) in the node order of the steps: cellwise conductivities on the couplings of neighbouring nodes plus a lumped reaction term. `dirichlet_inverse`: block (a, b, c) is the inverse, computed in float32, of local_matrix's block restricted to the inner nodes. `neumann_inverse`: block (a, b, c) is the node-by-node block of the inverse, computed in float32, of the saddle-point matrix [[A, Cm^T], [Cm, 0]], with A local_matrix's block and Cm the 20 x 729 primal constraints in the order of the coarse numbering: the value at each of the 8 corners, then the mean over the 7 inner nodes of each of the 12 edges. `coarse_basis`: block (a, b, c) is the constraint-by-node block of that same saddle-point inverse.
All inputs are finite; a program needn't handle non-finite values.
Results may differ from a plain program's by a relative error of at most 0.0014.
Values sent between devices are 32-bit elements; how exact they have to be, the bound alone decides.
No kernel may reach another device: no remote copies, remote signals or barrier semaphores. Data moves between devices by JAX's collectives and lax.ppermute only.
A program may use at most 128 MiB of HBM per device.

v0:
```python
import jax
import jax.numpy as jnp
from jax import lax
from jax.sharding import PartitionSpec as P

ITERS = 2


def with_halo(array, sides, width):
    for axis, dim in sides:
        size, length = (lax.axis_size(axis), array.shape[dim])
        up = [(i, (i + 1) % size) for i in range(size)]
        down = [(j, i) for i, j in up]
        last = lax.slice_in_dim(array, length - width, length, axis=dim)
        leading = lax.slice_in_dim(array, 0, width, axis=dim)
        before = lax.ppermute(last, axis, up)
        after = lax.ppermute(leading, axis, down)
        array = jnp.concatenate([before, array, after], axis=dim)
    return array


def matmul(left_side, right_side):
    return jnp.dot(
        left_side, right_side, precision=lax.Precision.HIGHEST, preferred_element_type=jnp.float32
    )


def coarse_ids(along_x, along_y, along_z, count_x, count_y, count_z):
    total = count_x * count_y * count_z

    def vertex(shift_x, shift_y, shift_z):
        return (
            (along_x + shift_x) % count_x * count_y + (along_y + shift_y) % count_y
        ) * count_z + (along_z + shift_z) % count_z

    listed = [vertex(sx, sy, sz) for sx in (0, 1) for sy in (0, 1) for sz in (0, 1)]
    listed += [total + vertex(0, sy, sz) for sy in (0, 1) for sz in (0, 1)]
    listed += [2 * total + vertex(sx, 0, sz) for sx in (0, 1) for sz in (0, 1)]
    listed += [3 * total + vertex(sx, sy, 0) for sx in (0, 1) for sy in (0, 1)]
    return jnp.stack(listed, axis=-1)


def node_weights(node_side):
    places = jnp.arange(node_side, dtype=jnp.int32)
    on_rim = ((places == 0) | (places == node_side - 1)).astype(jnp.int32)
    rims = on_rim[:, None, None] + on_rim[None, :, None] + on_rim[None, None, :]
    copies = (
        (1.0 + on_rim[:, None, None].astype(jnp.float32))
        * (1.0 + on_rim[None, :, None].astype(jnp.float32))
        * (1.0 + on_rim[None, None, :].astype(jnp.float32))
    )
    share = (1.0 / copies)[..., None]
    border = jnp.where(rims[..., None] > 0, share, jnp.zeros_like(share))
    return (share, border)


def fold_rim(padded, axis_dim):
    length = padded.shape[axis_dim]
    inside = lax.slice_in_dim(padded, 1, length - 1, axis=axis_dim)
    lowest = lax.slice_in_dim(padded, 0, 1, axis=axis_dim)
    highest = lax.slice_in_dim(padded, length - 1, length, axis=axis_dim)
    middle_shape = list(lowest.shape)
    middle_shape[axis_dim] = length - 4
    addend = jnp.concatenate(
        [lowest, jnp.zeros(middle_shape, padded.dtype), highest], axis=axis_dim
    )
    return inside + addend


def local(element_load, local_matrix, dirichlet_inverse, neumann_inverse, coarse_basis):
    highest_prec = lax.Precision.HIGHEST
    node_side = element_load.shape[0]
    rhs_count = element_load.shape[3]
    node_count = node_side**3
    inner_side = node_side - 2
    inner_count = inner_side**3
    primal = coarse_basis.shape[3]
    stiffness = local_matrix.reshape(node_count, node_count)
    interior_inverse = dirichlet_inverse.reshape(inner_count, inner_count)
    neumann = neumann_inverse.reshape(node_count, node_count)
    basis = coarse_basis.reshape(primal, node_count)
    stiff_cols = stiffness.reshape(node_count, node_side, node_side, node_side)[
        :, 1:-1, 1:-1, 1:-1
    ].reshape(node_count, inner_count)
    stiff_rows = stiffness.reshape(node_side, node_side, node_side, node_count)[
        1:-1, 1:-1, 1:-1
    ].reshape(inner_count, node_count)
    share, border = node_weights(node_side)
    count_x = lax.axis_size("gx")
    count_y = lax.axis_size("gy")
    count_z = lax.axis_size("gz")
    coarse_count = 4 * count_x * count_y * count_z
    own_ids = coarse_ids(
        lax.axis_index("gx"), lax.axis_index("gy"), lax.axis_index("gz"), count_x, count_y, count_z
    )
    columns = jnp.arange(coarse_count, dtype=jnp.int32)
    own_indicator = (own_ids[:, None] == columns[None, :]).astype(jnp.float32)
    coarse_local = matmul(basis, matmul(stiffness, basis.T))

    def piece_indicator(count_rows):
        linear = jnp.arange(count_rows, dtype=jnp.int32)
        piece_ids = coarse_ids(
            linear // (count_y * count_z),
            linear // count_z % count_y,
            linear % count_z,
            count_x,
            count_y,
            count_z,
        )
        return (piece_ids[:, :, None] == columns[None, None, :]).astype(jnp.float32)

    received = lax.all_gather(coarse_local[None], ("gx", "gy", "gz"), axis=0, tiled=True)
    indicator = piece_indicator(received.shape[0])
    partial_rows = jnp.einsum("zpm,zpq->zmq", indicator, received, precision=highest_prec)
    coarse_matrix = jnp.einsum("zmq,zqn->mn", partial_rows, indicator, precision=highest_prec)
    factor = jnp.linalg.cholesky(coarse_matrix)

    def coarse_rhs(primal_load):
        received = lax.all_gather(primal_load[None], ("gx", "gy", "gz"), axis=0, tiled=True)
        indicator = piece_indicator(received.shape[0])
        return jnp.einsum("zpm,zpk->mk", indicator, received, precision=highest_prec)

    def assemble(field):
        padded = with_halo(field, (("gx", 0),), 1)
        field = fold_rim(padded, 0)
        padded = with_halo(field, (("gy", 1),), 1)
        field = fold_rim(padded, 1)
        padded = with_halo(field, (("gz", 2),), 1)
        result_field = fold_rim(padded, 2)
        return result_field

    cube_shape = (node_side, node_side, node_side, rhs_count)

    def precondition(current):
        inner_part = current[1:-1, 1:-1, 1:-1].reshape(inner_count, rhs_count)
        start = matmul(interior_inverse, inner_part)
        spill = matmul(stiff_cols, start).reshape(cube_shape)
        first_residual = current - assemble(spill)
        weighted = (border * first_residual).reshape(node_count, rhs_count)
        local_part = matmul(neumann, weighted)
        primal_load = matmul(basis, weighted)
        coarse_values = jax.scipy.linalg.cho_solve((factor, True), coarse_rhs(primal_load))
        primal_values = matmul(own_indicator, coarse_values)
        combined = local_part + matmul(basis.T, primal_values)
        surface = assemble(border * combined.reshape(cube_shape))
        inner_new = start - matmul(
            interior_inverse, matmul(stiff_rows, surface.reshape(node_count, rhs_count))
        )
        padded_inner = jnp.pad(
            inner_new.reshape(inner_side, inner_side, inner_side, rhs_count),
            ((1, 1), (1, 1), (1, 1), (0, 0)),
        )
        return surface + padded_inner

    right_side = assemble(element_load)
    solution = jnp.zeros(cube_shape, jnp.float32)
    residual = right_side

    def precond_dot(left_field, right_field):
        return lax.psum(
            jnp.sum(left_field * right_field * share, axis=(0, 1, 2)), ("gx", "gy", "gz")
        )

    precond_now = precondition(residual)
    direction = precond_now
    energy = precond_dot(residual, precond_now)
    for iteration in range(ITERS):
        mapped = assemble(
            matmul(stiffness, direction.reshape(node_count, rhs_count)).reshape(cube_shape)
        )
        step_size = energy / lax.psum(
            jnp.sum(direction * mapped * share, axis=(0, 1, 2)), ("gx", "gy", "gz")
        )
        solution = solution + step_size * direction
        residual = residual - step_size * mapped
        if iteration + 1 < ITERS:
            precond_now = precondition(residual)
            energy_next = precond_dot(residual, precond_now)
            direction = precond_now + energy_next / energy * direction
            energy = energy_next
    return (solution, residual)


def solution(mesh):
    in_specs = (
        P("gx", "gy", "gz", None),
        P("gx", "gy", "gz", None, None),
        P("gx", "gy", "gz", None, None),
        P("gx", "gy", "gz", None, None),
        P("gx", "gy", "gz", None, None),
    )
    out_specs = (P("gx", "gy", "gz", None), P("gx", "gy", "gz", None))
    return jax.shard_map(local, mesh=mesh, in_specs=in_specs, out_specs=out_specs, check_vma=False)
```

profile of v0, /device:TPU:0, one launch (start us, length us, event | category | flops | bytes accessed | tf_op | source)
XLA Modules:
  0.0 517.5 jit_solution(8985004358485511838)
XLA Ops:
  1.6 4.0 collective-permute-start.1
  5.9 3.7 fusion.4
  9.9 43.8 %all-gather.3 = f32[32,20,20]{2,1,0:T(8,128)S(1)} all-gather(f32[1,20,20]{2,1,0:T(8,128)S(1)} %copy.11), channel_id=2, replica_groups=mesh['gx'=4,'gy'=4,'gz'=2] {'gx','gy','gz'}, dimensions={0}, use_global_device_ids=true | all-gather | bytes 52800 | tf_op jit(solution)/shard_map/all_gather | solution.py:112
  65.3 5.0 copy.10
  70.3 3.7 reshape_reshape.6
  79.0 13.2 %cholesky.18 = f32[128,128]{1,0:T(8,128)} custom-call(f32[128,128]{1,0:T(8,128)} %fusion.80), custom_call_target="Cholesky" | custom-call | tf_op jit(solution)/shard_map/jit(cholesky)/cholesky | solution.py:116
  97.4 3.3 convolution_bitcast_fusion.1
  122.5 11.3 %custom-call.9 = f32[1,128,128]{1,2,0:T(8,128)} custom-call(f32[1,128,128]{2,1,0:T(8,128)} %fusion.71), custom_call_target="InvertDiagBlocksLowerTriangular" | custom-call | tf_op jit(solution)/shard_map/jit(_cho_solve)/triangular_solve | solution.py:142
  140.2 3.7 fusion.8
  143.9 38.8 %all-gather.4 = f32[32,20,128]{2,1,0:T(8,128)S(1)} all-gather(f32[1,20,128]{2,1,0:T(8,128)S(1)} %convolution_bitcast_fusion.7), channel_id=3, replica_groups=mesh['gx'=4,'gy'=4,'gz'=2] {'gx','gy','gz'}, dimensions={0}, use_global_device_ids=true | all-gather | bytes 337920 | tf_op jit(solution)/shard_map/all_gather | solution.py:119
  208.3 7.4 %reduce.6 = f32[729,729]{1,0:T(8,128)} reduce(f32[1,1,1,729,729]{4,2,3,1,0:T(1,128)S(1)} %copy-done, f32[]{:T(128)} %constant.929), dimensions={0,1,2}, to_apply=%param.8.reduce_sub_computation | reduce | bytes 4251532 | tf_op args[1]
  215.7 3.7 reshape_reshape.7
  267.8 37.9 %all-reduce.2 = (f32[128]{0:T(128)}, f32[128]{0:T(128)}) all-reduce(f32[128]{0:T(128)} %get-tuple-element.4, f32[128]{0:T(128)} %get-tuple-element.3), channel_id=1, replica_groups=mesh['gx'=4,'gy'=4,'gz'=2] {'gx','gy','gz'}, use_global_device_ids=true, to_apply=%region_3.5 | all-reduce | flops 256 | bytes 2048 | tf_op jit(solution)/shard_map/psum | solution.py:160
  309.7 3.3 convolution_bitcast_fusion
  313.7 3.3 collective-permute-start.25
  319.7 3.6 collective-permute-done.24
  338.4 3.6 fusion.6
  342.4 38.3 %all-gather.5 = f32[32,20,128]{2,1,0:T(8,128)S(1)} all-gather(f32[1,20,128]{2,1,0:T(8,128)S(1)} %convolution_bitcast_fusion.6), channel_id=4, replica_groups=mesh['gx'=4,'gy'=4,'gz'=2] {'gx','gy','gz'}, dimensions={0}, use_global_device_ids=true | all-gather | bytes 337920 | tf_op jit(solution)/shard_map/all_gather | solution.py:119
  386.9 3.1 collective-permute-done.31
  396.4 3.4 collective-permute-done.32
  415.4 36.9 %psum.30 = f32[128]{0:T(128)S(1)} all-reduce(f32[128]{0:T(128)S(1)} %multiply_reduce_fusion.1), channel_id=1, replica_groups=mesh['gx'=4,'gy'=4,'gz'=2] {'gx','gy','gz'}, use_global_device_ids=true, to_apply=%region_7.9 | all-reduce | flops 128 | bytes 1024 | tf_op jit(solution)/shard_map/psum | solution.py:160
  465.0 3.3 collective-permute-done.36
  473.5 3.5 collective-permute-done.38
  479.0 36.9 %psum.31 = f32[128]{0:T(128)S(1)} all-reduce(f32[128]{0:T(128)S(1)} %multiply_reduce_fusion), channel_id=1, replica_groups=mesh['gx'=4,'gy'=4,'gz'=2] {'gx','gy','gz'}, use_global_device_ids=true, to_apply=%region_9.11 | all-reduce | flops 128 | bytes 1024 | tf_op jit(solution)/shard_map/psum | solution.py:171
  (317 shorter events, 196.9 us)
Async XLA Ops:
  1.6 54.7 %collective-permute-start.1 = (f32[1,9,9,128]{3,2,1,0:T(8,128)S(1)}, f32[1,9,9,128]{3,2,1,0:T(8,128)S(1)}, u32[]{:S(2)}, u32[]{:S(2)}) collective-permute-start(f32[1,9,9,128]{3,2,1,0:T(8,128)S(1)} %get-tuple-element.40), channel_id=1, source_target_pairs={{8,0},{16,8},{24,16},{0,24},{9,1},{17,9},{25,17},{1,25},{10,2},{18... | collective-permute-start | bytes 124424 | tf_op jit(solution)/shard_map/ppermute | solution.py:17
  5.6 50.7 %collective-permute-start = (f32[1,9,9,128]{3,2,1,0:T(8,128)S(1)}, f32[1,9,9,128]{3,2,1,0:T(8,128)S(1)}, u32[]{:S(2)}, u32[]{:S(2)}) collective-permute-start(f32[1,9,9,128]{3,2,1,0:T(8,128)S(1)} %get-tuple-element.39), channel_id=1, source_target_pairs={{0,8},{8,16},{16,24},{24,0},{1,9},{9,17},{17,25},{25,1},{2,10},{10... | collective-permute-start | bytes 124424 | tf_op jit(solution)/shard_map/ppermute | solution.py:16
  56.5 6.7 %collective-permute-start.2 = (f32[9,1,9,128]{3,2,1,0:T(8,128)S(1)}, f32[9,1,9,128]{3,2,1,0:T(8,128)S(1)}, u32[]{:S(2)}, u32[]{:S(2)}) collective-permute-start(f32[9,1,9,128]{3,2,1,0:T(8,128)S(1)} %get-tuple-element.37), channel_id=1, source_target_pairs={{0,2},{2,4},{4,6},{6,0},{1,3},{3,5},{5,7},{7,1},{8,10},{10,12},{12... | collective-permute-start | bytes 124424 | tf_op jit(solution)/shard_map/ppermute | solution.py:16
  64.0 28.2 %collective-permute-start.5 = (f32[9,9,1,128]{3,2,1,0:T(1,128)}, f32[9,9,1,128]{3,2,1,0:T(1,128)S(1)}, u32[]{:S(2)}, u32[]{:S(2)}) collective-permute-start(f32[9,9,1,128]{3,2,1,0:T(1,128)} %get-tuple-element.36), channel_id=1, source_target_pairs={{1,0},{0,1},{3,2},{2,3},{5,4},{4,5},{7,6},{6,7},{9,8},{8,9},{11,10... | collective-permute-start | bytes 124424 | tf_op jit(solution)/shard_map/ppermute | solution.py:17
  64.0 28.2 %collective-permute-start.4 = (f32[9,9,1,128]{3,2,1,0:T(1,128)}, f32[9,9,1,128]{3,2,1,0:T(1,128)}, u32[]{:S(2)}, u32[]{:S(2)}) collective-permute-start(f32[9,9,1,128]{3,2,1,0:T(1,128)} %get-tuple-element.35), channel_id=1, source_target_pairs={{0,1},{1,0},{2,3},{3,2},{4,5},{5,4},{6,7},{7,6},{8,9},{9,8},{10,11... | collective-permute-start | bytes 124424 | tf_op jit(solution)/shard_map/ppermute | solution.py:16
  103.6 6.7 %collective-permute-start.7 = (f32[1,9,9,128]{3,2,1,0:T(8,128)}, f32[1,9,9,128]{3,2,1,0:T(8,128)}, u32[]{:S(2)}, u32[]{:S(2)}) collective-permute-start(f32[1,9,9,128]{3,2,1,0:T(8,128)} %slice.187), channel_id=1, source_target_pairs={{8,0},{16,8},{24,16},{0,24},{9,1},{17,9},{25,17},{1,25},{10,2},{18... | collective-permute-start | bytes 124424 | tf_op jit(solution)/shard_map/ppermute | solution.py:17
  105.0 5.6 %collective-permute-start.6 = (f32[1,9,9,128]{3,2,1,0:T(8,128)}, f32[1,9,9,128]{3,2,1,0:T(8,128)}, u32[]{:S(2)}, u32[]{:S(2)}) collective-permute-start(f32[1,9,9,128]{3,2,1,0:T(8,128)} %slice.185), channel_id=1, source_target_pairs={{0,8},{8,16},{16,24},{24,0},{1,9},{9,17},{17,25},{25,1},{2,10},{10... | collective-permute-start | bytes 124424 | tf_op jit(solution)/shard_map/ppermute | solution.py:16
  112.1 6.7 %collective-permute-start.8 = (f32[9,1,9,128]{3,2,1,0:T(8,128)S(1)}, f32[9,1,9,128]{3,2,1,0:T(8,128)S(1)}, u32[]{:S(2)}, u32[]{:S(2)}) collective-permute-start(f32[9,1,9,128]{3,2,1,0:T(8,128)S(1)} %get-tuple-element.33), channel_id=1, source_target_pairs={{0,2},{2,4},{4,6},{6,0},{1,3},{3,5},{5,7},{7,1},{8,10},{10,12},{12... | collective-permute-start | bytes 124424 | tf_op jit(solution)/shard_map/ppermute | solution.py:16
  120.7 13.7 %collective-permute-start.11 = (f32[9,9,1,128]{3,2,1,0:T(1,128)}, f32[9,9,1,128]{3,2,1,0:T(1,128)}, u32[]{:S(2)}, u32[]{:S(2)}) collective-permute-start(f32[9,9,1,128]{3,2,1,0:T(1,128)} %get-tuple-element.32), channel_id=1, source_target_pairs={{1,0},{0,1},{3,2},{2,3},{5,4},{4,5},{7,6},{6,7},{9,8},{8,9},{11,10... | collective-permute-start | bytes 124424 | tf_op jit(solution)/shard_map/ppermute | solution.py:17
  120.7 13.7 %collective-permute-start.10 = (f32[9,9,1,128]{3,2,1,0:T(1,128)}, f32[9,9,1,128]{3,2,1,0:T(1,128)}, u32[]{:S(2)}, u32[]{:S(2)}) collective-permute-start(f32[9,9,1,128]{3,2,1,0:T(1,128)} %get-tuple-element.31), channel_id=1, source_target_pairs={{0,1},{1,0},{2,3},{3,2},{4,5},{5,4},{6,7},{7,6},{8,9},{9,8},{10,11... | collective-permute-start | bytes 124424 | tf_op jit(solution)/shard_map/ppermute | solution.py:16
  188.8 7.1 %collective-permute-start.12 = (f32[1,9,9,128]{3,2,1,0:T(8,128)S(1)}, f32[1,9,9,128]{3,2,1,0:T(8,128)S(1)}, u32[]{:S(2)}, u32[]{:S(2)}) collective-permute-start(f32[1,9,9,128]{3,2,1,0:T(8,128)S(1)} %get-tuple-element.29), channel_id=1, source_target_pairs={{0,8},{8,16},{16,24},{24,0},{1,9},{9,17},{17,25},{25,1},{2,10},{10... | collective-permute-start | bytes 124424 | tf_op jit(solution)/shard_map/ppermute | solution.py:16
  198.1 6.4 %collective-permute-start.14 = (f32[9,1,9,128]{3,2,1,0:T(8,128)S(1)}, f32[9,1,9,128]{3,2,1,0:T(8,128)S(1)}, u32[]{:S(2)}, u32[]{:S(2)}) collective-permute-start(f32[9,1,9,128]{3,2,1,0:T(8,128)S(1)} %get-tuple-element.27), channel_id=1, source_target_pairs={{0,2},{2,4},{4,6},{6,0},{1,3},{3,5},{5,7},{7,1},{8,10},{10,12},{12... | collective-permute-start | bytes 124424 | tf_op jit(solution)/shard_map/ppermute | solution.py:16
  207.0 21.0 %collective-permute-start.17 = (f32[9,9,1,128]{3,2,1,0:T(1,128)}, f32[9,9,1,128]{3,2,1,0:T(1,128)}, u32[]{:S(2)}, u32[]{:S(2)}) collective-permute-start(f32[9,9,1,128]{3,2,1,0:T(1,128)} %get-tuple-element.26), channel_id=1, source_target_pairs={{1,0},{0,1},{3,2},{2,3},{5,4},{4,5},{7,6},{6,7},{9,8},{8,9},{11,10... | collective-permute-start | bytes 124424 | tf_op jit(solution)/shard_map/ppermute | solution.py:17
  207.0 21.0 %collective-permute-start.16 = (f32[9,9,1,128]{3,2,1,0:T(1,128)}, f32[9,9,1,128]{3,2,1,0:T(1,128)}, u32[]{:S(2)}, u32[]{:S(2)}) collective-permute-start(f32[9,9,1,128]{3,2,1,0:T(1,128)} %get-tuple-element.25), channel_id=1, source_target_pairs={{0,1},{1,0},{2,3},{3,2},{4,5},{5,4},{6,7},{7,6},{8,9},{9,8},{10,11... | collective-permute-start | bytes 124424 | tf_op jit(solution)/shard_map/ppermute | solution.py:16
  247.3 5.6 %collective-permute-start.19 = (f32[1,9,9,128]{3,2,1,0:T(8,128)}, f32[1,9,9,128]{3,2,1,0:T(8,128)}, u32[]{:S(2)}, u32[]{:S(2)}) collective-permute-start(f32[1,9,9,128]{3,2,1,0:T(8,128)} %slice.202), channel_id=1, source_target_pairs={{8,0},{16,8},{24,16},{0,24},{9,1},{17,9},{25,17},{1,25},{10,2},{18... | collective-permute-start | bytes 124424 | tf_op jit(solution)/shard_map/ppermute | solution.py:17
  249.4 5.8 %collective-permute-start.18 = (f32[1,9,9,128]{3,2,1,0:T(8,128)}, f32[1,9,9,128]{3,2,1,0:T(8,128)}, u32[]{:S(2)}, u32[]{:S(2)}) collective-permute-start(f32[1,9,9,128]{3,2,1,0:T(8,128)} %slice.200), channel_id=1, source_target_pairs={{0,8},{8,16},{16,24},{24,0},{1,9},{9,17},{17,25},{25,1},{2,10},{10... | collective-permute-start | bytes 124424 | tf_op jit(solution)/shard_map/ppermute | solution.py:16
  256.7 6.2 %collective-permute-start.20 = (f32[9,1,9,128]{3,2,1,0:T(8,128)S(1)}, f32[9,1,9,128]{3,2,1,0:T(8,128)S(1)}, u32[]{:S(2)}, u32[]{:S(2)}) collective-permute-start(f32[9,1,9,128]{3,2,1,0:T(8,128)S(1)} %get-tuple-element.23), channel_id=1, source_target_pairs={{0,2},{2,4},{4,6},{6,0},{1,3},{3,5},{5,7},{7,1},{8,10},{10,12},{12... | collective-permute-start | bytes 124424 | tf_op jit(solution)/shard_map/ppermute | solution.py:16
  313.7 5.9 %collective-permute-start.25 = (f32[1,9,9,128]{3,2,1,0:T(8,128)}, f32[1,9,9,128]{3,2,1,0:T(8,128)}, u32[]{:S(2)}, u32[]{:S(2)}) collective-permute-start(f32[1,9,9,128]{3,2,1,0:T(8,128)} %slice.211), channel_id=1, source_target_pairs={{8,0},{16,8},{24,16},{0,24},{9,1},{17,9},{25,17},{1,25},{10,2},{18... | collective-permute-start | bytes 124424 | tf_op jit(solution)/shard_map/ppermute | solution.py:17
  317.7 5.6 %collective-permute-start.24 = (f32[1,9,9,128]{3,2,1,0:T(8,128)}, f32[1,9,9,128]{3,2,1,0:T(8,128)}, u32[]{:S(2)}, u32[]{:S(2)}) collective-permute-start(f32[1,9,9,128]{3,2,1,0:T(8,128)} %slice.209), channel_id=1, source_target_pairs={{0,8},{8,16},{16,24},{24,0},{1,9},{9,17},{17,25},{25,1},{2,10},{10... | collective-permute-start | bytes 124424 | tf_op jit(solution)/shard_map/ppermute | solution.py:16
  326.2 6.2 %collective-permute-start.26 = (f32[9,1,9,128]{3,2,1,0:T(8,128)S(1)}, f32[9,1,9,128]{3,2,1,0:T(8,128)S(1)}, u32[]{:S(2)}, u32[]{:S(2)}) collective-permute-start(f32[9,1,9,128]{3,2,1,0:T(8,128)S(1)} %get-tuple-element.19), channel_id=1, source_target_pairs={{0,2},{2,4},{4,6},{6,0},{1,3},{3,5},{5,7},{7,1},{8,10},{10,12},{12... | collective-permute-start | bytes 124424 | tf_op jit(solution)/shard_map/ppermute | solution.py:16
  384.9 6.1 %collective-permute-start.30 = (f32[1,9,9,128]{3,2,1,0:T(8,128)S(1)}, f32[1,9,9,128]{3,2,1,0:T(8,128)S(1)}, u32[]{:S(2)}, u32[]{:S(2)}) collective-permute-start(f32[1,9,9,128]{3,2,1,0:T(8,128)S(1)} %get-tuple-element.15), channel_id=1, source_target_pairs={{0,8},{8,16},{16,24},{24,0},{1,9},{9,17},{17,25},{25,1},{2,10},{10... | collective-permute-start | bytes 124424 | tf_op jit(solution)/shard_map/ppermute | solution.py:16
  393.3 6.4 %collective-permute-start.32 = (f32[9,1,9,128]{3,2,1,0:T(8,128)S(1)}, f32[9,1,9,128]{3,2,1,0:T(8,128)S(1)}, u32[]{:S(2)}, u32[]{:S(2)}) collective-permute-start(f32[9,1,9,128]{3,2,1,0:T(8,128)S(1)} %get-tuple-element.13), channel_id=1, source_target_pairs={{0,2},{2,4},{4,6},{6,0},{1,3},{3,5},{5,7},{7,1},{8,10},{10,12},{12... | collective-permute-start | bytes 124424 | tf_op jit(solution)/shard_map/ppermute | solution.py:16
  463.0 5.3 %collective-permute-start.36 = (f32[1,9,9,128]{3,2,1,0:T(8,128)S(1)}, f32[1,9,9,128]{3,2,1,0:T(8,128)S(1)}, u32[]{:S(2)}, u32[]{:S(2)}) collective-permute-start(f32[1,9,9,128]{3,2,1,0:T(8,128)S(1)} %slice.223), channel_id=1, source_target_pairs={{0,8},{8,16},{16,24},{24,0},{1,9},{9,17},{17,25},{25,1},{2,10},{10... | collective-permute-start | bytes 124424 | tf_op jit(solution)/shard_map/ppermute | solution.py:16
  470.8 6.2 %collective-permute-start.38 = (f32[9,1,9,128]{3,2,1,0:T(8,128)S(1)}, f32[9,1,9,128]{3,2,1,0:T(8,128)S(1)}, u32[]{:S(2)}, u32[]{:S(2)}) collective-permute-start(f32[9,1,9,128]{3,2,1,0:T(8,128)S(1)} %get-tuple-element.9), channel_id=1, source_target_pairs={{0,2},{2,4},{4,6},{6,0},{1,3},{3,5},{5,7},{7,1},{8,10},{10,12},{12... | collective-permute-start | bytes 124424 | tf_op jit(solution)/shard_map/ppermute | solution.py:16
  (70 other events, 895.7 us)
where the time goes:
time: 524 us; the launch traced here: 518 us
  blocking collectives  233 us (44%)
  other arithmetic  73.6 us (14%)
  local copies, waits for them, and re-layouts  71.8 us (14%)
  waiting for transfers between devices  56.2 us (11%)
  matrix products  42.8 us (8%)
  starting transfers between devices  38.6 us (7%)
    all_gather x2, blocking collectives, coarse_rhs(): lax.all_gather(primal_load[None], ('gx', 'gy', 'gz'), axis=0, tiled=True)  77.1 us
    psum x2, blocking collectives, precond_dot(): lax.psum(jnp.sum(left_field * right_field * share, axis=(0, 1, 2)), ('gx'...  74.8 us
    all_gather x1, blocking collectives, local(): lax.all_gather(coarse_local[None], ('gx', 'gy', 'gz'), axis=0, tiled=True)  43.8 us
    dot_general x20, matrix products, matmul(): jnp.dot(left_side, right_side, precision=lax.Precision.HIGHEST, preferred...  39.7 us
    psum x1, blocking collectives, local(): lax.psum(jnp.sum(direction * mapped * share, axis=(0, 1, 2)), ('gx', 'gy'...  36.9 us
    ppermute x21, waiting for transfers between devices, with_halo(): before = lax.ppermute(last, axis, up)  30.2 us
    ppermute x21, waiting for transfers between devices, with_halo(): after = lax.ppermute(leading, axis, down)  26 us
    ppermute x21, starting transfers between devices, with_halo(): before = lax.ppermute(last, axis, up)  21.4 us
  transfers between devices with their start and end apart: 42, of which 29 were waited for; matrix products, arithmetic and copies ran while one was open for 16% of the time, Pallas kernels for 0%

commit v1 on v0

v1 whole, which is shorter than its diff:
```python
import functools

import jax
import jax.numpy as jnp
import numpy as np
from jax import lax
from jax.experimental import pallas as pl
from jax.experimental.pallas import tpu as pltpu
from jax.sharding import PartitionSpec as P

AXES = ("gx", "gy", "gz")
HIGHEST = lax.Precision.HIGHEST
PALLAS = True


def dot(left, right, contract=(1, 0)):
    dims = (((contract[0],), (contract[1],)), ((), ()))
    return lax.dot_general(
        left, right, dims, precision=HIGHEST, preferred_element_type=jnp.float32
    )


def run(function, *operands, flops=10**7):
    if not PALLAS:
        return function(*operands)
    shapes = jax.eval_shape(function, *operands)
    single = not isinstance(shapes, tuple)
    outs = (shapes,) if single else shapes
    count = len(operands)

    def body(*refs):
        results = function(*[ref[...] for ref in refs[:count]])
        results = (results,) if single else results
        for ref, result in zip(refs[count:], results):
            ref[...] = result

    vmem = pl.BlockSpec(memory_space=pltpu.VMEM)
    size = sum(4 * np.prod(x.shape) for x in (*operands, *outs))
    results = pl.pallas_call(
        body,
        out_shape=[jax.ShapeDtypeStruct(x.shape, x.dtype) for x in outs],
        in_specs=[vmem] * count,
        out_specs=[vmem] * len(outs),
        cost_estimate=pl.CostEstimate(
            flops=flops, bytes_accessed=int(size), transcendentals=0
        ),
    )(*operands)
    return results[0] if single else tuple(results)


class Layout:
    def __init__(self, n):
        half = 2 * (n - 1)
        self.n, self.half = n, half
        self.ring_rows = n * 2 * half
        flat = (n - 2) ** 2
        self.flat = -(-flat // 8) * 8
        self.rows = self.ring_rows + 2 * self.flat
        at = lambda i, j, k: (i * n + j) * n + k
        order = []
        for i in range(n):
            for j, k in ((0, 0), (n - 1, n - 1)):
                order += [at(i, j, m) for m in range(n)]
                order += [at(i, m, k) for m in range(1, n - 1)]
        for i in (0, n - 1):
            order += [at(i, j, k) for j in range(1, n - 1) for k in range(1, n - 1)]
            order += [-1] * (self.flat - flat)
        self.order = np.array(order, np.int32)
        inner = range(1, n - 1)
        self.inner = np.array([at(i, j, k) for i in inner for j in inner for k in inner], np.int32)
        share = np.zeros((self.rows, 1), np.float32)
        for row, node in enumerate(order):
            if node >= 0:
                place = (node // (n * n), node // n % n, node % n)
                share[row] = 0.5 ** sum(x in (0, n - 1) for x in place)
        self.share = share

    def split(self, field):
        ring = field[: self.ring_rows].reshape(self.n, 2 * self.half, field.shape[1])
        flat = field[self.ring_rows :].reshape(2, self.flat, field.shape[1])
        return ring, flat

    def join(self, ring, flat):
        width = ring.shape[-1]
        return jnp.concatenate(
            [ring.reshape(self.ring_rows, width), flat.reshape(2 * self.flat, width)], axis=0
        )

    def fold_z(self, ring, below, above):
        n, half = self.n, self.half
        row = lax.broadcasted_iota(jnp.int32, ring.shape, 1)
        swap = lambda x: jnp.concatenate([x[:, half:], x[:, :half]], axis=1)

        def corner(x):
            m = n - 1
            parts = [x[:, s : s + m] for s in (m, 0, half + m, half)]
            return jnp.concatenate(parts, axis=1)

        low_side = (row >= n) & (row < half)
        high_side = row >= half + n
        low_end = (row == 0) | (row == half)
        high_end = (row == n - 1) | (row == half + n - 1)
        zero = jnp.zeros_like(ring)
        if below is above:
            side = jnp.where(low_side | high_side, swap(below), zero)
            return ring + side + jnp.where(low_end | high_end, corner(below), zero)
        ring = ring + jnp.where(low_side, swap(below), zero)
        ring = ring + jnp.where(high_side, swap(above), zero)
        ring = ring + jnp.where(low_end, corner(below), zero)
        return ring + jnp.where(high_end, corner(above), zero)

    def fold_y(self, ring, below, above):
        add = jnp.concatenate([below, above], axis=1)
        row = lax.broadcasted_iota(jnp.int32, ring.shape, 1) % self.half
        return ring + jnp.where(row < self.n, add, jnp.zeros_like(add))

    def fold_x(self, ring, flat, below, above):
        width = 2 * self.half
        first = ring[:1] + below[None, :width]
        last = ring[-1:] + above[None, :width]
        ring = jnp.concatenate([first, ring[1:-1], last], axis=0)
        flat = flat + jnp.stack([below[width:], above[width:]])
        return ring, flat


def shifted(value, axis, step):
    size = lax.axis_size(axis)
    return lax.ppermute(value, axis, [(i, (i + step) % size) for i in range(size)])


def both_ways(low, high, axis):
    return shifted(high, axis, 1), shifted(low, axis, -1)


def gathered(block):
    count = lax.axis_size(AXES)
    spread = jnp.broadcast_to(block[None], (count, *block.shape))
    return lax.all_to_all(spread, AXES, 0, 0, tiled=True)


def cat(parts):
    return parts[0] if len(parts) == 1 else jnp.concatenate(parts, axis=0)


def assemble(layout, fields, finish):
    count = len(fields)
    width = 2 * layout.half
    half = layout.half

    def rings_of(*fields):
        return cat([f[: layout.ring_rows] for f in fields])

    rings = run(rings_of, *fields)
    if lax.axis_size("gz") == 2:
        other = shifted(rings, "gz", 1)
        others = (other,)
    else:
        others = (shifted(rings, "gz", 1), shifted(rings, "gz", -1))

    def after_z(rings, *others):
        shape = (count * layout.n, width, rings.shape[1])
        shaped = [x.reshape(shape) for x in others]
        ring = layout.fold_z(rings.reshape(shape), shaped[0], shaped[-1])
        low = ring[:, :half].reshape(-1, rings.shape[1])
        high = ring[:, half:].reshape(-1, rings.shape[1])
        return ring.reshape(rings.shape), low, high

    rings, low, high = run(after_z, rings, *others)
    below, above = both_ways(low, high, "gy")

    def after_y(rings, below, above, *fields):
        lanes = rings.shape[1]
        shape = (count * layout.n, half, lanes)
        ring = layout.fold_y(
            rings.reshape(count * layout.n, width, lanes), below.reshape(shape), above.reshape(shape)
        )
        ring = ring.reshape(count, layout.n, width, lanes)
        low, high = [], []
        for index, field in enumerate(fields):
            flat = layout.split(field)[1]
            low += [ring[index, 0], flat[0]]
            high += [ring[index, -1], flat[1]]
        return ring.reshape(rings.shape), cat(low), cat(high)

    rings, low, high = run(after_y, rings, below, above, *fields)
    below, above = both_ways(low, high, "gx")
    extra, function = finish

    def after_x(rings, below, above, *rest):
        fields, rest = rest[:count], rest[count:]
        message = width + layout.flat
        done = []
        for index, field in enumerate(fields):
            ring = rings[index * layout.ring_rows : (index + 1) * layout.ring_rows]
            ring = ring.reshape(layout.n, width, rings.shape[1])
            flat = layout.split(field)[1]
            place = slice(index * message, (index + 1) * message)
            done.append(layout.join(*layout.fold_x(ring, flat, below[place], above[place])))
        return function(*done, *rest)

    return run(after_x, rings, below, above, *fields, *extra)


def split3(value):
    high = value.astype(jnp.bfloat16)
    rest = value - high.astype(jnp.float32)
    middle = rest.astype(jnp.bfloat16)
    low = (rest - middle.astype(jnp.float32)).astype(jnp.bfloat16)
    return high, middle, low


def pick_rows(chosen, value):
    total = None
    for part in split3(value):
        term = jnp.dot(chosen, part, preferred_element_type=jnp.float32)
        total = term if total is None else total + term
    return total


def pick_columns(value, chosen):
    total = None
    for part in split3(value):
        term = lax.dot_general(
            part, chosen, (((1,), (1,)), ((), ())), preferred_element_type=jnp.float32
        )
        total = term if total is None else total + term
    return total


def one_hot(places, count):
    columns = lax.broadcasted_iota(jnp.int32, (places.shape[0], count), 1)
    return jnp.where(columns == places, 1.0, 0.0).astype(jnp.bfloat16)


def coarse_table(count_x, count_y, count_z, rows):
    total = count_x * count_y * count_z
    linear = np.arange(total)
    along = (linear // (count_y * count_z), linear // count_z % count_y, linear % count_z)

    def vertex(sx, sy, sz):
        x, y, z = along
        return ((x + sx) % count_x * count_y + (y + sy) % count_y) * count_z + (z + sz) % count_z

    two = (0, 1)
    listed = [vertex(sx, sy, sz) for sx in two for sy in two for sz in two]
    listed += [total + vertex(0, sy, sz) for sy in two for sz in two]
    listed += [2 * total + vertex(sx, 0, sz) for sx in two for sz in two]
    listed += [3 * total + vertex(sx, sy, 0) for sx in two for sy in two]
    table = np.full((total, rows), -1, np.int32)
    table[:, : len(listed)] = np.stack(listed, axis=-1)
    return table


def spd_inverse(matrix):
    count = matrix.shape[0]
    rows = lax.broadcasted_iota(jnp.int32, (count, 1), 0)
    lanes = lax.broadcasted_iota(jnp.int32, (1, count), 1)
    for k in range(count):
        column = matrix[:, k : k + 1]
        pivot = matrix[k : k + 1, k : k + 1]
        row = jnp.where(lanes == k, 1.0, matrix[k : k + 1, :]) / pivot
        kept = jnp.where(lanes == k, 0.0, matrix)
        factor = jnp.where(rows == k, 0.0, column)
        matrix = jnp.where(rows == k, 0.0, kept) - factor * row + jnp.where(rows == k, row, 0.0)
    return matrix


def local(element_load, local_matrix, dirichlet_inverse, neumann_inverse, coarse_basis):
    n = element_load.shape[0]
    lanes = element_load.shape[3]
    node_count = n**3
    layout = Layout(n)
    inner_count = (n - 2) ** 3
    primal = coarse_basis.shape[3]
    stiffness = local_matrix.reshape(node_count, node_count)
    interior_inverse = dirichlet_inverse.reshape(inner_count, inner_count)
    neumann = neumann_inverse.reshape(node_count, node_count)
    basis = coarse_basis.reshape(primal, node_count)
    counts = [lax.axis_size(axis) for axis in AXES]
    chunk = -(-primal // 8) * 8
    table = coarse_table(*counts, chunk)
    coarse_count = 4 * counts[0] * counts[1] * counts[2]
    me = lax.axis_index(AXES)
    own_ids = lax.dynamic_slice_in_dim(jnp.asarray(table), me, 1, axis=0).reshape(chunk, 1)
    all_ids = jnp.asarray(table.reshape(-1, 1))
    order = jnp.asarray(layout.order[:, None])
    inner = jnp.asarray(layout.inner[:, None])
    share = jnp.asarray(layout.share)
    share_row = jnp.asarray(layout.share.reshape(1, -1))
    basis = jnp.pad(basis, ((0, chunk - primal), (0, 0)))

    load = element_load.reshape(node_count, lanes)

    def start(stiffness, interior_inverse, basis, load, order, inner, share_row, own_ids):
        surface = one_hot(order, node_count)
        inside = one_hot(inner, node_count)
        picked = pick_columns(stiffness, surface)
        within = pick_rows(surface, picked)
        coupling = pick_rows(inside, picked)
        load_surface = pick_rows(surface, load)
        load_inside = pick_rows(inside, load)
        begun = dot(interior_inverse, load_inside)
        condensed = load_surface - dot(coupling, begun, (0, 0))
        weighted = pick_columns(basis, surface) * share_row
        own = one_hot(own_ids, coarse_count)
        three = [
            lax.dot_general(
                part, own, (((0,), (0,)), ((), ())), preferred_element_type=jnp.float32
            )
            for part in split3(weighted)
        ]
        spread = three[0] + three[1] + three[2]
        tau = jnp.sum(load_inside * begun, axis=0, keepdims=True)
        coarse_local = dot(dot(basis, stiffness), basis, (1, 1))
        coarse_rows = dot(coarse_local, own.astype(jnp.float32))
        return (
            within, coupling, load_surface, load_inside, begun, condensed, weighted, spread, tau,
            coarse_rows,
        )

    (
        within, coupling, load_surface, load_inside, begun, condensed, weighted, spread, tau,
        coarse_rows,
    ) = run(start, stiffness, interior_inverse, basis, load, order, inner, share_row, own_ids)

    def reorder(neumann, order, share, share_row):
        surface = one_hot(order, node_count)
        return pick_rows(surface, pick_columns(neumann, surface)) * share * share_row

    scaled = run(reorder, neumann, order, share, share_row)

    coarse_all = gathered(coarse_rows).reshape(-1, coarse_count)

    def gather_sum(all_ids, rows):
        indicator = one_hot(all_ids, coarse_count)
        return sum(
            lax.dot_general(
                indicator, part, (((0,), (0,)), ((), ())), preferred_element_type=jnp.float32
            )
            for part in split3(rows)
        )

    def invert(all_ids, rows):
        return spd_inverse(gather_sum(all_ids, rows))

    if coarse_count <= 128:
        coarse_inverse = run(invert, all_ids, coarse_all)
    else:
        factor = jnp.linalg.cholesky(run(gather_sum, all_ids, coarse_all))
        coarse_inverse = jax.scipy.linalg.cho_solve(
            (factor, True), jnp.eye(coarse_count, dtype=jnp.float32)
        )

    def neumann_step(field, scaled, weighted):
        return dot(scaled, field), dot(weighted, field)

    def first_step(field, spread, scaled, weighted):
        return (field, spread, *neumann_step(field, scaled, weighted))

    def add_rows(loads, extra):
        rows = lax.broadcasted_iota(jnp.int32, loads.shape, 0)
        for index, value in enumerate(extra):
            loads = jnp.where(rows == primal + index, value, loads)
        return loads

    def operate(field, within, coupling, interior_inverse):
        extended = dot(interior_inverse, dot(coupling, field))
        image = dot(within, field) - dot(coupling, extended, (0, 0))
        return image, extended

    def coarse_step(all_ids, rows, coarse_inverse, spread):
        return dot(spread, dot(coarse_inverse, gather_sum(all_ids, rows)))

    pieces = [spread[:, s : s + lanes] for s in range(0, coarse_count, lanes)]

    def first(field, *rest):
        pieces, (scaled, weighted) = rest[:-2], rest[-2:]
        return (field, *pieces, *neumann_step(field, scaled, weighted))

    results = assemble(layout, [condensed, *pieces], ((scaled, weighted), first))
    residual, pieces, (mapped, loads) = results[0], results[1:-2], results[-2:]
    spread = jnp.concatenate(pieces, axis=1) if len(pieces) > 1 else pieces[0]

    coarse0 = run(
        coarse_step, all_ids, gathered(loads).reshape(-1, lanes), coarse_inverse, spread
    )

    def apply_first(mapped, coarse, within, coupling, interior_inverse, condensed, tau):
        field = mapped + coarse
        image, extended = operate(field, within, coupling, interior_inverse)
        energy = tau + jnp.sum(condensed * field, axis=0, keepdims=True)
        curvature = tau + jnp.sum(field * image, axis=0, keepdims=True)
        return field, image, extended, jnp.concatenate([energy, curvature], axis=0)

    field0, image0, extended0, sums0 = assemble(
        layout,
        [mapped],
        ((coarse0, within, coupling, interior_inverse, condensed, tau), apply_first),
    )

    def second(image, load_surface, scaled, weighted, sums):
        mapped, loads = neumann_step(image, scaled, weighted)
        return image, load_surface, mapped, add_rows(loads, [sums[:1], sums[1:2]])

    image0_sum, load_sum, mapped, loads = assemble(
        layout, [image0, load_surface], ((scaled, weighted, sums0), second)
    )
    rows = gathered(loads)
    coarse1 = run(coarse_step, all_ids, rows.reshape(-1, lanes), coarse_inverse, spread)

    def scalars(rows):
        return jnp.sum(rows, axis=0)

    totals0 = run(scalars, rows)[primal : primal + 2]

    def apply_second(
        mapped, coarse, within, coupling, interior_inverse, condensed, tau, field0, image0, totals
    ):
        field = mapped + coarse
        image, extended = operate(field, within, coupling, interior_inverse)
        step = totals[:1] / totals[1:2]
        rest = 1.0 - step
        direction = field0 - step * field
        direction_image = image0 - step * image
        energy = rest * rest * tau + jnp.sum(
            (condensed - step * image0) * direction, axis=0, keepdims=True
        )
        curvature = rest * rest * tau + jnp.sum(
            direction * direction_image, axis=0, keepdims=True
        )
        cross = rest * tau + jnp.sum(direction * image0, axis=0, keepdims=True)
        fill = jnp.zeros((5, tau.shape[1]), jnp.float32)
        return field, image, extended, jnp.concatenate([energy, curvature, cross, fill], axis=0)

    field1, image1, extended1, sums1 = assemble(
        layout,
        [mapped],
        (
            (coarse1, within, coupling, interior_inverse, condensed, tau, field0, image0, totals0),
            apply_second,
        ),
    )
    rows1 = gathered(sums1)

    def finish(
        image1, image0, residual, load_sum, field0, field1, extended0, extended1, begun,
        load_inside, totals, rows,
    ):
        energy, curvature = totals[:1], totals[1:2]
        sums = jnp.sum(rows, axis=0)
        step = energy / curvature
        energy_next, curvature_next, cross = sums[:1], sums[1:2], sums[2:3]
        ratio = energy_next / energy
        curvature_next = curvature_next + 2.0 * ratio * cross + ratio * ratio * curvature
        step_next = energy_next / curvature_next
        first = step + step_next * (1.0 + ratio)
        second = -step_next * step
        solution_surface = first * field0 + second * field1
        solution_inside = (first + second) * begun - (first * extended0 + second * extended1)
        spill = load_sum - residual
        residual_surface = load_sum - first * (image0 + spill) - second * (image1 + spill)
        residual_inside = (1.0 - first - second) * load_inside
        return solution_surface, solution_inside, residual_surface, residual_inside

    out = assemble(
        layout,
        [image1],
        (
            (
                image0_sum, residual, load_sum, field0, field1, extended0, extended1, begun,
                load_inside, totals0, rows1,
            ),
            finish,
        ),
    )
    place = np.zeros(node_count, np.int32)
    for row, node in enumerate(layout.order):
        if node >= 0:
            place[node] = row
    place[layout.inner] = layout.rows + np.arange(inner_count)
    place = jnp.asarray(place[:, None])
    total_rows = layout.rows + inner_count

    def natural(surface, inside, place):
        chosen = one_hot(place, total_rows)
        return pick_rows(chosen, jnp.concatenate([surface, inside], axis=0))

    shape = element_load.shape
    return (
        run(natural, out[0], out[1], place).reshape(shape),
        run(natural, out[2], out[3], place).reshape(shape),
    )


def solution(mesh):
    in_specs = (
        P("gx", "gy", "gz", None),
        P("gx", "gy", "gz", None, None),
        P("gx", "gy", "gz", None, None),
        P("gx", "gy", "gz", None, None),
        P("gx", "gy", "gz", None, None),
    )
    out_specs = (P("gx", "gy", "gz", None), P("gx", "gy", "gz", None))
    return jax.shard_map(local, mesh=mesh, in_specs=in_specs, out_specs=out_specs, check_vma=False)
```

time: 524 us -> 218 us (0.42)
  blocking collectives: 233 us -> 0 us
  Pallas kernels: 0 us -> 92 us
  other arithmetic: 73.6 us -> 0 us
  matrix products: 42.8 us -> 0 us
  local copies, waits for them, and re-layouts: 71.8 us -> 31.5 us
  waiting for transfers between devices: 56.2 us -> 41.1 us
  starting transfers between devices: 38.6 us -> 51.2 us
    all_gather x3 -> x0, blocking collectives: 121 us -> none  [the longest x2 77.1 us: coarse_rhs(): lax.all_gather(primal_load[None], ('gx', 'gy', 'gz'), axis=0, tiled=True)]
    psum x3 -> x0, blocking collectives: 112 us -> none  [the longest x2 74.8 us: precond_dot(): lax.psum(jnp.sum(left_field * right_field * share, axis=(0, 1, 2)), ('gx'...]
    pallas_call x0 -> x28, Pallas kernels: none -> 92 us  [run(): pl.pallas_call(body, out_shape=[jax.ShapeDtypeStruct(x.shape, x.dtype) fo...]
    dot_general x24 -> x0, matrix products: 41.8 us -> none  [the longest x20 39.7 us: matmul(): jnp.dot(left_side, right_side, precision=lax.Precision.HIGHEST, preferred...]
    another operation x5 -> x0, other arithmetic: 28.3 us -> none  [the longest x3 15.8 us: local(): factor = jnp.linalg.cholesky(coarse_matrix)]
    reshape x16 -> x5, local copies, waits for them, and re-layouts: 24.6 us -> 5.9 us  [the longest x1 1.87 us: local(): run(natural, out[2], out[3], place).reshape(shape)]
    slice x33 -> x1, local copies, waits for them, and re-layouts: 17.9 us -> 1.22 us  [local(): totals0 = run(scalars, rows)[primal:primal + 2]]
    all_to_all x0 -> x4, starting transfers between devices: none -> 16.7 us  [gathered(): return lax.all_to_all(spread, AXES, 0, 0, tiled=True)]
  transfers between devices with their start and end apart: 42 -> 29, of which waited for: 29 -> 18; matrix products, arithmetic and copies ran while one was open for 16% -> 2% of each run, Pallas kernels for 0% -> 23%
where the time goes in v1:
time: 218 us; the launch traced here: 217 us
  Pallas kernels  92 us (42%)
  starting transfers between devices  51.2 us (23%)
  waiting for transfers between devices  41.1 us (19%)
  local copies, waits for them, and re-layouts  31.5 us (14%)
    pallas_call x28, Pallas kernels, run(): pl.pallas_call(body, out_shape=[jax.ShapeDtypeStruct(x.shape, x.dtype) fo...  92 us
    ppermute x25, waiting for transfers between devices, shifted(): lax.ppermute(value, axis, [(i, (i + step) % size) for i in range(size)])  41.1 us
    ppermute x25, starting transfers between devices, shifted(): lax.ppermute(value, axis, [(i, (i + step) % size) for i in range(size)])  34.5 us
    unnamed x68, local copies, waits for them, and re-layouts  17.8 us
    all_to_all x4, starting transfers between devices, gathered(): return lax.all_to_all(spread, AXES, 0, 0, tiled=True)  16.7 us
    broadcast_in_dim x4, local copies, waits for them, and re-layouts, gathered(): spread = jnp.broadcast_to(block[None], (count, *block.shape))  5.94 us
  transfers between devices with their start and end apart: 29, of which 18 were waited for; matrix products, arithmetic and copies ran while one was open for 2% of the time, Pallas kernels for 23%

profile of v1, /device:TPU:0, one launch (start us, length us, event | category | flops | bytes accessed | tf_op | source)
XLA Modules:
  0.0 216.7 jit_solution(3990896048205284216)
XLA Ops:
  3.9 3.2 %copy.24 = f32[1,1,1,729,729]{4,3,2,1,0:T(8,128)} copy(f32[1,1,1,729,729]{4,2,3,1,0:T(1,128)} %param.13) | data formatting | bytes 4251528
  8.5 11.9 %shard_map.131 = (f32[400,400]{1,0:T(8,128)}, f32[343,400]{1,0:T(8,128)}, f32[400,128]{1,0:T(8,128)}, f32[343,128]{1,0:T(8,128)}, f32[343,128]{1,0:T(8,128)}, /*...) custom-call(f32[729,729]{1,0:T(8,128)} %bitcast.18, ...), custom_call_target="tpu_custom_call" | custom-call | flops 10000000 | bytes 5249892 | tf_op jit(solution)/shard_map/pallas_call | solution.py:39
  22.1 7.3 %all-to-all-start.1 = ((f32[32,24,128]{2,1,0:T(8,128)}), f32[32,24,128]{2,1,0:T(8,128)S(1)}, u32[]{:S(2)}, u32[]{:S(2)}) async-start(f32[32,24,128]{2,1,0:T(8,128)} %broadcast_in_dim.9), calls=%async_computation.1 | async-start | bytes 786432 | tf_op jit(solution)/shard_map/all_to_all | solution.py:138
  39.4 4.9 %collective-permute-done.1.refs_1_ = f32[288,128]{1,0:T(8,128)S(1)} collective-permute-done((f32[288,128]{1,0:T(8,128)}, f32[288,128]{1,0:T(8,128)S(1)}, u32[]{:S(2)}, u32[]{:S(2)}) %collective-permute-start.1) | collective-permute-done | bytes 147488 | tf_op jit(solution)/shard_map/ppermute | solution.py:128
  44.3 2.9 %collective-permute-done.2.refs_2_ = f32[288,128]{1,0:T(8,128)S(1)} collective-permute-done((f32[288,128]{1,0:T(8,128)}, f32[288,128]{1,0:T(8,128)S(1)}, u32[]{:S(2)}, u32[]{:S(2)}) %collective-permute-start.2) | collective-permute-done | bytes 147488 | tf_op jit(solution)/shard_map/ppermute | solution.py:128
  54.4 5.7 %shard_map.135.refs_5_ = f32[400,400]{1,0:T(8,128)} custom-call(f32[729,729]{1,0:T(8,128)} %bitcast.17, s32[400,1]{1,0:T(8,128)} %constant.37.clone.refs_4_.refs_1_, f32[400,1]{1,0:T(8,128)} %constant.39.clone.refs_2_, f32[1,400]{1,0:T(1,128)} %constant.40.clone.refs_6_.refs_3_), custom_call_target="tpu_custom_call" | custom-call | flops 10000000 | bytes 2770564 | tf_op jit(solution)/shard_map/pallas_call | solution.py:39
  60.8 3.1 %shard_map.136 = (f32[400,128]{1,0:T(8,128)}, f32[400,128]{1,0:T(8,128)}, f32[400,128]{1,0:T(8,128)}, f32[24,128]{1,0:T(8,128)}) custom-call(f32[576,128]{1,0:T(8,128)} %get-tuple-element.67.refs_0_, f32[176,128]{1,0:T(8,128)} %copy-done.17, f32[176,128]{1,0:T(8,128)} %copy-done.18, f32[400,128]{1,0:T(8,128)} %get-tuple-element.62.refs_0_.refs_3_.refs_8_, ...), custom_call_target="tpu_custom_call" | custom-call | flops 10000000 | bytes 2189824 | tf_op jit(solution)/shard_map/pallas_call | solution.py:39
  65.3 2.9 %all-to-all-start = ((f32[32,24,128]{2,1,0:T(8,128)}), f32[32,24,128]{2,1,0:T(8,128)S(1)}, u32[]{:S(2)}, u32[]{:S(2)}) async-start(f32[32,24,128]{2,1,0:T(8,128)} %broadcast_in_dim.8), calls=%async_computation | async-start | bytes 786432 | tf_op jit(solution)/shard_map/all_to_all | solution.py:138
  77.6 3.8 %collective-permute-done.6.refs_1_ = f32[144,128]{1,0:T(8,128)S(1)} collective-permute-done((f32[144,128]{1,0:T(8,128)}, f32[144,128]{1,0:T(8,128)S(1)}, u32[]{:S(2)}, u32[]{:S(2)}) %collective-permute-start.6) | collective-permute-done | bytes 73760 | tf_op jit(solution)/shard_map/ppermute | solution.py:128
  87.8 13.2 %shard_map.140.refs_2_ = f32[128,128]{1,0:T(8,128)} custom-call(s32[768,1]{1,0:T(8,128)} %constant.36.clone.refs_0_, f32[768,128]{1,0:T(8,128)} %bitcast.24), custom_call_target="tpu_custom_call" | custom-call | flops 10000000 | bytes 461824 | tf_op jit(solution)/shard_map/pallas_call | solution.py:39
  101.8 2.9 %shard_map.141.refs_4_ = f32[400,128]{1,0:T(8,128)} custom-call(s32[768,1]{1,0:T(8,128)} %constant.36.clone.refs_0_, f32[768,128]{1,0:T(8,128)} %bitcast.23, f32[128,128]{1,0:T(8,128)} %shard_map.140.refs_2_, f32[400,128]{1,0:T(8,128)} %get-tuple-element.80.refs_3_), custom_call_target="tpu_custom_call" | custom-call | flops 10000000 | bytes 871424 | tf_op jit(solution)/shard_map/pallas_call | solution.py:39
  105.3 6.0 %shard_map.142 = (f32[400,128]{1,0:T(8,128)}, f32[400,128]{1,0:T(8,128)}, f32[343,128]{1,0:T(8,128)}, f32[2,128]{1,0:T(2,128)}) custom-call(f32[288,128]{1,0:T(8,128)} %get-tuple-element.75.refs_0_, f32[88,128]{1,0:T(8,128)} %copy-done.28, f32[88,128]{1,0:T(8,128)} %copy-done.29, f32[400,128]{1,0:T(8,128)} %get-tuple-element.71.refs_0_.refs_3_, ...), custom_call_target="tpu_custom_call" | custom-call | flops 10000000 | bytes 3098116 | tf_op jit(solution)/shard_map/pallas_call | solution.py:39
  121.3 4.9 %collective-permute-done.11.refs_1_ = f32[288,128]{1,0:T(8,128)S(1)} collective-permute-done((f32[288,128]{1,0:T(8,128)}, f32[288,128]{1,0:T(8,128)S(1)}, u32[]{:S(2)}, u32[]{:S(2)}) %collective-permute-start.11) | collective-permute-done | bytes 147488 | tf_op jit(solution)/shard_map/ppermute | solution.py:128
  133.7 3.3 %collective-permute-done.13.refs_1_ = f32[176,128]{1,0:T(8,128)S(1)} collective-permute-done((f32[176,128]{1,0:T(8,128)}, f32[176,128]{1,0:T(8,128)S(1)}, u32[]{:S(2)}, u32[]{:S(2)}) %collective-permute-start.13) | collective-permute-done | bytes 90144 | tf_op jit(solution)/shard_map/ppermute | solution.py:128
  138.7 3.1 %shard_map.146 = (f32[400,128]{1,0:T(8,128)}, f32[400,128]{1,0:T(8,128)}, f32[400,128]{1,0:T(8,128)}, f32[24,128]{1,0:T(8,128)}) custom-call(f32[576,128]{1,0:T(8,128)} %get-tuple-element.89.refs_0_, f32[176,128]{1,0:T(8,128)} %copy-done.15, f32[176,128]{1,0:T(8,128)} %copy-done.16, f32[400,128]{1,0:T(8,128)} %get-tuple-element.84.refs_0_.refs_3_.refs_11_, ...), custom_call_target="tpu_custom_call" | custom-call | flops 10000000 | bytes 2190848 | tf_op jit(solution)/shard_map/pallas_call | solution.py:39
  143.2 3.2 %all-to-all-start.2 = ((f32[32,24,128]{2,1,0:T(8,128)}), f32[32,24,128]{2,1,0:T(8,128)S(1)}, u32[]{:S(2)}, u32[]{:S(2)}) async-start(f32[32,24,128]{2,1,0:T(8,128)} %broadcast_in_dim.10), calls=%async_computation.2 | async-start | bytes 786432 | tf_op jit(solution)/shard_map/all_to_all | solution.py:138
  155.8 3.7 %collective-permute-done.16.refs_1_ = f32[144,128]{1,0:T(8,128)S(1)} collective-permute-done((f32[144,128]{1,0:T(8,128)}, f32[144,128]{1,0:T(8,128)S(1)}, u32[]{:S(2)}, u32[]{:S(2)}) %collective-permute-start.16) | collective-permute-done | bytes 73760 | tf_op jit(solution)/shard_map/ppermute | solution.py:128
  169.6 2.9 %shard_map.150.refs_4_ = f32[400,128]{1,0:T(8,128)} custom-call(s32[768,1]{1,0:T(8,128)} %constant.36.clone.refs_0_, f32[768,128]{1,0:T(8,128)} %bitcast.22, f32[128,128]{1,0:T(8,128)} %shard_map.140.refs_2_, f32[400,128]{1,0:T(8,128)} %get-tuple-element.80.refs_3_), custom_call_target="tpu_custom_call" | custom-call | flops 10000000 | bytes 871424 | tf_op jit(solution)/shard_map/pallas_call | solution.py:39
  173.1 6.1 %shard_map.152 = (f32[400,128]{1,0:T(8,128)}, f32[400,128]{1,0:T(8,128)}, f32[343,128]{1,0:T(8,128)}, f32[8,128]{1,0:T(8,128)}) custom-call(f32[288,128]{1,0:T(8,128)} %get-tuple-element.97.refs_0_, f32[88,128]{1,0:T(8,128)} %copy-done.30, f32[88,128]{1,0:T(8,128)} %copy-done.31, f32[400,128]{1,0:T(8,128)} %get-tuple-element.93.refs_0_.refs_3_, ...), custom_call_target="tpu_custom_call" | custom-call | flops 10000000 | bytes 3511812 | tf_op jit(solution)/shard_map/pallas_call | solution.py:39
  182.2 3.2 %all-to-all-start.3 = ((f32[32,8,128]{2,1,0:T(8,128)}), f32[32,8,128]{2,1,0:T(8,128)S(1)}, u32[]{:S(2)}, u32[]{:S(2)}) async-start(f32[32,8,128]{2,1,0:T(8,128)} %broadcast_in_dim.11), calls=%async_computation.3 | async-start | bytes 262144 | tf_op jit(solution)/shard_map/all_to_all | solution.py:138
  191.6 2.8 %collective-permute-done.21.refs_1_ = f32[144,128]{1,0:T(8,128)S(1)} collective-permute-done((f32[144,128]{1,0:T(8,128)}, f32[144,128]{1,0:T(8,128)S(1)}, u32[]{:S(2)}, u32[]{:S(2)}) %collective-permute-start.21) | collective-permute-done | bytes 73760 | tf_op jit(solution)/shard_map/ppermute | solution.py:128
  204.1 2.6 %shard_map.156 = (f32[400,128]{1,0:T(8,128)}, f32[343,128]{1,0:T(8,128)}, f32[400,128]{1,0:T(8,128)}, f32[343,128]{1,0:T(8,128)}) custom-call(f32[288,128]{1,0:T(8,128)} %get-tuple-element.106.refs_0_, f32[88,128]{1,0:T(8,128)} %copy-done.26, f32[88,128]{1,0:T(8,128)} %copy-done.27, f32[400,128]{1,0:T(8,128)} %get-tuple-element.102.refs_0_.refs_3_, ...), custom_call_target="tpu_custom_call" | custom-call | flops 10000000 | bytes 3061760 | tf_op jit(solution)/shard_map/pallas_call | solution.py:39
  206.8 3.1 %shard_map.158 = f32[729,128]{1,0:T(8,128)} custom-call(f32[400,128]{1,0:T(8,128)} %get-tuple-element.120.refs_0_, f32[343,128]{1,0:T(8,128)} %get-tuple-element.121.refs_1_, s32[729,1]{1,0:T(8,128)} %constant.41.clone.refs_2_), custom_call_target="tpu_custom_call" | custom-call | flops 10000000 | bytes 756580 | tf_op jit(solution)/shard_map/pallas_call | solution.py:39
  211.7 3.1 %shard_map.157 = f32[729,128]{1,0:T(8,128)} custom-call(f32[400,128]{1,0:T(8,128)} %get-tuple-element.118.refs_0_, f32[343,128]{1,0:T(8,128)} %get-tuple-element.119.refs_1_, s32[729,1]{1,0:T(8,128)} %constant.41.clone.refs_2_), custom_call_target="tpu_custom_call" | custom-call | flops 10000000 | bytes 756580 | tf_op jit(solution)/shard_map/pallas_call | solution.py:39
  (141 shorter events, 106.0 us)
Async XLA Ops:
  22.1 41.8 %all-to-all-start.1 = ((f32[32,24,128]{2,1,0:T(8,128)}), f32[32,24,128]{2,1,0:T(8,128)S(1)}, u32[]{:S(2)}, u32[]{:S(2)}) async-start(f32[32,24,128]{2,1,0:T(8,128)} %broadcast_in_dim.9), calls=%async_computation.1 | async-start | bytes 786432 | tf_op jit(solution)/shard_map/all_to_all | solution.py:138
  35.6 8.7 %collective-permute-start.1 = (f32[288,128]{1,0:T(8,128)}, f32[288,128]{1,0:T(8,128)S(1)}, u32[]{:S(2)}, u32[]{:S(2)}) collective-permute-start(f32[288,128]{1,0:T(8,128)} %get-tuple-element.65), channel_id=1, source_target_pairs={{0,2},{2,4},{4,6},{6,0},{1,3},{3,5},{5,7},{7,1},{8,10},{10,12},{12... | collective-permute-start | bytes 442376 | tf_op jit(solution)/shard_map/ppermute | solution.py:128
  37.4 9.9 %collective-permute-start.2 = (f32[288,128]{1,0:T(8,128)}, f32[288,128]{1,0:T(8,128)S(1)}, u32[]{:S(2)}, u32[]{:S(2)}) collective-permute-start(f32[288,128]{1,0:T(8,128)} %get-tuple-element.66), channel_id=1, source_target_pairs={{0,6},{2,0},{4,2},{6,4},{1,7},{3,1},{5,3},{7,5},{8,14},{10,8},{12,... | collective-permute-start | bytes 442376 | tf_op jit(solution)/shard_map/ppermute | solution.py:128
  50.0 10.1 %collective-permute-start.3 = (f32[176,128]{1,0:T(8,128)}, f32[176,128]{1,0:T(8,128)S(1)}, u32[]{:S(2)}, u32[]{:S(2)}) collective-permute-start(f32[176,128]{1,0:T(8,128)} %get-tuple-element.68), channel_id=1, source_target_pairs={{0,8},{8,16},{16,24},{24,0},{1,9},{9,17},{17,25},{25,1},{2,10},{10... | collective-permute-start | bytes 270344 | tf_op jit(solution)/shard_map/ppermute | solution.py:128
  51.4 8.7 %collective-permute-start.4 = (f32[176,128]{1,0:T(8,128)}, f32[176,128]{1,0:T(8,128)S(1)}, u32[]{:S(2)}, u32[]{:S(2)}) collective-permute-start(f32[176,128]{1,0:T(8,128)} %get-tuple-element.69), channel_id=1, source_target_pairs={{0,24},{8,0},{16,8},{24,16},{1,25},{9,1},{17,9},{25,17},{2,26},{10... | collective-permute-start | bytes 270344 | tf_op jit(solution)/shard_map/ppermute | solution.py:128
  65.3 35.7 %all-to-all-start = ((f32[32,24,128]{2,1,0:T(8,128)}), f32[32,24,128]{2,1,0:T(8,128)S(1)}, u32[]{:S(2)}, u32[]{:S(2)}) async-start(f32[32,24,128]{2,1,0:T(8,128)} %broadcast_in_dim.8), calls=%async_computation | async-start | bytes 786432 | tf_op jit(solution)/shard_map/all_to_all | solution.py:138
  73.8 7.6 %collective-permute-start.6 = (f32[144,128]{1,0:T(8,128)}, f32[144,128]{1,0:T(8,128)S(1)}, u32[]{:S(2)}, u32[]{:S(2)}) collective-permute-start(f32[144,128]{1,0:T(8,128)} %get-tuple-element.73), channel_id=1, source_target_pairs={{0,2},{2,4},{4,6},{6,0},{1,3},{3,5},{5,7},{7,1},{8,10},{10,12},{12... | collective-permute-start | bytes 221192 | tf_op jit(solution)/shard_map/ppermute | solution.py:128
  75.6 6.9 %collective-permute-start.7 = (f32[144,128]{1,0:T(8,128)}, f32[144,128]{1,0:T(8,128)S(1)}, u32[]{:S(2)}, u32[]{:S(2)}) collective-permute-start(f32[144,128]{1,0:T(8,128)} %get-tuple-element.74), channel_id=1, source_target_pairs={{0,6},{2,0},{4,2},{6,4},{1,7},{3,1},{5,3},{7,5},{8,14},{10,8},{12,... | collective-permute-start | bytes 221192 | tf_op jit(solution)/shard_map/ppermute | solution.py:128
  84.9 19.8 %collective-permute-start.8 = (f32[88,128]{1,0:T(8,128)}, f32[88,128]{1,0:T(8,128)S(1)}, u32[]{:S(2)}, u32[]{:S(2)}) collective-permute-start(f32[88,128]{1,0:T(8,128)} %get-tuple-element.76), channel_id=1, source_target_pairs={{0,8},{8,16},{16,24},{24,0},{1,9},{9,17},{17,25},{25,1},{2,10},{10... | collective-permute-start | bytes 135176 | tf_op jit(solution)/shard_map/ppermute | solution.py:128
  86.3 18.4 %collective-permute-start.9 = (f32[88,128]{1,0:T(8,128)}, f32[88,128]{1,0:T(8,128)S(1)}, u32[]{:S(2)}, u32[]{:S(2)}) collective-permute-start(f32[88,128]{1,0:T(8,128)} %get-tuple-element.77), channel_id=1, source_target_pairs={{0,24},{8,0},{16,8},{24,16},{1,25},{9,1},{17,9},{25,17},{2,26},{10... | collective-permute-start | bytes 135176 | tf_op jit(solution)/shard_map/ppermute | solution.py:128
  117.5 8.8 %collective-permute-start.11 = (f32[288,128]{1,0:T(8,128)}, f32[288,128]{1,0:T(8,128)S(1)}, u32[]{:S(2)}, u32[]{:S(2)}) collective-permute-start(f32[288,128]{1,0:T(8,128)} %get-tuple-element.87), channel_id=1, source_target_pairs={{0,2},{2,4},{4,6},{6,0},{1,3},{3,5},{5,7},{7,1},{8,10},{10,12},{12... | collective-permute-start | bytes 442376 | tf_op jit(solution)/shard_map/ppermute | solution.py:128
  119.1 9.0 %collective-permute-start.12 = (f32[288,128]{1,0:T(8,128)}, f32[288,128]{1,0:T(8,128)S(1)}, u32[]{:S(2)}, u32[]{:S(2)}) collective-permute-start(f32[288,128]{1,0:T(8,128)} %get-tuple-element.88), channel_id=1, source_target_pairs={{0,6},{2,0},{4,2},{6,4},{1,7},{3,1},{5,3},{7,5},{8,14},{10,8},{12,... | collective-permute-start | bytes 442376 | tf_op jit(solution)/shard_map/ppermute | solution.py:128
  130.8 6.2 %collective-permute-start.13 = (f32[176,128]{1,0:T(8,128)}, f32[176,128]{1,0:T(8,128)S(1)}, u32[]{:S(2)}, u32[]{:S(2)}) collective-permute-start(f32[176,128]{1,0:T(8,128)} %get-tuple-element.90), channel_id=1, source_target_pairs={{0,8},{8,16},{16,24},{24,0},{1,9},{9,17},{17,25},{25,1},{2,10},{10... | collective-permute-start | bytes 270344 | tf_op jit(solution)/shard_map/ppermute | solution.py:128
  131.3 6.7 %collective-permute-start.14 = (f32[176,128]{1,0:T(8,128)}, f32[176,128]{1,0:T(8,128)S(1)}, u32[]{:S(2)}, u32[]{:S(2)}) collective-permute-start(f32[176,128]{1,0:T(8,128)} %get-tuple-element.91), channel_id=1, source_target_pairs={{0,24},{8,0},{16,8},{24,16},{1,25},{9,1},{17,9},{25,17},{2,26},{10... | collective-permute-start | bytes 270344 | tf_op jit(solution)/shard_map/ppermute | solution.py:128
  143.2 22.8 %all-to-all-start.2 = ((f32[32,24,128]{2,1,0:T(8,128)}), f32[32,24,128]{2,1,0:T(8,128)S(1)}, u32[]{:S(2)}, u32[]{:S(2)}) async-start(f32[32,24,128]{2,1,0:T(8,128)} %broadcast_in_dim.10), calls=%async_computation.2 | async-start | bytes 786432 | tf_op jit(solution)/shard_map/all_to_all | solution.py:138
  152.0 7.6 %collective-permute-start.16 = (f32[144,128]{1,0:T(8,128)}, f32[144,128]{1,0:T(8,128)S(1)}, u32[]{:S(2)}, u32[]{:S(2)}) collective-permute-start(f32[144,128]{1,0:T(8,128)} %get-tuple-element.95), channel_id=1, source_target_pairs={{0,2},{2,4},{4,6},{6,0},{1,3},{3,5},{5,7},{7,1},{8,10},{10,12},{12... | collective-permute-start | bytes 221192 | tf_op jit(solution)/shard_map/ppermute | solution.py:128
  153.8 6.9 %collective-permute-start.17 = (f32[144,128]{1,0:T(8,128)}, f32[144,128]{1,0:T(8,128)S(1)}, u32[]{:S(2)}, u32[]{:S(2)}) collective-permute-start(f32[144,128]{1,0:T(8,128)} %get-tuple-element.96), channel_id=1, source_target_pairs={{0,6},{2,0},{4,2},{6,4},{1,7},{3,1},{5,3},{7,5},{8,14},{10,8},{12,... | collective-permute-start | bytes 221192 | tf_op jit(solution)/shard_map/ppermute | solution.py:128
  163.1 9.4 %collective-permute-start.18 = (f32[88,128]{1,0:T(8,128)}, f32[88,128]{1,0:T(8,128)S(1)}, u32[]{:S(2)}, u32[]{:S(2)}) collective-permute-start(f32[88,128]{1,0:T(8,128)} %get-tuple-element.98), channel_id=1, source_target_pairs={{0,8},{8,16},{16,24},{24,0},{1,9},{9,17},{17,25},{25,1},{2,10},{10... | collective-permute-start | bytes 135176 | tf_op jit(solution)/shard_map/ppermute | solution.py:128
  164.6 7.9 %collective-permute-start.19 = (f32[88,128]{1,0:T(8,128)}, f32[88,128]{1,0:T(8,128)S(1)}, u32[]{:S(2)}, u32[]{:S(2)}) collective-permute-start(f32[88,128]{1,0:T(8,128)} %get-tuple-element.99), channel_id=1, source_target_pairs={{0,24},{8,0},{16,8},{24,16},{1,25},{9,1},{17,9},{25,17},{2,26},{10... | collective-permute-start | bytes 135176 | tf_op jit(solution)/shard_map/ppermute | solution.py:128
  180.8 4.6 %collective-permute-start.20 = (f32[288,128]{1,0:T(8,128)}, f32[288,128]{1,0:T(8,128)S(1)}, u32[]{:S(2)}, u32[]{:S(2)}) collective-permute-start(f32[288,128]{1,0:T(8,128)} %shard_map.153.refs_0_), channel_id=1, source_target_pairs={{0,1},{1,0},{2,3},{3,2},{4,5},{5,4},{6,7},{7,6},{8,9},{9,8},{10,11... | collective-permute-start | bytes 442376 | tf_op jit(solution)/shard_map/ppermute | solution.py:128
  182.2 18.6 %all-to-all-start.3 = ((f32[32,8,128]{2,1,0:T(8,128)}), f32[32,8,128]{2,1,0:T(8,128)S(1)}, u32[]{:S(2)}, u32[]{:S(2)}) async-start(f32[32,8,128]{2,1,0:T(8,128)} %broadcast_in_dim.11), calls=%async_computation.3 | async-start | bytes 262144 | tf_op jit(solution)/shard_map/all_to_all | solution.py:138
  187.8 6.6 %collective-permute-start.21 = (f32[144,128]{1,0:T(8,128)}, f32[144,128]{1,0:T(8,128)S(1)}, u32[]{:S(2)}, u32[]{:S(2)}) collective-permute-start(f32[144,128]{1,0:T(8,128)} %get-tuple-element.104), channel_id=1, source_target_pairs={{0,2},{2,4},{4,6},{6,0},{1,3},{3,5},{5,7},{7,1},{8,10},{10,12},{12... | collective-permute-start | bytes 221192 | tf_op jit(solution)/shard_map/ppermute | solution.py:128
  189.6 5.8 %collective-permute-start.22 = (f32[144,128]{1,0:T(8,128)}, f32[144,128]{1,0:T(8,128)S(1)}, u32[]{:S(2)}, u32[]{:S(2)}) collective-permute-start(f32[144,128]{1,0:T(8,128)} %get-tuple-element.105), channel_id=1, source_target_pairs={{0,6},{2,0},{4,2},{6,4},{1,7},{3,1},{5,3},{7,5},{8,14},{10,8},{12,... | collective-permute-start | bytes 221192 | tf_op jit(solution)/shard_map/ppermute | solution.py:128
  197.8 5.2 %collective-permute-start.23 = (f32[88,128]{1,0:T(8,128)}, f32[88,128]{1,0:T(8,128)S(1)}, u32[]{:S(2)}, u32[]{:S(2)}) collective-permute-start(f32[88,128]{1,0:T(8,128)} %get-tuple-element.107), channel_id=1, source_target_pairs={{0,8},{8,16},{16,24},{24,0},{1,9},{9,17},{17,25},{25,1},{2,10},{10... | collective-permute-start | bytes 135176 | tf_op jit(solution)/shard_map/ppermute | solution.py:128
  (37 other events, 100.1 us)

commit v2 on v1

v2 whole, which is shorter than its diff:
```python
import jax
import jax.numpy as jnp
import numpy as np
from jax import lax
from jax.experimental import pallas as pl
from jax.experimental.pallas import tpu as pltpu
from jax.sharding import PartitionSpec as P

AXES = ("gx", "gy", "gz")
HIGHEST = lax.Precision.HIGHEST
PALLAS = True
LIMIT = 24 * 2**20
VMEM = pltpu.VMEM
PIECES = 4
FILL = 10**8


def dot(left, right, contract=(1, 0)):
    dims = (((contract[0],), (contract[1],)), ((), ()))
    return lax.dot_general(
        left, right, dims, precision=HIGHEST, preferred_element_type=jnp.float32
    )


def whole(count):
    return [pl.BlockSpec(memory_space=VMEM)] * count


def call(body, operands, outs, scratch=(), in_hbm=(), flops=10**6):
    places = whole(len(operands))
    for index in in_hbm:
        places[index] = pl.BlockSpec(memory_space=pl.ANY)
    size = sum(4 * np.prod(x.shape) for x in (*operands, *outs))
    return pl.pallas_call(
        body,
        out_shape=[jax.ShapeDtypeStruct(x.shape, x.dtype) for x in outs],
        in_specs=places,
        out_specs=whole(len(outs)),
        scratch_shapes=scratch,
        compiler_params=pltpu.CompilerParams(vmem_limit_bytes=LIMIT),
        cost_estimate=pl.CostEstimate(flops=flops, bytes_accessed=int(size), transcendentals=0),
    )(*operands)


def run(function, *operands, flops=10**6):
    if not PALLAS:
        return function(*operands)
    shapes = jax.eval_shape(function, *operands)
    single = not isinstance(shapes, tuple)
    outs = (shapes,) if single else shapes
    count = len(operands)

    def body(*refs):
        results = function(*[ref[...] for ref in refs[:count]])
        results = (results,) if single else results
        for ref, result in zip(refs[count:], results):
            ref[...] = result

    results = call(body, operands, outs, flops=flops)
    return results[0] if single else tuple(results)


def floats(*shape):
    return jax.ShapeDtypeStruct(shape, jnp.float32)


class Layout:
    def __init__(self, n):
        m = n - 1
        self.n, self.m = n, m
        self.block = n * m
        self.ring_rows = 4 * self.block
        flat = (n - 2) ** 2
        self.flat = -(-flat // 8) * 8
        self.rows = self.ring_rows + 2 * self.flat
        self.y_rows = self.block + -(-n // 8) * 8
        self.x_rows = 4 * m + self.flat
        at = lambda i, j, k: (i * n + j) * n + k
        inner = range(1, m)
        order = [at(i, j, k) for j in (0, m) for i in range(n) for k in range(m)]
        for j, k in ((0, 0), (m, m)):
            for i in range(n):
                order += [at(i, x, k) for x in inner] + [at(i, j, m)]
        for i in (0, m):
            order += [at(i, j, k) for j in inner for k in inner]
            order += [-1] * (self.flat - flat)
        self.order = np.array(order, np.int32)
        self.inner = np.array([at(i, j, k) for i in inner for j in inner for k in inner], np.int32)
        share = np.zeros((self.rows, 1), np.float32)
        for row, node in enumerate(order):
            if node >= 0:
                place = (node // (n * n), node // n % n, node % n)
                share[row] = 0.5 ** sum(x in (0, m) for x in place)
        self.share = share

    def blocks(self, ring):
        return [ring[s * self.block : (s + 1) * self.block] for s in range(4)]

    def row_in_tile(self, block):
        return lax.broadcasted_iota(jnp.int32, block.shape, 0) % self.m

    def fold_z(self, ring, below, above):
        first, last, low, high = self.blocks(ring)
        below, above = self.blocks(below), self.blocks(above)
        row = self.row_in_tile(first)
        start, end = row == 0, row == self.m - 1
        back = lambda x: roll_rows(x, x.shape[0] - (self.m - 1))
        ahead = lambda x: roll_rows(x, self.m - 1)
        zero = jnp.zeros_like(first)
        first = first + jnp.where(start, back(below[2]), zero)
        last = last + jnp.where(start, back(below[3]), zero)
        low = low + jnp.where(end, ahead(above[0]), below[3])
        high = high + jnp.where(end, ahead(above[1]), above[2])
        return jnp.concatenate([first, last, low, high], axis=0)

    def side(self, block, corners):
        lanes = block.shape[1]
        rows = corners.reshape(self.n, self.m, lanes)[:, self.m - 1, :]
        fill = jnp.zeros((self.y_rows - self.block - self.n, lanes), block.dtype)
        return jnp.concatenate([block, rows, fill], axis=0)

    def sides_y(self, ring):
        first, last, low, high = self.blocks(ring)
        return self.side(first, low), self.side(last, high)

    def fold_y(self, ring, below, above):
        first, last, low, high = self.blocks(ring)
        lanes = ring.shape[1]
        end = self.row_in_tile(first) == self.m - 1

        def ends(message):
            rows = message[self.block : self.block + self.n].reshape(self.n, 1, lanes)
            wide = jnp.broadcast_to(rows, (self.n, self.m, lanes)).reshape(self.block, lanes)
            return jnp.where(end, wide, jnp.zeros_like(wide))

        first = first + below[: self.block]
        low = low + ends(below)
        last = last + above[: self.block]
        high = high + ends(above)
        return jnp.concatenate([first, last, low, high], axis=0)

    def sides_x(self, ring, flat):
        m, block = self.m, self.block
        low = [ring[s * block : s * block + m] for s in range(4)] + [flat[: self.flat]]
        high = [ring[(s + 1) * block - m : (s + 1) * block] for s in range(4)] + [flat[self.flat :]]
        return jnp.concatenate(low, axis=0), jnp.concatenate(high, axis=0)

    def fold_x(self, ring, flat, below, above):
        m, block = self.m, self.block
        parts = []
        for s in range(4):
            parts += [
                ring[s * block : s * block + m] + below[s * m : (s + 1) * m],
                ring[s * block + m : (s + 1) * block - m],
                ring[(s + 1) * block - m : (s + 1) * block] + above[s * m : (s + 1) * m],
            ]
        parts += [flat[: self.flat] + below[4 * m :], flat[self.flat :] + above[4 * m :]]
        return jnp.concatenate(parts, axis=0)


def roll_rows(value, shift):
    if PALLAS:
        return pltpu.roll(value, shift, 0)
    return jnp.roll(value, shift, axis=0)


def shifted(value, axis, step):
    size = lax.axis_size(axis)
    return lax.ppermute(value, axis, [(i, (i + step) % size) for i in range(size)])


def both_ways(low, high, axis):
    return shifted(high, axis, 1), shifted(low, axis, -1)


def cat(parts):
    return parts[0] if len(parts) == 1 else jnp.concatenate(parts, axis=0)


def assemble(layout, fields, extra, function, flops=10**6):
    count = len(fields)
    rings, rows = layout.ring_rows, layout.rows

    sent = fields if count == 1 else [cat([f[:rings] for f in fields])]
    message = sent[0][:rings] if count == 1 else sent[0]
    if lax.axis_size("gz") == 2:
        others = (shifted(message, "gz", 1),)
    else:
        others = (shifted(message, "gz", 1), shifted(message, "gz", -1))

    def after_z(*values):
        fields, others = values[:count], values[count:]
        done, low, high = [], [], []
        for index, field in enumerate(fields):
            place = slice(index * rings, (index + 1) * rings)
            ring = layout.fold_z(field[:rings], others[0][place], others[-1][place])
            sides = layout.sides_y(ring)
            done.append(ring)
            low.append(sides[0])
            high.append(sides[1])
        return cat(done), cat(low), cat(high)

    ring, low, high = run(after_z, *fields, *others)
    below, above = both_ways(low, high, "gy")

    def after_y(ring, below, above, *fields):
        done, low, high = [], [], []
        for index, field in enumerate(fields):
            place = slice(index * layout.y_rows, (index + 1) * layout.y_rows)
            one = ring[index * rings : (index + 1) * rings]
            one = layout.fold_y(one, below[place], above[place])
            sides = layout.sides_x(one, field[rings:])
            done.append(one)
            low.append(sides[0])
            high.append(sides[1])
        return cat(done), cat(low), cat(high)

    ring, low, high = run(after_y, ring, below, above, *fields)
    below, above = both_ways(low, high, "gx")

    def after_x(ring, below, above, *rest):
        fields, rest = rest[:count], rest[count:]
        done = []
        for index, field in enumerate(fields):
            place = slice(index * layout.x_rows, (index + 1) * layout.x_rows)
            one = ring[index * rings : (index + 1) * rings]
            done.append(layout.fold_x(one, field[rings:], below[place], above[place]))
        return function(*done, *rest)

    return run(after_x, ring, below, above, *fields, *extra, flops=flops)


def parts_of(value):
    high = value.astype(jnp.bfloat16)
    rest = value - high.astype(jnp.float32)
    middle = rest.astype(jnp.bfloat16)
    low = (rest - middle.astype(jnp.float32)).astype(jnp.bfloat16)
    return high, middle, low


def pick(left, right, contract=(1, 0)):
    dims = (((contract[0],), (contract[1],)), ((), ()))
    if left.dtype == jnp.bfloat16:
        pairs = [(left, part) for part in parts_of(right)]
    else:
        pairs = [(part, right) for part in parts_of(left)]
    terms = [lax.dot_general(a, b, dims, preferred_element_type=jnp.float32) for a, b in pairs]
    return terms[0] + terms[1] + terms[2]


def one_hot_rows(column, count):
    lanes = lax.broadcasted_iota(jnp.int32, (column.shape[0], count), 1).astype(jnp.float32)
    return jnp.where(lanes == column, 1.0, 0.0).astype(jnp.bfloat16)


def one_hot_columns(row, count):
    places = lax.broadcasted_iota(jnp.int32, (count, row.shape[1]), 0).astype(jnp.float32)
    return jnp.where(places == row, 1.0, 0.0).astype(jnp.bfloat16)


def as_column(row):
    return jnp.broadcast_to(row, (8, row.shape[1])).T[:, :1]


def coarse_table(count_x, count_y, count_z, rows):
    total = count_x * count_y * count_z
    linear = np.arange(total)
    along = (linear // (count_y * count_z), linear // count_z % count_y, linear % count_z)

    def vertex(sx, sy, sz):
        x, y, z = along
        return ((x + sx) % count_x * count_y + (y + sy) % count_y) * count_z + (z + sz) % count_z

    two = (0, 1)
    listed = [vertex(sx, sy, sz) for sx in two for sy in two for sz in two]
    listed += [total + vertex(0, sy, sz) for sy in two for sz in two]
    listed += [2 * total + vertex(sx, 0, sz) for sx in two for sz in two]
    listed += [3 * total + vertex(sx, sy, 0) for sx in two for sy in two]
    table = np.full((total, rows), -1, np.float32)
    table[:, : len(listed)] = np.stack(listed, axis=-1)
    return table


def eliminate(matrix, pivots):
    count = matrix.shape[0]
    rows = lax.broadcasted_iota(jnp.int32, (count, 1), 0)
    lanes = lax.broadcasted_iota(jnp.int32, (1, count), 1)
    for k in pivots:
        column = matrix[:, k : k + 1]
        pivot = matrix[k : k + 1, k : k + 1]
        row = jnp.where(lanes == k, 1.0, matrix[k : k + 1, :]) / pivot
        kept = jnp.where(lanes == k, 0.0, matrix)
        factor = jnp.where(rows == k, -1.0, column)
        matrix = jnp.where(rows == k, 0.0, kept) - factor * row
    return matrix


def local(element_load, local_matrix, dirichlet_inverse, neumann_inverse, coarse_basis):
    n = element_load.shape[0]
    lanes = element_load.shape[3]
    nodes = n**3
    layout = Layout(n)
    inside = (n - 2) ** 3
    primal = coarse_basis.shape[3]
    counts = [lax.axis_size(axis) for axis in AXES]
    devices = counts[0] * counts[1] * counts[2]
    coarse = 4 * devices
    chunk = -(-primal // 8) * 8
    rows = layout.rows
    table = coarse_table(*counts, chunk)
    own_table = jnp.asarray(np.pad(table, ((0, 0), (0, 128 - chunk)), constant_values=-1))
    all_ids = jnp.asarray(table.reshape(1, -1))
    places = np.stack([layout.order.astype(np.float32), layout.share[:, 0]])
    places = jnp.asarray(np.pad(places, ((0, 6), (0, 0))))
    pairs = [(i, j) for i in range(n) for j in range(n)]
    inner_pairs = [(i, j) for i in range(1, n - 1) for j in range(1, n - 1)]
    deep = n - 2

    def spread_out(block):
        return jnp.broadcast_to(block[None], (devices, *block.shape))

    def start(
        load_in, matrix_in, inverse_in, neumann_in, basis_in, places, own_table,
        condensed, spread, load_surface, load_inside, begun, tau, weighted, coarse_rows,
        matrix, inverse, neumann, load, natural, begun_natural, sems,
    ):
        moves = [
            pltpu.make_async_copy(source, target, sems.at[index])
            for index, (source, target) in enumerate(
                (
                    (load_in, load),
                    (inverse_in.at[0, 0, 0], inverse),
                    (matrix_in.at[0, 0, 0], matrix),
                    (neumann_in.at[0, 0, 0], neumann),
                )
            )
        ]
        for move in moves:
            move.start()
        order = places[0:1, :]
        surface = one_hot_rows(as_column(order), nodes)
        across = one_hot_columns(order, nodes)
        moves[0].wait()
        for i, j in pairs:
            natural[pl.ds((i * n + j) * n, n), :] = load[i, j]
        for index, (i, j) in enumerate(inner_pairs):
            load_inside[pl.ds(index * deep, deep), :] = load[i, j, pl.ds(1, deep), :]
        moves[1].wait()
        begun[...] = dot(inverse[...], load_inside[...])
        tau[...] = jnp.sum(load_inside[...] * begun[...], axis=0, keepdims=True)
        begun_natural[...] = jnp.zeros_like(begun_natural)
        for index, (i, j) in enumerate(inner_pairs):
            begun_natural[pl.ds((i * n + j) * n + 1, deep), :] = begun[pl.ds(index * deep, deep), :]
        basis = jnp.concatenate(
            [basis_in[0, 0, 0], jnp.zeros((chunk - primal, nodes), jnp.float32)], axis=0
        )
        weighted[...] = pick(basis, across) * places[1:2, :]
        own = one_hot_rows(as_column(own_table[pl.ds(lax.axis_index(AXES), 1), :])[:chunk], coarse)
        spread[...] = pick(weighted[...], own, (0, 0))
        wide = jnp.concatenate([basis, jnp.zeros((128 - chunk, nodes), jnp.float32)], axis=0).T
        moves[2].wait()
        images = dot(matrix[...], jnp.concatenate([begun_natural[...], wide], axis=1))
        both = jnp.concatenate([natural[...], natural[...] - images[:, :lanes]], axis=1)
        both = pick(surface, both)
        load_surface[...] = both[:, :lanes]
        condensed[...] = both[:, lanes:]
        coarse_local = dot(basis, images[:, lanes:])
        coarse_rows[...] = spread_out(pick(coarse_local[:, :chunk], own))
        moves[3].wait()

    (
        condensed, spread, load_surface, load_inside, begun, tau, weighted, coarse_rows,
        matrix, inverse, neumann,
    ) = call(
        start,
        (element_load, local_matrix, dirichlet_inverse, neumann_inverse, coarse_basis, places, own_table),
        (
            floats(rows, lanes), floats(rows, coarse), floats(rows, lanes), floats(inside, lanes),
            floats(inside, lanes), floats(1, lanes), floats(chunk, rows),
            floats(devices, chunk, coarse), floats(nodes, nodes), floats(inside, inside),
            floats(nodes, nodes),
        ),
        scratch=[
            VMEM((n, n, n, lanes), jnp.float32), VMEM((nodes, lanes), jnp.float32),
            VMEM((nodes, lanes), jnp.float32), pltpu.SemaphoreType.DMA((4,)),
        ],
        in_hbm=(0, 1, 2, 3),
    )

    coarse_all = lax.all_to_all(coarse_rows, AXES, 0, 0, tiled=True).reshape(-1, coarse)

    def reorder(neumann, places):
        order, share = places[0:1, :], places[1:2, :]
        across = one_hot_columns(order, nodes)
        surface = one_hot_rows(as_column(order), nodes)
        return pick(surface, pick(neumann, across)) * as_column(share) * share

    scaled = run(reorder, neumann, places, flops=FILL)

    def condense(matrix, inverse, places):
        order = places[0:1, :]
        picked = pick(matrix, one_hot_columns(order, nodes))
        surface = one_hot_rows(as_column(order), nodes)
        within = pick(surface, picked)
        coupling = jnp.concatenate(
            [picked[(i * n + j) * n + 1 : (i * n + j) * n + 1 + deep] for i, j in inner_pairs], axis=0
        )
        return within - dot(coupling, dot(inverse, coupling), (0, 0)), coupling

    schur, coupling = run(condense, matrix, inverse, places, flops=FILL)

    def gather_sum(all_ids, rows):
        return pick(one_hot_columns(all_ids, coarse), rows)

    if coarse <= 128:
        step = coarse // PIECES

        def first_piece(all_ids, rows):
            return eliminate(gather_sum(all_ids, rows), range(step))

        coarse_inverse = run(first_piece, all_ids, coarse_all, flops=FILL)
        for piece in range(1, PIECES):

            def next_piece(matrix, piece=piece):
                return eliminate(matrix, range(piece * step, (piece + 1) * step))

            coarse_inverse = run(next_piece, coarse_inverse, flops=FILL)
    else:
        factor = jnp.linalg.cholesky(run(gather_sum, all_ids, coarse_all))
        coarse_inverse = jax.scipy.linalg.cho_solve(
            (factor, True), jnp.eye(coarse, dtype=jnp.float32)
        )

    def neumann_step(field, scaled, weighted):
        return dot(scaled, field), dot(weighted, field)

    def add_rows(loads, extra):
        place = lax.broadcasted_iota(jnp.int32, loads.shape, 0)
        for index in range(extra.shape[0]):
            loads = jnp.where(place == primal + index, extra[index : index + 1], loads)
        return loads

    def coarse_step(all_ids, rows, coarse_inverse, spread):
        return dot(spread, dot(coarse_inverse, gather_sum(all_ids, rows)))

    pieces = [spread[:, s : s + lanes] for s in range(0, coarse, lanes)]

    def first(field, *rest):
        pieces, (scaled, weighted) = rest[:-2], rest[-2:]
        mapped, loads = neumann_step(field, scaled, weighted)
        return (field, *pieces, mapped, spread_out(loads))

    results = assemble(layout, [condensed, *pieces], (scaled, weighted), first)
    residual, pieces, (mapped, loads) = results[0], results[1:-2], results[-2:]
    spread = jnp.concatenate(pieces, axis=1) if len(pieces) > 1 else pieces[0]

    gathered = lax.all_to_all(loads, AXES, 0, 0, tiled=True)
    coarse0 = run(coarse_step, all_ids, gathered.reshape(-1, lanes), coarse_inverse, spread)

    def apply_first(mapped, coarse, schur, condensed, tau):
        field = mapped + coarse
        image = dot(schur, field)
        energy = tau + jnp.sum(condensed * field, axis=0, keepdims=True)
        curvature = tau + jnp.sum(field * image, axis=0, keepdims=True)
        return field, image, jnp.concatenate([energy, curvature], axis=0)

    field0, image0, sums0 = assemble(
        layout, [mapped], (coarse0, schur, condensed, tau), apply_first
    )

    def second(image, load_surface, scaled, weighted, sums):
        mapped, loads = neumann_step(image, scaled, weighted)
        return image, load_surface, mapped, spread_out(add_rows(loads, sums))

    image0_sum, load_sum, mapped, loads = assemble(
        layout, [image0, load_surface], (scaled, weighted, sums0), second
    )
    gathered = lax.all_to_all(loads, AXES, 0, 0, tiled=True)

    def coarse_and_totals(all_ids, rows, coarse_inverse, spread):
        flat = rows.reshape(-1, lanes)
        totals = jnp.sum(rows, axis=0)[primal : primal + 2]
        return coarse_step(all_ids, flat, coarse_inverse, spread), totals

    coarse1, totals0 = run(coarse_and_totals, all_ids, gathered, coarse_inverse, spread)

    def apply_second(mapped, coarse, schur, condensed, tau, field0, image0, totals):
        field = mapped + coarse
        image = dot(schur, field)
        step = totals[:1] / totals[1:2]
        rest = 1.0 - step
        direction = field0 - step * field
        direction_image = image0 - step * image
        energy = rest * rest * tau + jnp.sum(
            (condensed - step * image0) * direction, axis=0, keepdims=True
        )
        curvature = rest * rest * tau + jnp.sum(
            direction * direction_image, axis=0, keepdims=True
        )
        cross = rest * tau + jnp.sum(direction * image0, axis=0, keepdims=True)
        fill = jnp.zeros((5, lanes), jnp.float32)
        sums = jnp.concatenate([energy, curvature, cross, fill], axis=0)
        return field, image, spread_out(sums)

    field1, image1, sums1 = assemble(
        layout, [mapped], (coarse1, schur, condensed, tau, field0, image0, totals0), apply_second
    )
    rows1 = lax.all_to_all(sums1, AXES, 0, 0, tiled=True)

    def weigh(totals, rows, begun, coupling, inverse, field0, field1):
        energy, curvature = totals[:1], totals[1:2]
        sums = jnp.sum(rows, axis=0)
        step = energy / curvature
        energy_next, curvature_next, cross = sums[:1], sums[1:2], sums[2:3]
        ratio = energy_next / energy
        curvature_next = curvature_next + 2.0 * ratio * cross + ratio * ratio * curvature
        step_next = energy_next / curvature_next
        first = step + step_next * (1.0 + ratio)
        second = -step_next * step
        surface = first * field0 + second * field1
        deep = (first + second) * begun - dot(inverse, dot(coupling, surface))
        return surface, deep, jnp.concatenate([first, second], axis=0)

    solution_surface, solution_inside, weights = run(
        weigh, totals0, rows1, begun, coupling, inverse, field0, field1, flops=FILL
    )

    def leftover(image1, image0, residual, load_sum, load_inside, weights):
        first, second = weights[:1], weights[1:2]
        spill = load_sum - residual
        surface = load_sum - first * (image0 + spill) - second * (image1 + spill)
        return surface, (1.0 - first - second) * load_inside

    residual_surface, residual_inside = assemble(
        layout, [image1], (image0_sum, residual, load_sum, load_inside, weights), leftover
    )

    def place(solution_surface, solution_inside, residual_surface, residual_inside, one, two):
        m, block = n - 1, layout.block
        for surface, deep_rows, out in (
            (solution_surface, solution_inside, one), (residual_surface, residual_inside, two)
        ):
            for i in range(n):
                for s, j in ((0, 0), (1, m)):
                    out[i, j, pl.ds(0, m), :] = surface[pl.ds(s * block + i * m, m), :]
                    out[i, j, pl.ds(m, 1), :] = surface[pl.ds((s + 2) * block + i * m + m - 1, 1), :]
                for j in range(1, m):
                    for s, k in ((2, 0), (3, m)):
                        out[i, j, pl.ds(k, 1), :] = surface[pl.ds(s * block + i * m + j - 1, 1), :]
                    if i in (0, m):
                        at = layout.ring_rows + (layout.flat if i else 0) + (j - 1) * deep
                        out[i, j, pl.ds(1, deep), :] = surface[pl.ds(at, deep), :]
                    else:
                        at = ((i - 1) * deep + j - 1) * deep
                        out[i, j, pl.ds(1, deep), :] = deep_rows[pl.ds(at, deep), :]

    shape = floats(*element_load.shape)
    out = call(
        place, (solution_surface, solution_inside, residual_surface, residual_inside), (shape, shape)
    )
    return out[0], out[1]


def solution(mesh):
    in_specs = (
        P("gx", "gy", "gz", None),
        P("gx", "gy", "gz", None, None),
        P("gx", "gy", "gz", None, None),
        P("gx", "gy", "gz", None, None),
        P("gx", "gy", "gz", None, None),
    )
    out_specs = (P("gx", "gy", "gz", None), P("gx", "gy", "gz", None))
    return jax.shard_map(local, mesh=mesh, in_specs=in_specs, out_specs=out_specs, check_vma=False)
```

time: 218 us -> 163 us (0.75)
  Pallas kernels: 92 us -> 40.6 us
  local copies, waits for them, and re-layouts: 31.5 us -> 22 us
  starting transfers between devices: 51.2 us -> 55.5 us
    pallas_call x28 -> x26, Pallas kernels: 92 us -> 40.6 us  [call(): pl.pallas_call(body, out_shape=[jax.ShapeDtypeStruct(x.shape, x.dtype) fo...]
    broadcast_in_dim x4 -> x0, local copies, waits for them, and re-layouts: 5.94 us -> none  [gathered(): spread = jnp.broadcast_to(block[None], (count, *block.shape))]
    reshape x5 -> x0, local copies, waits for them, and re-layouts: 5.9 us -> none  [the longest x1 1.87 us: local(): run(natural, out[2], out[3], place).reshape(shape)]
    unnamed x68 -> x72, local copies, waits for them, and re-layouts: 17.8 us -> 21.2 us
    all_to_all x4, starting transfers between devices: 16.7 us -> 20.1 us  [the longest x2 8.41 us: local(): gathered = lax.all_to_all(loads, AXES, 0, 0, tiled=True)]
  transfers between devices with their start and end apart: 29 -> 29, of which waited for: 18 -> 17; matrix products, arithmetic and copies ran while one was open for 2% -> 0% of each run, Pallas kernels for 23% -> 17%
where the time goes in v2:
time: 163 us; the launch traced here: 162 us
  starting transfers between devices  55.5 us (34%)
  waiting for transfers between devices  41.5 us (25%)
  Pallas kernels  40.6 us (25%)
  local copies, waits for them, and re-layouts  22 us (13%)
    ppermute x25, waiting for transfers between devices, shifted(): lax.ppermute(value, axis, [(i, (i + step) % size) for i in range(size)])  41.5 us
    pallas_call x26, Pallas kernels, call(): pl.pallas_call(body, out_shape=[jax.ShapeDtypeStruct(x.shape, x.dtype) fo...  40.6 us
    ppermute x25, starting transfers between devices, shifted(): lax.ppermute(value, axis, [(i, (i + step) % size) for i in range(size)])  35.4 us
    unnamed x72, local copies, waits for them, and re-layouts  21.2 us
    all_to_all x2, starting transfers between devices, local(): gathered = lax.all_to_all(loads, AXES, 0, 0, tiled=True)  8.41 us
    all_to_all x1, starting transfers between devices, local(): lax.all_to_all(coarse_rows, AXES, 0, 0, tiled=True).reshape(-1, coarse)  7.33 us
    all_to_all x1, starting transfers between devices, local(): rows1 = lax.all_to_all(sums1, AXES, 0, 0, tiled=True)  4.36 us
  transfers between devices with their start and end apart: 29, of which 17 were waited for; matrix products, arithmetic and copies ran while one was open for 0% of the time, Pallas kernels for 17%

profile of v2, /device:TPU:0, one launch (start us, length us, event | category | flops | bytes accessed | tf_op | source)
XLA Modules:
  0.0 161.7 jit_solution(7747260746735309159)
XLA Ops:
  6.0 7.5 %shard_map.95 = (f32[400,128]{1,0:T(8,128)S(1)}, f32[400,128]{1,0:T(8,128)S(1)}, f32[400,128]{1,0:T(8,128)S(1)}, f32[343,128]{1,0:T(8,128)S(1)}, f32[343,128]{1,...) custom-call(f32[9,9,9,128]{3,2,1,0:T(8,128)S(1)} %copy-done.9, ...), custom_call_target="tpu_custom_call" | custom-call | flops 1000000 | bytes 11302760 | tf_op jit(solution)/shard_map/pallas_call | solution.py:34
  17.6 7.3 %all-to-all-start.1 = ((f32[32,24,128]{2,1,0:T(8,128)}), f32[32,24,128]{2,1,0:T(8,128)S(1)}, u32[]{:S(2)}, u32[]{:S(2)}) async-start(f32[32,24,128]{2,1,0:T(8,128)} %get-tuple-element.84), calls=%async_computation.1 | async-start | bytes 786432 | tf_op jit(solution)/shard_map/all_to_all | solution.py:390
  28.5 2.1 %collective-permute-start.2 = (f32[176,128]{1,0:T(8,128)S(1)}, f32[176,128]{1,0:T(8,128)S(1)}, u32[]{:S(2)}, u32[]{:S(2)}) collective-permute-start(f32[176,128]{1,0:T(8,128)S(1)} %get-tuple-element.70), channel_id=1, source_target_pairs={{0,6},{2,0},{4,2},{6,4},{1,7},{3,1},{5,3},{7,5},{8,14},{10,8},{12,... | collective-permute-start | bytes 270344 | tf_op jit(solution)/shard_map/ppermute | solution.py:169
  30.6 7.8 %collective-permute-done.1.refs_1_ = f32[176,128]{1,0:T(8,128)S(1)} collective-permute-done((f32[176,128]{1,0:T(8,128)S(1)}, f32[176,128]{1,0:T(8,128)S(1)}, u32[]{:S(2)}, u32[]{:S(2)}) %collective-permute-start.1) | collective-permute-done | bytes 90144 | tf_op jit(solution)/shard_map/ppermute | solution.py:169
  41.4 2.9 %shard_map.98.refs_5_ = f32[400,400]{1,0:T(8,128)S(1)} custom-call(f32[729,729]{1,0:T(8,128)S(1)} %copy-done.3, f32[8,400]{1,0:T(8,128)S(1)} %copy-done.21), custom_call_target="tpu_custom_call" | custom-call | flops 100000000 | bytes 2778564 | tf_op jit(solution)/shard_map/pallas_call | solution.py:34
  48.0 5.4 %all-to-all-start = ((f32[32,24,128]{2,1,0:T(8,128)}), f32[32,24,128]{2,1,0:T(8,128)}, u32[]{:S(2)}, u32[]{:S(2)}) async-start(f32[32,24,128]{2,1,0:T(8,128)} %get-tuple-element.83), calls=%async_computation | async-start | bytes 786432 | tf_op jit(solution)/shard_map/all_to_all | solution.py:457
  56.7 2.1 %collective-permute-start.7 = (f32[88,128]{1,0:T(8,128)S(1)}, f32[88,128]{1,0:T(8,128)S(1)}, u32[]{:S(2)}, u32[]{:S(2)}) collective-permute-start(f32[88,128]{1,0:T(8,128)S(1)} %get-tuple-element.79), channel_id=1, source_target_pairs={{0,6},{2,0},{4,2},{6,4},{1,7},{3,1},{5,3},{7,5},{8,14},{10,8},{12,... | collective-permute-start | bytes 135176 | tf_op jit(solution)/shard_map/ppermute | solution.py:169
  59.5 6.3 %collective-permute-done.6.refs_1_ = f32[88,128]{1,0:T(8,128)S(1)} collective-permute-done((f32[88,128]{1,0:T(8,128)S(1)}, f32[88,128]{1,0:T(8,128)S(1)}, u32[]{:S(2)}, u32[]{:S(2)}) %collective-permute-start.6) | collective-permute-done | bytes 45088 | tf_op jit(solution)/shard_map/ppermute | solution.py:169
  71.7 5.7 %shard_map.107 = (f32[400,400]{1,0:T(8,128)S(1)}, f32[343,400]{1,0:T(8,128)S(1)}) custom-call(f32[729,729]{1,0:T(8,128)S(1)} %copy-done.1, f32[343,343]{1,0:T(8,128)S(1)} %get-tuple-element.87.refs_1_.refs_4_, f32[8,400]{1,0:T(8,128)S(1)} %copy-done.21), custom_call_target="tpu_custom_call" | custom-call | flops 100000000 | bytes 3797960 | tf_op jit(solution)/shard_map/pallas_call | solution.py:34
  78.2 3.0 %shard_map.102.refs_0_ = f32[128,128]{1,0:T(8,128)S(1)} custom-call(f32[1,768]{1,0:T(1,128)S(1)} %copy-done.26, f32[768,128]{1,0:T(8,128)S(1)} %bitcast.2), custom_call_target="tpu_custom_call" | custom-call | flops 100000000 | bytes 461824 | tf_op jit(solution)/shard_map/pallas_call | solution.py:34
  81.2 2.7 %shard_map.103.refs_0_ = f32[128,128]{1,0:T(8,128)S(1)} custom-call(f32[128,128]{1,0:T(8,128)S(1)} %shard_map.102.refs_0_), custom_call_target="tpu_custom_call" | custom-call | flops 100000000 | bytes 131072 | tf_op jit(solution)/shard_map/pallas_call | solution.py:34
  83.9 2.7 %shard_map.104.refs_0_ = f32[128,128]{1,0:T(8,128)S(1)} custom-call(f32[128,128]{1,0:T(8,128)S(1)} %shard_map.103.refs_0_), custom_call_target="tpu_custom_call" | custom-call | flops 100000000 | bytes 131072 | tf_op jit(solution)/shard_map/pallas_call | solution.py:34
  86.6 2.7 %shard_map.105.refs_2_ = f32[128,128]{1,0:T(8,128)S(1)} custom-call(f32[128,128]{1,0:T(8,128)S(1)} %shard_map.104.refs_0_), custom_call_target="tpu_custom_call" | custom-call | flops 100000000 | bytes 131072 | tf_op jit(solution)/shard_map/pallas_call | solution.py:34
  97.2 2.3 %collective-permute-start.11 = (f32[176,128]{1,0:T(8,128)S(1)}, f32[176,128]{1,0:T(8,128)S(1)}, u32[]{:S(2)}, u32[]{:S(2)}) collective-permute-start(f32[176,128]{1,0:T(8,128)S(1)} %get-tuple-element.93), channel_id=1, source_target_pairs={{0,2},{2,4},{4,6},{6,0},{1,3},{3,5},{5,7},{7,1},{8,10},{10,12},{12... | collective-permute-start | bytes 270344 | tf_op jit(solution)/shard_map/ppermute | solution.py:169
  101.1 3.5 %collective-permute-done.11.refs_1_ = f32[176,128]{1,0:T(8,128)S(1)} collective-permute-done((f32[176,128]{1,0:T(8,128)S(1)}, f32[176,128]{1,0:T(8,128)S(1)}, u32[]{:S(2)}, u32[]{:S(2)}) %collective-permute-start.11) | collective-permute-done | bytes 90144 | tf_op jit(solution)/shard_map/ppermute | solution.py:169
  106.4 2.4 %collective-permute-start.14 = (f32[176,128]{1,0:T(8,128)S(1)}, f32[176,128]{1,0:T(8,128)S(1)}, u32[]{:S(2)}, u32[]{:S(2)}) collective-permute-start(f32[176,128]{1,0:T(8,128)S(1)} %get-tuple-element.97), channel_id=1, source_target_pairs={{0,24},{8,0},{16,8},{24,16},{1,25},{9,1},{17,9},{25,17},{2,26},{10... | collective-permute-start | bytes 270344 | tf_op jit(solution)/shard_map/ppermute | solution.py:169
  108.8 3.5 %collective-permute-done.13.refs_1_ = f32[176,128]{1,0:T(8,128)S(1)} collective-permute-done((f32[176,128]{1,0:T(8,128)S(1)}, f32[176,128]{1,0:T(8,128)S(1)}, u32[]{:S(2)}, u32[]{:S(2)}) %collective-permute-start.13) | collective-permute-done | bytes 90144 | tf_op jit(solution)/shard_map/ppermute | solution.py:169
  116.3 3.0 %all-to-all-start.2 = ((f32[32,24,128]{2,1,0:T(8,128)}), f32[32,24,128]{2,1,0:T(8,128)S(1)}, u32[]{:S(2)}, u32[]{:S(2)}) async-start(f32[32,24,128]{2,1,0:T(8,128)} %copy-done.10), calls=%async_computation.2 | async-start | bytes 786432 | tf_op jit(solution)/shard_map/all_to_all | solution.py:478
  122.6 2.1 %collective-permute-start.17 = (f32[88,128]{1,0:T(8,128)S(1)}, f32[88,128]{1,0:T(8,128)S(1)}, u32[]{:S(2)}, u32[]{:S(2)}) collective-permute-start(f32[88,128]{1,0:T(8,128)S(1)} %get-tuple-element.104), channel_id=1, source_target_pairs={{0,6},{2,0},{4,2},{6,4},{1,7},{3,1},{5,3},{7,5},{8,14},{10,8},{12,... | collective-permute-start | bytes 135176 | tf_op jit(solution)/shard_map/ppermute | solution.py:169
  124.6 7.1 %collective-permute-done.16.refs_1_ = f32[88,128]{1,0:T(8,128)S(1)} collective-permute-done((f32[88,128]{1,0:T(8,128)S(1)}, f32[88,128]{1,0:T(8,128)S(1)}, u32[]{:S(2)}, u32[]{:S(2)}) %collective-permute-start.16) | collective-permute-done | bytes 45088 | tf_op jit(solution)/shard_map/ppermute | solution.py:169
  140.4 4.4 %all-to-all-start.3 = ((f32[32,8,128]{2,1,0:T(8,128)}), f32[32,8,128]{2,1,0:T(8,128)S(1)}, u32[]{:S(2)}, u32[]{:S(2)}) async-start(f32[32,8,128]{2,1,0:T(8,128)} %get-tuple-element.110), calls=%async_computation.3 | async-start | bytes 262144 | tf_op jit(solution)/shard_map/all_to_all | solution.py:508
  148.1 2.1 %collective-permute-start.22 = (f32[88,128]{1,0:T(8,128)S(1)}, f32[88,128]{1,0:T(8,128)S(1)}, u32[]{:S(2)}, u32[]{:S(2)}) collective-permute-start(f32[88,128]{1,0:T(8,128)S(1)} %get-tuple-element.119), channel_id=1, source_target_pairs={{0,6},{2,0},{4,2},{6,4},{1,7},{3,1},{5,3},{7,5},{8,14},{10,8},{12,... | collective-permute-start | bytes 135176 | tf_op jit(solution)/shard_map/ppermute | solution.py:169
  150.1 2.5 %collective-permute-done.21.refs_1_ = f32[88,128]{1,0:T(8,128)S(1)} collective-permute-done((f32[88,128]{1,0:T(8,128)S(1)}, f32[88,128]{1,0:T(8,128)S(1)}, u32[]{:S(2)}, u32[]{:S(2)}) %collective-permute-start.21) | collective-permute-done | bytes 45088 | tf_op jit(solution)/shard_map/ppermute | solution.py:169
  157.9 2.5 %shard_map.116 = (f32[400,128]{1,0:T(8,128)S(1)}, f32[343,128]{1,0:T(8,128)S(1)}, f32[2,128]{1,0:T(2,128)S(1)}) custom-call(f32[2,128]{1,0:T(2,128)S(1)} %get-tuple-element.100.refs_10_.refs_0_, f32[32,8,128]{2,1,0:T(8,128)S(1)} %all-to-all-done.3.refs_1_, f32[343,128]{1,0:T(8,128)S(1)} %copy-done.20, f32[343,400]{1,0:T(8,128)S(1)} %copy-done.8, ...), custom_call_target="tpu_custom_call" | custom-call | flops 100000000 | bytes 2118148 | tf_op jit(solution)/shard_map/pallas_call | solution.py:34
  (141 shorter events, 67.3 us)
Async XLA Ops:
  17.6 30.4 %all-to-all-start.1 = ((f32[32,24,128]{2,1,0:T(8,128)}), f32[32,24,128]{2,1,0:T(8,128)S(1)}, u32[]{:S(2)}, u32[]{:S(2)}) async-start(f32[32,24,128]{2,1,0:T(8,128)} %get-tuple-element.84), calls=%async_computation.1 | async-start | bytes 786432 | tf_op jit(solution)/shard_map/all_to_all | solution.py:390
  26.7 11.7 %collective-permute-start.1 = (f32[176,128]{1,0:T(8,128)S(1)}, f32[176,128]{1,0:T(8,128)S(1)}, u32[]{:S(2)}, u32[]{:S(2)}) collective-permute-start(f32[176,128]{1,0:T(8,128)S(1)} %get-tuple-element.69), channel_id=1, source_target_pairs={{0,2},{2,4},{4,6},{6,0},{1,3},{3,5},{5,7},{7,1},{8,10},{10,12},{12... | collective-permute-start | bytes 270344 | tf_op jit(solution)/shard_map/ppermute | solution.py:169
  28.5 9.9 %collective-permute-start.2 = (f32[176,128]{1,0:T(8,128)S(1)}, f32[176,128]{1,0:T(8,128)S(1)}, u32[]{:S(2)}, u32[]{:S(2)}) collective-permute-start(f32[176,128]{1,0:T(8,128)S(1)} %get-tuple-element.70), channel_id=1, source_target_pairs={{0,6},{2,0},{4,2},{6,4},{1,7},{3,1},{5,3},{7,5},{8,14},{10,8},{12,... | collective-permute-start | bytes 270344 | tf_op jit(solution)/shard_map/ppermute | solution.py:169
  38.4 5.9 %collective-permute-start.3 = (f32[176,128]{1,0:T(8,128)S(1)}, f32[176,128]{1,0:T(8,128)S(1)}, u32[]{:S(2)}, u32[]{:S(2)}) collective-permute-start(f32[176,128]{1,0:T(8,128)S(1)} %get-tuple-element.72), channel_id=1, source_target_pairs={{0,8},{8,16},{16,24},{24,0},{1,9},{9,17},{17,25},{25,1},{2,10},{10... | collective-permute-start | bytes 270344 | tf_op jit(solution)/shard_map/ppermute | solution.py:169
  40.0 4.9 %collective-permute-start.4 = (f32[176,128]{1,0:T(8,128)S(1)}, f32[176,128]{1,0:T(8,128)S(1)}, u32[]{:S(2)}, u32[]{:S(2)}) collective-permute-start(f32[176,128]{1,0:T(8,128)S(1)} %get-tuple-element.73), channel_id=1, source_target_pairs={{0,24},{8,0},{16,8},{24,16},{1,25},{9,1},{17,9},{25,17},{2,26},{10... | collective-permute-start | bytes 270344 | tf_op jit(solution)/shard_map/ppermute | solution.py:169
  48.0 41.3 %all-to-all-start = ((f32[32,24,128]{2,1,0:T(8,128)}), f32[32,24,128]{2,1,0:T(8,128)}, u32[]{:S(2)}, u32[]{:S(2)}) async-start(f32[32,24,128]{2,1,0:T(8,128)} %get-tuple-element.83), calls=%async_computation | async-start | bytes 786432 | tf_op jit(solution)/shard_map/all_to_all | solution.py:457
  54.9 10.8 %collective-permute-start.6 = (f32[88,128]{1,0:T(8,128)S(1)}, f32[88,128]{1,0:T(8,128)S(1)}, u32[]{:S(2)}, u32[]{:S(2)}) collective-permute-start(f32[88,128]{1,0:T(8,128)S(1)} %get-tuple-element.78), channel_id=1, source_target_pairs={{0,2},{2,4},{4,6},{6,0},{1,3},{3,5},{5,7},{7,1},{8,10},{10,12},{12... | collective-permute-start | bytes 135176 | tf_op jit(solution)/shard_map/ppermute | solution.py:169
  56.7 9.1 %collective-permute-start.7 = (f32[88,128]{1,0:T(8,128)S(1)}, f32[88,128]{1,0:T(8,128)S(1)}, u32[]{:S(2)}, u32[]{:S(2)}) collective-permute-start(f32[88,128]{1,0:T(8,128)S(1)} %get-tuple-element.79), channel_id=1, source_target_pairs={{0,6},{2,0},{4,2},{6,4},{1,7},{3,1},{5,3},{7,5},{8,14},{10,8},{12,... | collective-permute-start | bytes 135176 | tf_op jit(solution)/shard_map/ppermute | solution.py:169
  67.1 24.8 %collective-permute-start.8 = (f32[88,128]{1,0:T(8,128)}, f32[88,128]{1,0:T(8,128)S(1)}, u32[]{:S(2)}, u32[]{:S(2)}) collective-permute-start(f32[88,128]{1,0:T(8,128)} %get-tuple-element.81), channel_id=1, source_target_pairs={{0,8},{8,16},{16,24},{24,0},{1,9},{9,17},{17,25},{25,1},{2,10},{10... | collective-permute-start | bytes 135176 | tf_op jit(solution)/shard_map/ppermute | solution.py:169
  68.6 23.4 %collective-permute-start.9 = (f32[88,128]{1,0:T(8,128)}, f32[88,128]{1,0:T(8,128)}, u32[]{:S(2)}, u32[]{:S(2)}) collective-permute-start(f32[88,128]{1,0:T(8,128)} %get-tuple-element.82), channel_id=1, source_target_pairs={{0,24},{8,0},{16,8},{24,16},{1,25},{9,1},{17,9},{25,17},{2,26},{10... | collective-permute-start | bytes 135176 | tf_op jit(solution)/shard_map/ppermute | solution.py:169
  97.2 7.4 %collective-permute-start.11 = (f32[176,128]{1,0:T(8,128)S(1)}, f32[176,128]{1,0:T(8,128)S(1)}, u32[]{:S(2)}, u32[]{:S(2)}) collective-permute-start(f32[176,128]{1,0:T(8,128)S(1)} %get-tuple-element.93), channel_id=1, source_target_pairs={{0,2},{2,4},{4,6},{6,0},{1,3},{3,5},{5,7},{7,1},{8,10},{10,12},{12... | collective-permute-start | bytes 270344 | tf_op jit(solution)/shard_map/ppermute | solution.py:169
  99.5 6.3 %collective-permute-start.12 = (f32[176,128]{1,0:T(8,128)S(1)}, f32[176,128]{1,0:T(8,128)S(1)}, u32[]{:S(2)}, u32[]{:S(2)}) collective-permute-start(f32[176,128]{1,0:T(8,128)S(1)} %get-tuple-element.94), channel_id=1, source_target_pairs={{0,6},{2,0},{4,2},{6,4},{1,7},{3,1},{5,3},{7,5},{8,14},{10,8},{12,... | collective-permute-start | bytes 270344 | tf_op jit(solution)/shard_map/ppermute | solution.py:169
  105.8 6.4 %collective-permute-start.13 = (f32[176,128]{1,0:T(8,128)S(1)}, f32[176,128]{1,0:T(8,128)S(1)}, u32[]{:S(2)}, u32[]{:S(2)}) collective-permute-start(f32[176,128]{1,0:T(8,128)S(1)} %get-tuple-element.96), channel_id=1, source_target_pairs={{0,8},{8,16},{16,24},{24,0},{1,9},{9,17},{17,25},{25,1},{2,10},{10... | collective-permute-start | bytes 270344 | tf_op jit(solution)/shard_map/ppermute | solution.py:169
  106.4 6.8 %collective-permute-start.14 = (f32[176,128]{1,0:T(8,128)S(1)}, f32[176,128]{1,0:T(8,128)S(1)}, u32[]{:S(2)}, u32[]{:S(2)}) collective-permute-start(f32[176,128]{1,0:T(8,128)S(1)} %get-tuple-element.97), channel_id=1, source_target_pairs={{0,24},{8,0},{16,8},{24,16},{1,25},{9,1},{17,9},{25,17},{2,26},{10... | collective-permute-start | bytes 270344 | tf_op jit(solution)/shard_map/ppermute | solution.py:169
  116.3 19.1 %all-to-all-start.2 = ((f32[32,24,128]{2,1,0:T(8,128)}), f32[32,24,128]{2,1,0:T(8,128)S(1)}, u32[]{:S(2)}, u32[]{:S(2)}) async-start(f32[32,24,128]{2,1,0:T(8,128)} %copy-done.10), calls=%async_computation.2 | async-start | bytes 786432 | tf_op jit(solution)/shard_map/all_to_all | solution.py:478
  120.7 11.0 %collective-permute-start.16 = (f32[88,128]{1,0:T(8,128)S(1)}, f32[88,128]{1,0:T(8,128)S(1)}, u32[]{:S(2)}, u32[]{:S(2)}) collective-permute-start(f32[88,128]{1,0:T(8,128)S(1)} %get-tuple-element.103), channel_id=1, source_target_pairs={{0,2},{2,4},{4,6},{6,0},{1,3},{3,5},{5,7},{7,1},{8,10},{10,12},{12... | collective-permute-start | bytes 135176 | tf_op jit(solution)/shard_map/ppermute | solution.py:169
  122.6 9.1 %collective-permute-start.17 = (f32[88,128]{1,0:T(8,128)S(1)}, f32[88,128]{1,0:T(8,128)S(1)}, u32[]{:S(2)}, u32[]{:S(2)}) collective-permute-start(f32[88,128]{1,0:T(8,128)S(1)} %get-tuple-element.104), channel_id=1, source_target_pairs={{0,6},{2,0},{4,2},{6,4},{1,7},{3,1},{5,3},{7,5},{8,14},{10,8},{12,... | collective-permute-start | bytes 135176 | tf_op jit(solution)/shard_map/ppermute | solution.py:169
  132.4 4.9 %collective-permute-start.18 = (f32[88,128]{1,0:T(8,128)S(1)}, f32[88,128]{1,0:T(8,128)S(1)}, u32[]{:S(2)}, u32[]{:S(2)}) collective-permute-start(f32[88,128]{1,0:T(8,128)S(1)} %get-tuple-element.106), channel_id=1, source_target_pairs={{0,8},{8,16},{16,24},{24,0},{1,9},{9,17},{17,25},{25,1},{2,10},{10... | collective-permute-start | bytes 135176 | tf_op jit(solution)/shard_map/ppermute | solution.py:169
  133.9 4.0 %collective-permute-start.19 = (f32[88,128]{1,0:T(8,128)S(1)}, f32[88,128]{1,0:T(8,128)S(1)}, u32[]{:S(2)}, u32[]{:S(2)}) collective-permute-start(f32[88,128]{1,0:T(8,128)S(1)} %get-tuple-element.107), channel_id=1, source_target_pairs={{0,24},{8,0},{16,8},{24,16},{1,25},{9,1},{17,9},{25,17},{2,26},{10... | collective-permute-start | bytes 135176 | tf_op jit(solution)/shard_map/ppermute | solution.py:169
  140.4 15.5 %all-to-all-start.3 = ((f32[32,8,128]{2,1,0:T(8,128)}), f32[32,8,128]{2,1,0:T(8,128)S(1)}, u32[]{:S(2)}, u32[]{:S(2)}) async-start(f32[32,8,128]{2,1,0:T(8,128)} %get-tuple-element.110), calls=%async_computation.3 | async-start | bytes 262144 | tf_op jit(solution)/shard_map/all_to_all | solution.py:508
  146.2 6.4 %collective-permute-start.21 = (f32[88,128]{1,0:T(8,128)S(1)}, f32[88,128]{1,0:T(8,128)S(1)}, u32[]{:S(2)}, u32[]{:S(2)}) collective-permute-start(f32[88,128]{1,0:T(8,128)S(1)} %get-tuple-element.118), channel_id=1, source_target_pairs={{0,2},{2,4},{4,6},{6,0},{1,3},{3,5},{5,7},{7,1},{8,10},{10,12},{12... | collective-permute-start | bytes 135176 | tf_op jit(solution)/shard_map/ppermute | solution.py:169
  148.1 4.8 %collective-permute-start.22 = (f32[88,128]{1,0:T(8,128)S(1)}, f32[88,128]{1,0:T(8,128)S(1)}, u32[]{:S(2)}, u32[]{:S(2)}) collective-permute-start(f32[88,128]{1,0:T(8,128)S(1)} %get-tuple-element.119), channel_id=1, source_target_pairs={{0,6},{2,0},{4,2},{6,4},{1,7},{3,1},{5,3},{7,5},{8,14},{10,8},{12,... | collective-permute-start | bytes 135176 | tf_op jit(solution)/shard_map/ppermute | solution.py:169
  152.9 7.5 %collective-permute-start.23 = (f32[88,128]{1,0:T(8,128)S(1)}, f32[88,128]{1,0:T(8,128)S(1)}, u32[]{:S(2)}, u32[]{:S(2)}) collective-permute-start(f32[88,128]{1,0:T(8,128)S(1)} %get-tuple-element.121), channel_id=1, source_target_pairs={{0,8},{8,16},{16,24},{24,0},{1,9},{9,17},{17,25},{25,1},{2,10},{10... | collective-permute-start | bytes 135176 | tf_op jit(solution)/shard_map/ppermute | solution.py:169
  154.5 5.9 %collective-permute-start.24 = (f32[88,128]{1,0:T(8,128)S(1)}, f32[88,128]{1,0:T(8,128)S(1)}, u32[]{:S(2)}, u32[]{:S(2)}) collective-permute-start(f32[88,128]{1,0:T(8,128)S(1)} %get-tuple-element.122), channel_id=1, source_target_pairs={{0,24},{8,0},{16,8},{24,16},{1,25},{9,1},{17,9},{25,17},{2,26},{10... | collective-permute-start | bytes 135176 | tf_op jit(solution)/shard_map/ppermute | solution.py:169
  (39 other events, 307.5 us)

commit v3 on v2

v3 whole, which is shorter than its diff:
```python
import jax
import jax.numpy as jnp
import numpy as np
from jax import lax
from jax.experimental import pallas as pl
from jax.experimental.pallas import tpu as pltpu
from jax.sharding import PartitionSpec as P

AXES = ("gx", "gy", "gz")
HIGHEST = lax.Precision.HIGHEST
PALLAS = True
LIMIT = 24 * 2**20
VMEM = pltpu.VMEM
PIECES = 4
PLAIN = 8
FILL = 10**8


def dot(left, right, contract=(1, 0)):
    dims = (((contract[0],), (contract[1],)), ((), ()))
    return lax.dot_general(
        left, right, dims, precision=HIGHEST, preferred_element_type=jnp.float32
    )


def whole(count):
    return [pl.BlockSpec(memory_space=VMEM)] * count


def call(body, operands, outs, scratch=(), in_hbm=(), flops=10**6, aliases=None):
    places = whole(len(operands))
    for index in in_hbm:
        places[index] = pl.BlockSpec(memory_space=pl.ANY)
    size = sum(4 * np.prod(x.shape) for x in (*operands, *outs))
    return pl.pallas_call(
        body,
        out_shape=[jax.ShapeDtypeStruct(x.shape, x.dtype) for x in outs],
        in_specs=places,
        out_specs=whole(len(outs)),
        scratch_shapes=scratch,
        input_output_aliases=aliases or {},
        compiler_params=pltpu.CompilerParams(vmem_limit_bytes=LIMIT),
        cost_estimate=pl.CostEstimate(flops=flops, bytes_accessed=int(size), transcendentals=0),
    )(*operands)


def run(function, *operands, flops=10**6, after=(), keep=None, use=(), store=()):
    arrays = {} if keep is None else keep.arrays
    names = list(arrays)
    used = [keep.read(arrays, name) for name in use]
    shapes = jax.eval_shape(function, *operands, *used)
    single = not isinstance(shapes, tuple)
    outs = (shapes,) if single else shapes
    outs = outs[: len(outs) - len(store)]
    count = len(operands)
    base = count + len(after)
    first_out = base + len(names)

    def body(*refs):
        kept = dict(zip(names, refs[base:first_out]))
        kept_out = dict(zip(names, refs[first_out + len(outs) :]))
        values = [ref[...] for ref in refs[:count]] + [keep.read(kept, name) for name in use]
        results = function(*values)
        results = (results,) if single else results
        for ref, result in zip(refs[first_out:], results[: len(outs)]):
            ref[...] = result
        for name, result in zip(store, results[len(outs) :]):
            bank, start, _ = keep.slots[name]
            kept_out[bank][pl.ds(start, result.shape[0]), :] = result

    held = [arrays[name] for name in names]
    aliases = {base + index: len(outs) + index for index in range(len(names))}
    results = call(
        body, (*operands, *after, *held), (*outs, *held), in_hbm=range(count, base), flops=flops,
        aliases=aliases,
    )
    arrays.update(zip(names, results[len(outs) :]))
    results = results[: len(outs)]
    return results[0] if single and results else tuple(results)


class Keep:
    def __init__(self):
        self.arrays, self.slots, self.rows = {}, {}, {}

    def plan(self, bank, sizes):
        self.rows[bank] = 0
        for name, size in sizes:
            self.slots[name] = (bank, self.rows[bank], size)
            self.rows[bank] += -(-size // 8) * 8

    def place(self, name):
        _, start, size = self.slots[name]
        return pl.ds(start, size)

    def read(self, arrays, name):
        name, wanted = name if isinstance(name, tuple) else (name, None)
        if name in self.slots:
            bank, start, size = self.slots[name]
            return arrays[bank][start : start + (wanted or size), :]
        return arrays[name][...]


def floats(*shape):
    return jax.ShapeDtypeStruct(shape, jnp.float32)


class Layout:
    def __init__(self, n):
        m = n - 1
        self.n, self.m = n, m
        self.block = n * m
        self.ring_rows = 4 * self.block
        flat = (n - 2) ** 2
        self.flat = -(-flat // 8) * 8
        self.rows = self.ring_rows + 2 * self.flat
        self.y_rows = self.block + -(-n // 8) * 8
        self.x_rows = 4 * m + self.flat
        at = lambda i, j, k: (i * n + j) * n + k
        inner = range(1, m)
        order = [at(i, j, k) for j in (0, m) for i in range(n) for k in range(m)]
        for j, k in ((0, 0), (m, m)):
            for i in range(n):
                order += [at(i, x, k) for x in inner] + [at(i, j, m)]
        for i in (0, m):
            order += [at(i, j, k) for j in inner for k in inner]
            order += [-1] * (self.flat - flat)
        self.order = np.array(order, np.int32)
        self.inner = np.array([at(i, j, k) for i in inner for j in inner for k in inner], np.int32)
        share = np.zeros((self.rows, 1), np.float32)
        for row, node in enumerate(order):
            if node >= 0:
                place = (node // (n * n), node // n % n, node % n)
                share[row] = 0.5 ** sum(x in (0, m) for x in place)
        self.share = share

    def blocks(self, ring):
        return [ring[s * self.block : (s + 1) * self.block] for s in range(4)]

    def row_in_tile(self, block):
        return lax.broadcasted_iota(jnp.int32, block.shape, 0) % self.m

    def fold_z(self, ring, below, above):
        first, last, low, high = self.blocks(ring)
        below, above = self.blocks(below), self.blocks(above)
        row = self.row_in_tile(first)
        start, end = row == 0, row == self.m - 1
        back = lambda x: roll_rows(x, x.shape[0] - (self.m - 1))
        ahead = lambda x: roll_rows(x, self.m - 1)
        zero = jnp.zeros_like(first)
        first = first + jnp.where(start, back(below[2]), zero)
        last = last + jnp.where(start, back(below[3]), zero)
        low = low + jnp.where(end, ahead(above[0]), below[3])
        high = high + jnp.where(end, ahead(above[1]), above[2])
        return jnp.concatenate([first, last, low, high], axis=0)

    def side(self, block, corners):
        lanes = block.shape[1]
        rows = corners.reshape(self.n, self.m, lanes)[:, self.m - 1, :]
        fill = jnp.zeros((self.y_rows - self.block - self.n, lanes), block.dtype)
        return jnp.concatenate([block, rows, fill], axis=0)

    def sides_y(self, ring):
        first, last, low, high = self.blocks(ring)
        return self.side(first, low), self.side(last, high)

    def fold_y(self, ring, below, above):
        first, last, low, high = self.blocks(ring)
        lanes = ring.shape[1]
        end = self.row_in_tile(first) == self.m - 1

        def ends(message):
            rows = message[self.block : self.block + self.n].reshape(self.n, 1, lanes)
            wide = jnp.broadcast_to(rows, (self.n, self.m, lanes)).reshape(self.block, lanes)
            return jnp.where(end, wide, jnp.zeros_like(wide))

        first = first + below[: self.block]
        low = low + ends(below)
        last = last + above[: self.block]
        high = high + ends(above)
        return jnp.concatenate([first, last, low, high], axis=0)

    def sides_x(self, ring, flat):
        m, block = self.m, self.block
        low = [ring[s * block : s * block + m] for s in range(4)] + [flat[: self.flat]]
        high = [ring[(s + 1) * block - m : (s + 1) * block] for s in range(4)] + [flat[self.flat :]]
        return jnp.concatenate(low, axis=0), jnp.concatenate(high, axis=0)

    def fold_x(self, ring, flat, below, above):
        m, block = self.m, self.block
        parts = []
        for s in range(4):
            parts += [
                ring[s * block : s * block + m] + below[s * m : (s + 1) * m],
                ring[s * block + m : (s + 1) * block - m],
                ring[(s + 1) * block - m : (s + 1) * block] + above[s * m : (s + 1) * m],
            ]
        parts += [flat[: self.flat] + below[4 * m :], flat[self.flat :] + above[4 * m :]]
        return jnp.concatenate(parts, axis=0)


def roll_rows(value, shift):
    if PALLAS:
        return pltpu.roll(value, shift, 0)
    return jnp.roll(value, shift, axis=0)


def shifted(value, axis, step):
    size = lax.axis_size(axis)
    return lax.ppermute(value, axis, [(i, (i + step) % size) for i in range(size)])


def both_ways(low, high, axis):
    return shifted(high, axis, 1), shifted(low, axis, -1)


def cat(parts):
    return parts[0] if len(parts) == 1 else jnp.concatenate(parts, axis=0)


def packed(layout, *fields):
    rings, rows = layout.ring_rows, layout.rows
    return cat([f[:rings] for f in fields]), cat([f[rings:rows] for f in fields])


def steps_of(axis):
    size = lax.axis_size(axis)
    return [1] if size == 2 else [1, size - 1, *range(2, size - 1)]


def assemble(
    layout, count, shares, rings, flats, function, keep, use=(), store=(), beside_y=None, beside_x=None
):
    ring_rows, flat_rows = layout.ring_rows, layout.rows - layout.ring_rows
    split = lambda value, size: [value[i * size : (i + 1) * size] for i in range(count)]
    column, slab = shares

    steps = steps_of("gz")
    sums = rings[count * ring_rows :] if len(steps) > 2 else None
    others = [shifted(rings, "gz", step) for step in steps[:2]]
    others += [shifted(sums, "gz", step) for step in steps[2:]]
    near = min(2, len(steps))

    def after_z(rings, flats, *others):
        done, low, high = [], [], []
        parts = [split(value, ring_rows) for value in (rings, others[0], others[near - 1])]
        for ring, below, above in zip(*parts):
            if near == 1:
                above = below
            ring = layout.fold_z(ring, below, above)
            sides = layout.sides_y(ring)
            done.append(ring)
            low.append(sides[0])
            high.append(sides[1])
        own = rings[count * ring_rows :]
        for index, other in enumerate(others):
            own = own + (other[count * ring_rows :] if index < near else other)
        return cat([*low, own]), cat([*high, own]), own, cat([*done, flats])

    work = ("work", count * layout.rows)
    low, high, own = run(after_z, rings, flats, *others, keep=keep, store=("work",))
    below, above = both_ways(low, high, "gy")
    steps = steps_of("gy")
    far = [shifted(own, "gy", step) for step in steps[2:]]
    ties = beside_y() if beside_y else ()

    def all_parts(own, below, above, far, edge, steps):
        parts = [own, below[edge:]]
        return parts + ([above[edge:]] if len(steps) > 1 else []) + list(far)

    def merged(chosen, parts, size):
        plain = sum(part[size:] for part in parts)
        wide = cat([part[:size] for part in parts])
        return pick(chosen[:, : wide.shape[0]].astype(jnp.bfloat16), wide), plain

    def after_y(below, above, own, *rest):
        far, (both, chosen) = rest[:-2], rest[-2:]
        done, low, high = [], [], []
        rings, flats = both[: count * ring_rows], both[count * ring_rows :]
        edge = count * layout.y_rows
        parts = (
            split(rings, ring_rows), split(flats, flat_rows), split(below[:edge], layout.y_rows),
            split(above[:edge], layout.y_rows),
        )
        for ring, flat, first, last in zip(*parts):
            ring = layout.fold_y(ring, first, last)
            sides = layout.sides_x(ring, flat)
            done.append(ring)
            low.append(sides[0])
            high.append(sides[1])
        own = cat(merged(chosen, all_parts(own, below, above, far, edge, steps), column))
        return cat([*low, own]), cat([*high, own]), own, cat([*done, flats])

    low, high, own = run(
        after_y, below, above, own, *far, after=ties, keep=keep, use=(work, "to_slab"), store=("work",)
    )
    below, above = both_ways(low, high, "gx")
    steps = steps_of("gx")
    far = [shifted(own, "gx", step) for step in steps[2:]]
    ties = beside_x() if beside_x else ()

    def after_x(below, above, own, *rest):
        far, (both, chosen), rest = rest[: len(steps) - 2], rest[len(steps) - 2 : len(steps)], rest[len(steps) :]
        rings, flats = both[: count * ring_rows], both[count * ring_rows :]
        edge = count * layout.x_rows
        parts = (
            split(rings, ring_rows), split(flats, flat_rows), split(below[:edge], layout.x_rows),
            split(above[:edge], layout.x_rows),
        )
        sums = merged(chosen, all_parts(own, below, above, far, edge, steps), slab)
        return function(*[layout.fold_x(*values) for values in zip(*parts)], *sums, *rest)

    return run(
        after_x, below, above, own, *far, after=ties, keep=keep, use=(work, "to_all", *use), store=store
    )


def parts_of(value):
    high = value.astype(jnp.bfloat16)
    rest = value - high.astype(jnp.float32)
    middle = rest.astype(jnp.bfloat16)
    low = (rest - middle.astype(jnp.float32)).astype(jnp.bfloat16)
    return high, middle, low


def pick(left, right, contract=(1, 0)):
    dims = (((contract[0],), (contract[1],)), ((), ()))
    if left.dtype == jnp.bfloat16:
        pairs = [(left, part) for part in parts_of(right)]
    else:
        pairs = [(part, right) for part in parts_of(left)]
    terms = [lax.dot_general(a, b, dims, preferred_element_type=jnp.float32) for a, b in pairs]
    return terms[0] + terms[1] + terms[2]


def one_hot_rows(column, count):
    lanes = lax.broadcasted_iota(jnp.int32, (column.shape[0], count), 1).astype(jnp.float32)
    return jnp.where(lanes == column, 1.0, 0.0).astype(jnp.bfloat16)


def one_hot_columns(row, count):
    places = lax.broadcasted_iota(jnp.int32, (count, row.shape[1]), 0).astype(jnp.float32)
    return jnp.where(places == row, 1.0, 0.0).astype(jnp.bfloat16)


def as_column(row):
    return jnp.broadcast_to(row, (8, row.shape[1])).T[:, :1]


def up(value, step):
    return -(-value // step) * step


def coarse_tables(counts, constraints):
    x, y, z = counts
    total = x * y * z

    def number(kind, i, j, k):
        return kind * total + (i % x * y + j % y) * z + k % z

    def own(a, b, c):
        two = (0, 1)
        listed = [number(0, a + i, b + j, c + k) for i in two for j in two for k in two]
        listed += [number(1, a, b + j, c + k) for j in two for k in two]
        listed += [number(2, a + i, b, c + k) for i in two for k in two]
        return listed + [number(3, a + i, b + j, c) for i in two for j in two]

    def unique(lists, pad):
        listed = sorted(set(sum(lists, [])))
        return listed + [pad] * (up(len(listed), 8) - len(listed))

    column = lambda a, b, pad: unique([own(a, b, c) for c in range(z)], pad)
    slab = lambda a, pad: unique([own(a, b, c) for b in range(y) for c in range(z)], pad)
    back_y = [0] + steps_of("gy")
    back_x = [0] + steps_of("gx")
    rows = []
    for a in range(x):
        for b in range(y):
            for c in range(z):
                first = own(a, b, c)
                rows.append([
                    first + [-1] * (constraints - len(first)), column(a, b, -2),
                    sum([column(a, (b - s) % y, -3) for s in back_y], []), slab(a, -4),
                    sum([slab((a - s) % x, -5) for s in back_x], []),
                ])
    starts, width = [], 0
    for listed in rows[0]:
        starts.append(width)
        width += up(len(listed), 128)
    table = np.full((total, width), -9, np.float32)
    for row, lists in zip(table, rows):
        for start, listed in zip(starts, lists):
            row[start : start + len(listed)] = listed
    sizes = [len(listed) for listed in rows[0]]
    return table, starts, sizes


def eliminate(matrix, pivots):
    count = matrix.shape[0]
    rows = lax.broadcasted_iota(jnp.int32, (8, count), 0)
    lanes = lax.broadcasted_iota(jnp.int32, (1, count), 1)
    for k in pivots:
        tile = k // 8 * 8
        column = jnp.take_along_axis(matrix, jnp.full(matrix.shape, k, jnp.int32), axis=1)
        row = jnp.where(lanes == k, 1.0, matrix[k : k + 1, :]) / column[k : k + 1, :]
        matrix = jnp.where(lanes == k, 0.0, matrix) - column * row
        own = jnp.where(rows == k - tile, row, matrix[tile : tile + 8])
        parts = [matrix[:tile], own, matrix[tile + 8 :]]
        matrix = jnp.concatenate([part for part in parts if part.shape[0]], axis=0)
    return matrix


def local(element_load, local_matrix, dirichlet_inverse, neumann_inverse, coarse_basis):
    n = element_load.shape[0]
    lanes = element_load.shape[3]
    nodes = n**3
    layout = Layout(n)
    inside = (n - 2) ** 3
    primal = coarse_basis.shape[3]
    counts = [lax.axis_size(axis) for axis in AXES]
    devices = counts[0] * counts[1] * counts[2]
    coarse = 4 * devices
    chunk = -(-primal // 8) * 8
    rows = layout.rows
    table, starts, sizes = coarse_tables(counts, chunk)
    shares = column, slab = sizes[1], sizes[3]
    rides = coarse == lanes
    own_table = jnp.asarray(table)
    places = np.stack([layout.order.astype(np.float32), layout.share[:, 0]])
    places = jnp.asarray(np.pad(places, ((0, 6), (0, 0))))
    pairs = [(i, j) for i in range(n) for j in range(n)]
    inner_pairs = [(i, j) for i in range(1, n - 1) for j in range(1, n - 1)]
    deep = n - 2

    def part(loads, chosen, *extra):
        mapped = pick(chosen[:, :chunk].astype(jnp.bfloat16), loads)
        fill = jnp.zeros((PLAIN - sum(rows.shape[0] for rows in extra), lanes), jnp.float32)
        return cat([mapped, *extra, fill])

    count = 1 + -(-coarse // lanes)
    ring_rows = layout.ring_rows
    names = ("condensed", "load", "residual", "field0", "image0", "image0_sum", "load_sum", "field1")
    keep = Keep()
    keep.plan(
        "bank",
        [("tau", 8), ("totals", 8), ("work", max(count, 2) * rows)] + [(name, rows) for name in names],
    )
    keep.plan("picks", [("to_column", column), ("to_slab", slab), ("to_all", coarse)])
    pick_lanes = up(max(sizes), 128)
    keep.plan(
        "matrices", [("schur", rows), ("scaled", rows), ("coupling", inside), ("weighted", chunk)]
    )

    def start(
        load, matrix, inverse, basis_in, places, own_table,
        bank, rings, flats, weighted, coarse_rows, picks,
        natural, load_inside, begun, begun_natural,
    ):
        order = places[0:1, :]
        surface = one_hot_rows(as_column(order), nodes)
        across = one_hot_columns(order, nodes)
        for i, j in pairs:
            natural[pl.ds((i * n + j) * n, n), :] = load[i, j]
        for index, (i, j) in enumerate(inner_pairs):
            load_inside[pl.ds(index * deep, deep), :] = load[i, j, pl.ds(1, deep), :]
        begun[...] = dot(inverse[0, 0, 0], load_inside[...])
        tau = jnp.sum(load_inside[...] * begun[...], axis=0, keepdims=True)
        begun_natural[...] = jnp.zeros_like(begun_natural)
        for index, (i, j) in enumerate(inner_pairs):
            begun_natural[pl.ds((i * n + j) * n + 1, deep), :] = begun[pl.ds(index * deep, deep), :]
        basis = jnp.concatenate(
            [basis_in[0, 0, 0], jnp.zeros((chunk - primal, nodes), jnp.float32)], axis=0
        )
        weighted[...] = pick(basis, across) * places[1:2, :]
        me = own_table[pl.ds(lax.axis_index(AXES), 1), :]
        lists = [me[:, s : s + up(size, 128)] for s, size in zip(starts, sizes)]
        own = one_hot_rows(as_column(lists[0])[:chunk], coarse)

        def match(name, targets, sources, size):
            found = jnp.where(targets == sources, 1.0, 0.0)
            lane = lax.broadcasted_iota(jnp.int32, found.shape, 1)
            found = jnp.where(lane < size, found, 0.0)
            picks[keep.place(name), pl.ds(0, found.shape[1])] = found
            return found

        to_column = match("to_column", as_column(lists[1])[:column], lists[0], chunk)
        match("to_slab", as_column(lists[3])[:slab], lists[2], sizes[2])
        every = lax.broadcasted_iota(jnp.int32, (coarse, 1), 0).astype(jnp.float32)
        match("to_all", every, lists[4], sizes[4])
        spread = pick(weighted[...], own, (0, 0))
        wide = jnp.concatenate([basis, jnp.zeros((128 - chunk, nodes), jnp.float32)], axis=0).T
        images = dot(matrix[0, 0, 0], jnp.concatenate([begun_natural[...], wide], axis=1))
        both = jnp.concatenate([natural[...], natural[...] - images[:, :lanes]], axis=1)
        both = pick(surface, both)
        condensed = both[:, lanes:]
        for name, value in (
            ("load", both[:, :lanes]), ("condensed", condensed),
            ("tau", jnp.broadcast_to(tau, (8, lanes))),
        ):
            bank[keep.place(name), :] = value
        fields = [condensed] + [spread[:, s : s + lanes] for s in range(0, coarse, lanes)]
        ringed, flats[...] = packed(layout, *fields)
        coarse_local = dot(basis, images[:, lanes:])
        spread_rows = pick(coarse_local[:, :chunk], own)
        coarse_rows[...] = spread_rows
        if rides:
            ridden = part(spread_rows, to_column)
        else:
            ridden = jnp.zeros((column + PLAIN, lanes), jnp.float32)
        rings[...] = cat([ringed, ridden])

    bank, rings, flats, weighted, coarse_rows, picks = call(
        start,
        (element_load, local_matrix, dirichlet_inverse, coarse_basis, places, own_table),
        (
            floats(keep.rows["bank"], lanes), floats(count * ring_rows + column + PLAIN, lanes),
            floats(count * (rows - ring_rows), lanes), floats(chunk, rows),
            floats(chunk, coarse), floats(keep.rows["picks"], pick_lanes),
        ),
        scratch=[
            VMEM((nodes, lanes), jnp.float32), VMEM((inside, lanes), jnp.float32),
            VMEM((inside, lanes), jnp.float32), VMEM((nodes, lanes), jnp.float32),
        ],
    )
    element_load, local_matrix, dirichlet_inverse = lax.optimization_barrier(
        (element_load, local_matrix, dirichlet_inverse)
    )

    keep.arrays.update(bank=bank, picks=picks)

    def reorder(neumann, places):
        order, share = places[0:1, :], places[1:2, :]
        across = one_hot_columns(order, nodes)
        surface = one_hot_rows(as_column(order), nodes)
        return pick(surface, pick(neumann[0, 0, 0], across)) * as_column(share) * share

    def condense(matrix, inverse, places, weighted, out):
        places = places[...]
        order = places[0:1, :]
        picked = pick(matrix[0, 0, 0], one_hot_columns(order, nodes))
        surface = one_hot_rows(as_column(order), nodes)
        within = pick(surface, picked)
        coupling = jnp.concatenate(
            [picked[(i * n + j) * n + 1 : (i * n + j) * n + 1 + deep] for i, j in inner_pairs], axis=0
        )
        out[keep.place("coupling"), :] = coupling
        out[keep.place("weighted"), :] = weighted[...]
        out[keep.place("schur"), :] = within - dot(coupling, dot(inverse[0, 0, 0], coupling), (0, 0))

    def make_schur():
        (keep.arrays["matrices"],) = call(
            condense, (local_matrix, dirichlet_inverse, places, weighted),
            (floats(keep.rows["matrices"], rows),), flops=FILL,
        )
        return ()

    def make_scaled():
        run(reorder, neumann_inverse, places, flops=FILL, keep=keep, store=("scaled",))
        return ()

    step = coarse // PIECES

    def invert(first, last):
        for piece in range(first, last):

            def eliminated(matrix, piece=piece):
                return eliminate(matrix, range(piece * step, (piece + 1) * step))

            keep.arrays["coarse"] = run(eliminated, keep.arrays["coarse"], flops=FILL)

    def invert_early():
        if rides:
            invert(0, PIECES - 1)
        return ()

    def finish_inverse():
        if rides:
            invert(PIECES - 1, PIECES)
        keep.arrays["lift"] = run(dot, keep.arrays.pop("spread"), keep.arrays.pop("coarse"))
        return ()

    def other_inverse():
        spread_rows = jnp.broadcast_to(coarse_rows[None], (devices, *coarse_rows.shape))
        gathered = lax.all_to_all(spread_rows, AXES, 0, 0, tiled=True).reshape(-1, coarse)
        ids = jnp.asarray(table[:, :chunk].reshape(1, -1))
        summed = run(lambda ids, rows: pick(one_hot_columns(ids, coarse), rows), ids, gathered)
        factor = jnp.linalg.cholesky(summed)
        eye = jnp.eye(coarse, dtype=jnp.float32)
        return jax.scipy.linalg.cho_solve((factor, True), eye)

    def neumann_step(field, scaled, weighted):
        return dot(scaled, field), dot(weighted, field)

    def sent(field, loads, chosen, *extra):
        ringed, flats = packed(layout, field)
        return cat([ringed, part(loads, chosen, *extra)]), flats

    def first(field, *rest):
        pieces, (summed, _, weighted, scaled, chosen) = rest[:-5], rest[-5:]
        mapped, loads = neumann_step(field, scaled, weighted)
        spread = jnp.concatenate(pieces, axis=1) if len(pieces) > 1 else pieces[0]
        return (spread, summed, *sent(mapped, loads, chosen), field)

    keep.arrays["spread"], keep.arrays["coarse"], rings, flats = assemble(
        layout, count, shares, rings, flats, first, keep, ("weighted", "scaled", "to_column"),
        ("residual",), make_schur, make_scaled,
    )
    if not rides:
        keep.arrays["coarse"] = other_inverse()

    def apply_first(mapped, summed, _, condensed, tau, load, schur, lift):
        field = mapped + dot(lift, summed)
        image = dot(schur, field)
        energy = tau[:1] + jnp.sum(condensed * field, axis=0, keepdims=True)
        curvature = tau[:1] + jnp.sum(field * image, axis=0, keepdims=True)
        fill = jnp.zeros((6, lanes), jnp.float32)
        ringed, flats = packed(layout, image, load)
        ridden = jnp.zeros((column + PLAIN, lanes), jnp.float32)
        sums = jnp.concatenate([energy, curvature, fill], axis=0)
        return cat([ringed, ridden]), flats, field, image, sums

    rings, flats = assemble(
        layout, 1, shares, rings, flats, apply_first, keep,
        ("condensed", "tau", "load", "schur", "lift"), ("field0", "image0", "totals"), invert_early,
        finish_inverse,
    )

    def second(image, load, summed, _, sums, scaled, weighted, chosen):
        mapped, loads = neumann_step(image, scaled, weighted)
        return (*sent(mapped, loads, chosen, sums[:2]), image, load)

    rings, flats = assemble(
        layout, 2, shares, rings, flats, second, keep,
        ("totals", "scaled", "weighted", "to_column"), ("image0_sum", "load_sum"),
    )

    def apply_second(mapped, summed, totals, schur, condensed, tau, field0, image0, lift):
        field = mapped + dot(lift, summed)
        image = dot(schur, field)
        step = totals[:1] / totals[1:2]
        rest = 1.0 - step
        direction = field0 - step * field
        direction_image = image0 - step * image
        energy = rest * rest * tau[:1] + jnp.sum(
            (condensed - step * image0) * direction, axis=0, keepdims=True
        )
        curvature = rest * rest * tau[:1] + jnp.sum(
            direction * direction_image, axis=0, keepdims=True
        )
        cross = rest * tau[:1] + jnp.sum(direction * image0, axis=0, keepdims=True)
        ringed, flats = packed(layout, image)
        ridden = jnp.zeros((column, lanes), jnp.float32)
        fill = jnp.zeros((PLAIN - 3, lanes), jnp.float32)
        return cat([ringed, ridden, energy, curvature, cross, fill]), flats, field, totals

    rings, flats = assemble(
        layout, 1, shares, rings, flats, apply_second, keep,
        ("schur", "condensed", "tau", "field0", "image0", "lift"), ("field1", "totals"),
    )

    def put(out, surface, deep_rows, load, factor):
        m, block = n - 1, layout.block
        for i in range(n):
            for s, j in ((0, 0), (1, m)):
                out[i, j, pl.ds(0, m), :] = surface[pl.ds(s * block + i * m, m), :]
                out[i, j, pl.ds(m, 1), :] = surface[pl.ds((s + 2) * block + i * m + m - 1, 1), :]
            for j in range(1, m):
                for s, k in ((2, 0), (3, m)):
                    out[i, j, pl.ds(k, 1), :] = surface[pl.ds(s * block + i * m + j - 1, 1), :]
                if i in (0, m):
                    at = layout.ring_rows + (layout.flat if i else 0) + (j - 1) * deep
                    out[i, j, pl.ds(1, deep), :] = surface[pl.ds(at, deep), :]
                elif deep_rows is None:
                    out[i, j, pl.ds(1, deep), :] = factor * load[i, j, pl.ds(1, deep), :]
                else:
                    at = ((i - 1) * deep + j - 1) * deep
                    out[i, j, pl.ds(1, deep), :] = deep_rows[pl.ds(at, deep), :]

    def solve_inside(bank, matrices, inverse, load, out, inner_load):
        for index, (i, j) in enumerate(inner_pairs):
            inner_load[pl.ds(index * deep, deep), :] = load[i, j, pl.ds(1, deep), :]
        fields = jnp.concatenate([bank[keep.place("field0"), :], bank[keep.place("field1"), :]], axis=1)
        loads = jnp.concatenate([inner_load[...], inner_load[...]], axis=1)
        right = loads - dot(matrices[keep.place("coupling"), :], fields)
        out[...] = dot(inverse[0, 0, 0], right)

    def finish_inside():
        (keep.arrays["deep"],) = call(
            solve_inside, (keep.arrays["bank"], keep.arrays["matrices"], dirichlet_inverse, element_load),
            (floats(inside, 2 * lanes),), scratch=[VMEM((inside, lanes), jnp.float32)], flops=FILL,
        )
        return ()

    def leftover(image1, _, sums, totals, field0, field1, image0, residual, load_sum):
        energy, curvature = totals[:1], totals[1:2]
        step = energy / curvature
        energy_next, curvature_next, cross = sums[:1], sums[1:2], sums[2:3]
        ratio = energy_next / energy
        curvature_next = curvature_next + 2.0 * ratio * cross + ratio * ratio * curvature
        step_next = energy_next / curvature_next
        first = step + step_next * (1.0 + ratio)
        second = -step_next * step
        spill = load_sum - residual
        residual_surface = load_sum - first * (image0 + spill) - second * (image1 + spill)
        fill = jnp.zeros((6, lanes), jnp.float32)
        weights = jnp.concatenate([first, second, fill], axis=0)
        return first * field0 + second * field1, residual_surface, weights

    solution_surface, residual_surface, weights = assemble(
        layout, 1, shares, rings, flats, leftover, keep,
        ("totals", "field0", "field1", "image0_sum", "residual", "load_sum"), (), finish_inside,
    )

    def place(solution_surface, residual_surface, weights, both, load, one, two, deep_rows):
        first, second = weights[0:1, :], weights[1:2, :]
        deep_rows[...] = first * both[:, :lanes] + second * both[:, lanes:]
        put(one, solution_surface, deep_rows, None, None)
        put(two, residual_surface, None, load, 1.0 - first - second)

    shape = floats(*element_load.shape)
    solution_out, residual_out = call(
        place, (solution_surface, residual_surface, weights, keep.arrays["deep"], element_load),
        (shape, shape), scratch=[VMEM((inside, lanes), jnp.float32)],
    )
    return solution_out, residual_out


def solution(mesh):
    in_specs = (
        P("gx", "gy", "gz", None),
        P("gx", "gy", "gz", None, None),
        P("gx", "gy", "gz", None, None),
        P("gx", "gy", "gz", None, None),
        P("gx", "gy", "gz", None, None),
    )
    out_specs = (P("gx", "gy", "gz", None), P("gx", "gy", "gz", None))
    return jax.shard_map(local, mesh=mesh, in_specs=in_specs, out_specs=out_specs, check_vma=False)
```

time: 163 us -> 114 us (0.70)
  local copies, waits for them, and re-layouts: 22 us -> 2.29 us
  starting transfers between devices: 55.5 us -> 43.1 us
  waiting for transfers between devices: 41.5 us -> 30.6 us
  Pallas kernels: 40.6 us -> 36.4 us
    all_to_all x4 -> x0, starting transfers between devices: 20.1 us -> none  [the longest x2 8.41 us: local(): gathered = lax.all_to_all(loads, AXES, 0, 0, tiled=True)]
    unnamed x72 -> x18, local copies, waits for them, and re-layouts: 21.2 us -> 2.11 us
    ppermute x25 -> x35, waiting for transfers between devices: 41.5 us -> 30.6 us  [shifted(): lax.ppermute(value, axis, [(i, (i + step) % size) for i in range(size)])]
    ppermute x25 -> x35, starting transfers between devices: 35.4 us -> 43.1 us  [shifted(): lax.ppermute(value, axis, [(i, (i + step) % size) for i in range(size)])]
    pallas_call x26 -> x25, Pallas kernels: 40.6 us -> 36.4 us  [call(): pl.pallas_call(body, out_shape=[jax.ShapeDtypeStruct(x.shape, x.dtype) fo...]
  transfers between devices with their start and end apart: 29 -> 35, of which waited for: 17 -> 14; matrix products, arithmetic and copies ran while one was open for 0% -> 0% of each run, Pallas kernels for 17% -> 20%
where the time goes in v3:
time: 114 us; the launch traced here: 113 us
  starting transfers between devices  43.1 us (38%)
  Pallas kernels  36.4 us (32%)
  waiting for transfers between devices  30.6 us (27%)
  local copies, waits for them, and re-layouts  2.29 us (2%)
    ppermute x35, starting transfers between devices, shifted(): lax.ppermute(value, axis, [(i, (i + step) % size) for i in range(size)])  43.1 us
    pallas_call x25, Pallas kernels, call(): pl.pallas_call(body, out_shape=[jax.ShapeDtypeStruct(x.shape, x.dtype) fo...  36.4 us
    ppermute x35, waiting for transfers between devices, shifted(): lax.ppermute(value, axis, [(i, (i + step) % size) for i in range(size)])  30.6 us
  transfers between devices with their start and end apart: 35, of which 14 were waited for; matrix products, arithmetic and copies ran while one was open for 0% of the time, Pallas kernels for 20%

profile of v3, /device:TPU:0, one launch (start us, length us, event | category | flops | bytes accessed | tf_op | source)
XLA Modules:
  0.0 113.4 jit_solution(165993806816558897)
XLA Ops:
  0.7 1.9 %copy.72.matrix = f32[1,1,1,729,729]{4,3,2,1,0:T(8,128)S(1)} copy(f32[1,1,1,729,729]{4,2,3,1,0:T(1,128)} %param.8) | data formatting | bytes 4251528 | tf_op args[1]
  2.7 6.1 %shard_map.86 = (f32[4016,128]{1,0:T(8,128)S(1)}, f32[608,128]{1,0:T(8,128)S(1)}, f32[224,128]{1,0:T(8,128)S(1)}, f32[24,400]{1,0:T(8,128)S(1)}, f32[24,128]{1,0:T(8,128)}, /*index=5*/f32[208,256]{1,0:T(8,128)S(1)}) custom-call(f32[9,9,9,128]{3,2,1,0:T(8,128)S(1)} %copy-done, f32[1,1,1,729,729]{4,3,2,1,0:T(8,128)S(1)} %copy.72.matrix, ...), custom_call_target="tpu_custom_call" | custom-call | flops 1000000 | bytes 5884888 | tf_op jit(solution)/shard_map/pallas_call | solution.py:35
  10.6 3.0 %collective-permute-start.1 = (f32[208,128]{1,0:T(8,128)S(1)}, f32[208,128]{1,0:T(8,128)S(1)}, u32[]{:S(2)}, u32[]{:S(2)}) collective-permute-start(f32[208,128]{1,0:T(8,128)S(1)} %get-tuple-element.116), channel_id=1, source_target_pairs={{0,2},{2,4},{4,6},{6,0},{1,3},{3,5},{5,7},{7,1},{8,10},{10,12},{12... | collective-permute-start | bytes 319496 | tf_op jit(solution)/shard_map/ppermute | solution.py:210
  13.6 2.1 %collective-permute-start.2 = (f32[208,128]{1,0:T(8,128)S(1)}, f32[208,128]{1,0:T(8,128)S(1)}, u32[]{:S(2)}, u32[]{:S(2)}) collective-permute-start(f32[208,128]{1,0:T(8,128)S(1)} %get-tuple-element.117), channel_id=1, source_target_pairs={{0,6},{2,0},{4,2},{6,4},{1,7},{3,1},{5,3},{7,5},{8,14},{10,8},{12,... | collective-permute-start | bytes 319496 | tf_op jit(solution)/shard_map/ppermute | solution.py:210
  16.8 5.7 %shard_map.88.refs_6_ = f32[1168,400]{1,0:T(8,128)S(1)} custom-call(f32[1,1,1,729,729]{4,3,2,1,0:T(8,128)S(1)} %copy.75.matrix, f32[1,1,1,343,343]{4,3,2,1,0:T(8,128)S(1)} %copy.76.inverse, f32[8,400]{1,0:T(8,128)S(1)} %copy-done.1, f32[24,400]{1,0:T(8,128)S(1)} %get-tuple-element.123.weighted), custom_call_target="tpu_custom_call" | custom-call | flops 100000000 | bytes 4516360 | tf_op jit(solution)/shard_map/pallas_call | solution.py:35
  27.4 2.9 %shard_map.90 = (f32[4016,128]{1,0:T(8,128)S(1)}, f32[208,256]{1,0:T(8,128)S(1)}, f32[1168,400]{1,0:T(8,128)S(1)}) custom-call(f32[1,1,1,729,729]{4,3,2,1,0:T(8,128)S(1)} %copy.77.refs_0_, f32[8,400]{1,0:T(8,128)S(1)} %copy-done.1, f32[4016,128]{1,0:T(8,128)S(1)} %get-tuple-element.127.refs_2_, ...), custom_call_target="tpu_custom_call", output_to_operand_aliasing={{0}: (2, {}), {1}: (3, {}), {2}: (4, {})} | custom-call | flops 100000000 | bytes 10414532 | tf_op jit(solution)/shard_map/pallas_call | solution.py:35
  35.2 2.3 %collective-permute-start.9 = (f32[120,128]{1,0:T(8,128)S(1)}, f32[120,128]{1,0:T(8,128)S(1)}, u32[]{:S(2)}, u32[]{:S(2)}) collective-permute-start(f32[120,128]{1,0:T(8,128)S(1)} %get-tuple-element.141), channel_id=1, source_target_pairs={{0,6},{2,0},{4,2},{6,4},{1,7},{3,1},{5,3},{7,5},{8,14},{10,8},{12,... | collective-permute-start | bytes 184328 | tf_op jit(solution)/shard_map/ppermute | solution.py:210
  37.9 2.7 %shard_map.93.refs_0_ = f32[128,128]{1,0:T(8,128)S(1)} custom-call(f32[128,128]{1,0:T(8,128)S(1)} %get-tuple-element.147.refs_0_), custom_call_target="tpu_custom_call" | custom-call | flops 100000000 | bytes 131072 | tf_op jit(solution)/shard_map/pallas_call | solution.py:35
  40.6 2.7 %shard_map.94.refs_0_ = f32[128,128]{1,0:T(8,128)S(1)} custom-call(f32[128,128]{1,0:T(8,128)S(1)} %shard_map.93.refs_0_), custom_call_target="tpu_custom_call" | custom-call | flops 100000000 | bytes 131072 | tf_op jit(solution)/shard_map/pallas_call | solution.py:35
  43.3 2.7 %shard_map.95.refs_8_ = f32[128,128]{1,0:T(8,128)S(1)} custom-call(f32[128,128]{1,0:T(8,128)S(1)} %shard_map.94.refs_0_), custom_call_target="tpu_custom_call" | custom-call | flops 100000000 | bytes 131072 | tf_op jit(solution)/shard_map/pallas_call | solution.py:35
  49.7 2.7 %shard_map.97.refs_1_ = f32[128,128]{1,0:T(8,128)S(1)} custom-call(f32[128,128]{1,0:T(8,128)S(1)} %get-tuple-element.155.refs_0_), custom_call_target="tpu_custom_call" | custom-call | flops 100000000 | bytes 131072 | tf_op jit(solution)/shard_map/pallas_call | solution.py:35
  56.7 3.7 %collective-permute-start.16 = (f32[208,128]{1,0:T(8,128)S(1)}, f32[208,128]{1,0:T(8,128)S(1)}, u32[]{:S(2)}, u32[]{:S(2)}) collective-permute-start(f32[208,128]{1,0:T(8,128)S(1)} %get-tuple-element.163), channel_id=1, source_target_pairs={{0,6},{2,0},{4,2},{6,4},{1,7},{3,1},{5,3},{7,5},{8,14},{10,8},{12,... | collective-permute-start | bytes 319496 | tf_op jit(solution)/shard_map/ppermute | solution.py:210
  61.1 5.2 %collective-permute-done.17.refs_3_ = f32[32,128]{1,0:T(8,128)S(1)} collective-permute-done((f32[32,128]{1,0:T(8,128)S(1)}, f32[32,128]{1,0:T(8,128)S(1)}, u32[]{:S(2)}, u32[]{:S(2)}) %collective-permute-start.17) | collective-permute-done | bytes 16416 | tf_op jit(solution)/shard_map/ppermute | solution.py:210
  67.4 2.1 %collective-permute-start.19 = (f32[240,128]{1,0:T(8,128)S(1)}, f32[240,128]{1,0:T(8,128)S(1)}, u32[]{:S(2)}, u32[]{:S(2)}) collective-permute-start(f32[240,128]{1,0:T(8,128)S(1)} %get-tuple-element.170), channel_id=1, source_target_pairs={{0,24},{8,0},{16,8},{24,16},{1,25},{9,1},{17,9},{25,17},{2,26},{10... | collective-permute-start | bytes 368648 | tf_op jit(solution)/shard_map/ppermute | solution.py:210
  70.8 3.1 %collective-permute-done.20.refs_3_ = f32[64,128]{1,0:T(8,128)S(1)} collective-permute-done((f32[64,128]{1,0:T(8,128)S(1)}, f32[64,128]{1,0:T(8,128)S(1)}, u32[]{:S(2)}, u32[]{:S(2)}) %collective-permute-start.20) | collective-permute-done | bytes 32800 | tf_op jit(solution)/shard_map/ppermute | solution.py:210
  77.8 3.8 %collective-permute-start.23 = (f32[120,128]{1,0:T(8,128)S(1)}, f32[120,128]{1,0:T(8,128)S(1)}, u32[]{:S(2)}, u32[]{:S(2)}) collective-permute-start(f32[120,128]{1,0:T(8,128)S(1)} %get-tuple-element.183), channel_id=1, source_target_pairs={{0,6},{2,0},{4,2},{6,4},{1,7},{3,1},{5,3},{7,5},{8,14},{10,8},{12,... | collective-permute-start | bytes 184328 | tf_op jit(solution)/shard_map/ppermute | solution.py:210
  81.6 4.6 %collective-permute-done.24.refs_3_ = f32[32,128]{1,0:T(8,128)S(1)} collective-permute-done((f32[32,128]{1,0:T(8,128)S(1)}, f32[32,128]{1,0:T(8,128)S(1)}, u32[]{:S(2)}, u32[]{:S(2)}) %collective-permute-start.24) | collective-permute-done | bytes 16416 | tf_op jit(solution)/shard_map/ppermute | solution.py:210
  87.3 2.1 %collective-permute-start.26 = (f32[152,128]{1,0:T(8,128)S(1)}, f32[152,128]{1,0:T(8,128)S(1)}, u32[]{:S(2)}, u32[]{:S(2)}) collective-permute-start(f32[152,128]{1,0:T(8,128)S(1)} %get-tuple-element.190), channel_id=1, source_target_pairs={{0,24},{8,0},{16,8},{24,16},{1,25},{9,1},{17,9},{25,17},{2,26},{10... | collective-permute-start | bytes 233480 | tf_op jit(solution)/shard_map/ppermute | solution.py:210
  90.3 3.1 %collective-permute-done.27.refs_3_ = f32[64,128]{1,0:T(8,128)S(1)} collective-permute-done((f32[64,128]{1,0:T(8,128)S(1)}, f32[64,128]{1,0:T(8,128)S(1)}, u32[]{:S(2)}, u32[]{:S(2)}) %collective-permute-start.27) | collective-permute-done | bytes 32800 | tf_op jit(solution)/shard_map/ppermute | solution.py:210
  96.5 3.8 %collective-permute-start.30 = (f32[120,128]{1,0:T(8,128)S(1)}, f32[120,128]{1,0:T(8,128)S(1)}, u32[]{:S(2)}, u32[]{:S(2)}) collective-permute-start(f32[120,128]{1,0:T(8,128)S(1)} %get-tuple-element.203), channel_id=1, source_target_pairs={{0,6},{2,0},{4,2},{6,4},{1,7},{3,1},{5,3},{7,5},{8,14},{10,8},{12,... | collective-permute-start | bytes 184328 | tf_op jit(solution)/shard_map/ppermute | solution.py:210
  100.4 2.4 %shard_map.107.refs_8_ = f32[343,256]{1,0:T(8,128)S(1)} custom-call(f32[4016,128]{1,0:T(8,128)S(1)} %get-tuple-element.205.bank.refs_4_, f32[1168,400]{1,0:T(8,128)S(1)} %get-tuple-element.207.matrices.refs_6_, f32[1,1,1,343,343]{4,3,2,1,0:T(8,128)S(1)} %copy.76.inverse, f32[9,9,9,128]{3,2,1,0:T(8,128)S(1)} %copy-done), custom_call_target="tpu_custom_call" | custom-call | flops 100000000 | bytes 5120068 | tf_op jit(solution)/shard_map/pallas_call | solution.py:35
  102.8 2.2 %collective-permute-done.31.refs_3_ = f32[32,128]{1,0:T(8,128)S(1)} collective-permute-done((f32[32,128]{1,0:T(8,128)S(1)}, f32[32,128]{1,0:T(8,128)S(1)}, u32[]{:S(2)}, u32[]{:S(2)}) %collective-permute-start.31) | collective-permute-done | bytes 16416 | tf_op jit(solution)/shard_map/ppermute | solution.py:210
  106.0 2.2 %collective-permute-start.33 = (f32[152,128]{1,0:T(8,128)S(1)}, f32[152,128]{1,0:T(8,128)S(1)}, u32[]{:S(2)}, u32[]{:S(2)}) collective-permute-start(f32[152,128]{1,0:T(8,128)S(1)} %get-tuple-element.211), channel_id=1, source_target_pairs={{0,24},{8,0},{16,8},{24,16},{1,25},{9,1},{17,9},{25,17},{2,26},{10... | collective-permute-start | bytes 233480 | tf_op jit(solution)/shard_map/ppermute | solution.py:210
  109.0 3.1 %collective-permute-done.34.refs_3_ = f32[64,128]{1,0:T(8,128)S(1)} collective-permute-done((f32[64,128]{1,0:T(8,128)S(1)}, f32[64,128]{1,0:T(8,128)S(1)}, u32[]{:S(2)}, u32[]{:S(2)}) %collective-permute-start.34) | collective-permute-done | bytes 32800 | tf_op jit(solution)/shard_map/ppermute | solution.py:210
  (91 shorter events, 36.3 us)
Async XLA Ops:
  10.6 11.9 %collective-permute-start.1 = (f32[208,128]{1,0:T(8,128)S(1)}, f32[208,128]{1,0:T(8,128)S(1)}, u32[]{:S(2)}, u32[]{:S(2)}) collective-permute-start(f32[208,128]{1,0:T(8,128)S(1)} %get-tuple-element.116), channel_id=1, source_target_pairs={{0,2},{2,4},{4,6},{6,0},{1,3},{3,5},{5,7},{7,1},{8,10},{10,12},{12... | collective-permute-start | bytes 319496 | tf_op jit(solution)/shard_map/ppermute | solution.py:210
  13.6 8.9 %collective-permute-start.2 = (f32[208,128]{1,0:T(8,128)S(1)}, f32[208,128]{1,0:T(8,128)S(1)}, u32[]{:S(2)}, u32[]{:S(2)}) collective-permute-start(f32[208,128]{1,0:T(8,128)S(1)} %get-tuple-element.117), channel_id=1, source_target_pairs={{0,6},{2,0},{4,2},{6,4},{1,7},{3,1},{5,3},{7,5},{8,14},{10,8},{12,... | collective-permute-start | bytes 319496 | tf_op jit(solution)/shard_map/ppermute | solution.py:210
  15.7 6.8 %collective-permute-start.3 = (f32[32,128]{1,0:T(8,128)S(1)}, f32[32,128]{1,0:T(8,128)S(1)}, u32[]{:S(2)}, u32[]{:S(2)}) collective-permute-start(f32[32,128]{1,0:T(8,128)S(1)} %get-tuple-element.118.refs_2_), channel_id=1, source_target_pairs={{0,4},{2,6},{4,0},{6,2},{1,5},{3,7},{5,1},{7,3},{8,12},{10,14},{12... | collective-permute-start | bytes 49160 | tf_op jit(solution)/shard_map/ppermute | solution.py:210
  22.8 7.6 %collective-permute-start.4 = (f32[240,128]{1,0:T(8,128)S(1)}, f32[240,128]{1,0:T(8,128)S(1)}, u32[]{:S(2)}, u32[]{:S(2)}) collective-permute-start(f32[240,128]{1,0:T(8,128)S(1)} %get-tuple-element.124), channel_id=1, source_target_pairs={{0,8},{8,16},{16,24},{24,0},{1,9},{9,17},{17,25},{25,1},{2,10},{10... | collective-permute-start | bytes 368648 | tf_op jit(solution)/shard_map/ppermute | solution.py:210
  24.3 6.7 %collective-permute-start.5 = (f32[240,128]{1,0:T(8,128)S(1)}, f32[240,128]{1,0:T(8,128)S(1)}, u32[]{:S(2)}, u32[]{:S(2)}) collective-permute-start(f32[240,128]{1,0:T(8,128)S(1)} %get-tuple-element.125), channel_id=1, source_target_pairs={{0,24},{8,0},{16,8},{24,16},{1,25},{9,1},{17,9},{25,17},{2,26},{10... | collective-permute-start | bytes 368648 | tf_op jit(solution)/shard_map/ppermute | solution.py:210
  33.6 12.4 %collective-permute-start.8 = (f32[120,128]{1,0:T(8,128)S(1)}, f32[120,128]{1,0:T(8,128)S(1)}, u32[]{:S(2)}, u32[]{:S(2)}) collective-permute-start(f32[120,128]{1,0:T(8,128)S(1)} %get-tuple-element.140), channel_id=1, source_target_pairs={{0,2},{2,4},{4,6},{6,0},{1,3},{3,5},{5,7},{7,1},{8,10},{10,12},{12... | collective-permute-start | bytes 184328 | tf_op jit(solution)/shard_map/ppermute | solution.py:210
  35.2 10.8 %collective-permute-start.9 = (f32[120,128]{1,0:T(8,128)S(1)}, f32[120,128]{1,0:T(8,128)S(1)}, u32[]{:S(2)}, u32[]{:S(2)}) collective-permute-start(f32[120,128]{1,0:T(8,128)S(1)} %get-tuple-element.141), channel_id=1, source_target_pairs={{0,6},{2,0},{4,2},{6,4},{1,7},{3,1},{5,3},{7,5},{8,14},{10,8},{12,... | collective-permute-start | bytes 184328 | tf_op jit(solution)/shard_map/ppermute | solution.py:210
  37.5 8.5 %collective-permute-start.10 = (f32[32,128]{1,0:T(8,128)S(1)}, f32[32,128]{1,0:T(8,128)S(1)}, u32[]{:S(2)}, u32[]{:S(2)}) collective-permute-start(f32[32,128]{1,0:T(8,128)S(1)} %get-tuple-element.142.refs_2_), channel_id=1, source_target_pairs={{0,4},{2,6},{4,0},{6,2},{1,5},{3,7},{5,1},{7,3},{8,12},{10,14},{12... | collective-permute-start | bytes 49160 | tf_op jit(solution)/shard_map/ppermute | solution.py:210
  46.3 6.9 %collective-permute-start.11 = (f32[152,128]{1,0:T(8,128)S(1)}, f32[152,128]{1,0:T(8,128)S(1)}, u32[]{:S(2)}, u32[]{:S(2)}) collective-permute-start(f32[152,128]{1,0:T(8,128)S(1)} %get-tuple-element.148), channel_id=1, source_target_pairs={{0,8},{8,16},{16,24},{24,0},{1,9},{9,17},{17,25},{25,1},{2,10},{10... | collective-permute-start | bytes 233480 | tf_op jit(solution)/shard_map/ppermute | solution.py:210
  47.8 5.4 %collective-permute-start.12 = (f32[152,128]{1,0:T(8,128)S(1)}, f32[152,128]{1,0:T(8,128)S(1)}, u32[]{:S(2)}, u32[]{:S(2)}) collective-permute-start(f32[152,128]{1,0:T(8,128)S(1)} %get-tuple-element.149), channel_id=1, source_target_pairs={{0,24},{8,0},{16,8},{24,16},{1,25},{9,1},{17,9},{25,17},{2,26},{10... | collective-permute-start | bytes 233480 | tf_op jit(solution)/shard_map/ppermute | solution.py:210
  56.5 9.8 %collective-permute-start.15 = (f32[208,128]{1,0:T(8,128)S(1)}, f32[208,128]{1,0:T(8,128)S(1)}, u32[]{:S(2)}, u32[]{:S(2)}) collective-permute-start(f32[208,128]{1,0:T(8,128)S(1)} %get-tuple-element.162), channel_id=1, source_target_pairs={{0,2},{2,4},{4,6},{6,0},{1,3},{3,5},{5,7},{7,1},{8,10},{10,12},{12... | collective-permute-start | bytes 319496 | tf_op jit(solution)/shard_map/ppermute | solution.py:210
  56.7 9.6 %collective-permute-start.16 = (f32[208,128]{1,0:T(8,128)S(1)}, f32[208,128]{1,0:T(8,128)S(1)}, u32[]{:S(2)}, u32[]{:S(2)}) collective-permute-start(f32[208,128]{1,0:T(8,128)S(1)} %get-tuple-element.163), channel_id=1, source_target_pairs={{0,6},{2,0},{4,2},{6,4},{1,7},{3,1},{5,3},{7,5},{8,14},{10,8},{12,... | collective-permute-start | bytes 319496 | tf_op jit(solution)/shard_map/ppermute | solution.py:210
  60.4 6.0 %collective-permute-start.17 = (f32[32,128]{1,0:T(8,128)S(1)}, f32[32,128]{1,0:T(8,128)S(1)}, u32[]{:S(2)}, u32[]{:S(2)}) collective-permute-start(f32[32,128]{1,0:T(8,128)S(1)} %get-tuple-element.164.refs_2_), channel_id=1, source_target_pairs={{0,4},{2,6},{4,0},{6,2},{1,5},{3,7},{5,1},{7,3},{8,12},{10,14},{12... | collective-permute-start | bytes 49160 | tf_op jit(solution)/shard_map/ppermute | solution.py:210
  66.6 7.2 %collective-permute-start.18 = (f32[240,128]{1,0:T(8,128)S(1)}, f32[240,128]{1,0:T(8,128)S(1)}, u32[]{:S(2)}, u32[]{:S(2)}) collective-permute-start(f32[240,128]{1,0:T(8,128)S(1)} %get-tuple-element.169), channel_id=1, source_target_pairs={{0,8},{8,16},{16,24},{24,0},{1,9},{9,17},{17,25},{25,1},{2,10},{10... | collective-permute-start | bytes 368648 | tf_op jit(solution)/shard_map/ppermute | solution.py:210
  67.4 7.7 %collective-permute-start.19 = (f32[240,128]{1,0:T(8,128)S(1)}, f32[240,128]{1,0:T(8,128)S(1)}, u32[]{:S(2)}, u32[]{:S(2)}) collective-permute-start(f32[240,128]{1,0:T(8,128)S(1)} %get-tuple-element.170), channel_id=1, source_target_pairs={{0,24},{8,0},{16,8},{24,16},{1,25},{9,1},{17,9},{25,17},{2,26},{10... | collective-permute-start | bytes 368648 | tf_op jit(solution)/shard_map/ppermute | solution.py:210
  77.7 8.5 %collective-permute-start.22 = (f32[120,128]{1,0:T(8,128)S(1)}, f32[120,128]{1,0:T(8,128)S(1)}, u32[]{:S(2)}, u32[]{:S(2)}) collective-permute-start(f32[120,128]{1,0:T(8,128)S(1)} %get-tuple-element.182), channel_id=1, source_target_pairs={{0,2},{2,4},{4,6},{6,0},{1,3},{3,5},{5,7},{7,1},{8,10},{10,12},{12... | collective-permute-start | bytes 184328 | tf_op jit(solution)/shard_map/ppermute | solution.py:210
  77.8 8.4 %collective-permute-start.23 = (f32[120,128]{1,0:T(8,128)S(1)}, f32[120,128]{1,0:T(8,128)S(1)}, u32[]{:S(2)}, u32[]{:S(2)}) collective-permute-start(f32[120,128]{1,0:T(8,128)S(1)} %get-tuple-element.183), channel_id=1, source_target_pairs={{0,6},{2,0},{4,2},{6,4},{1,7},{3,1},{5,3},{7,5},{8,14},{10,8},{12,... | collective-permute-start | bytes 184328 | tf_op jit(solution)/shard_map/ppermute | solution.py:210
  81.6 4.6 %collective-permute-start.24 = (f32[32,128]{1,0:T(8,128)S(1)}, f32[32,128]{1,0:T(8,128)S(1)}, u32[]{:S(2)}, u32[]{:S(2)}) collective-permute-start(f32[32,128]{1,0:T(8,128)S(1)} %get-tuple-element.184.refs_2_), channel_id=1, source_target_pairs={{0,4},{2,6},{4,0},{6,2},{1,5},{3,7},{5,1},{7,3},{8,12},{10,14},{12... | collective-permute-start | bytes 49160 | tf_op jit(solution)/shard_map/ppermute | solution.py:210
  86.4 6.9 %collective-permute-start.25 = (f32[152,128]{1,0:T(8,128)S(1)}, f32[152,128]{1,0:T(8,128)S(1)}, u32[]{:S(2)}, u32[]{:S(2)}) collective-permute-start(f32[152,128]{1,0:T(8,128)S(1)} %get-tuple-element.189), channel_id=1, source_target_pairs={{0,8},{8,16},{16,24},{24,0},{1,9},{9,17},{17,25},{25,1},{2,10},{10... | collective-permute-start | bytes 233480 | tf_op jit(solution)/shard_map/ppermute | solution.py:210
  87.3 6.0 %collective-permute-start.26 = (f32[152,128]{1,0:T(8,128)S(1)}, f32[152,128]{1,0:T(8,128)S(1)}, u32[]{:S(2)}, u32[]{:S(2)}) collective-permute-start(f32[152,128]{1,0:T(8,128)S(1)} %get-tuple-element.190), channel_id=1, source_target_pairs={{0,24},{8,0},{16,8},{24,16},{1,25},{9,1},{17,9},{25,17},{2,26},{10... | collective-permute-start | bytes 233480 | tf_op jit(solution)/shard_map/ppermute | solution.py:210
  96.5 8.5 %collective-permute-start.29 = (f32[120,128]{1,0:T(8,128)S(1)}, f32[120,128]{1,0:T(8,128)S(1)}, u32[]{:S(2)}, u32[]{:S(2)}) collective-permute-start(f32[120,128]{1,0:T(8,128)S(1)} %get-tuple-element.202), channel_id=1, source_target_pairs={{0,2},{2,4},{4,6},{6,0},{1,3},{3,5},{5,7},{7,1},{8,10},{10,12},{12... | collective-permute-start | bytes 184328 | tf_op jit(solution)/shard_map/ppermute | solution.py:210
  96.5 8.5 %collective-permute-start.30 = (f32[120,128]{1,0:T(8,128)S(1)}, f32[120,128]{1,0:T(8,128)S(1)}, u32[]{:S(2)}, u32[]{:S(2)}) collective-permute-start(f32[120,128]{1,0:T(8,128)S(1)} %get-tuple-element.203), channel_id=1, source_target_pairs={{0,6},{2,0},{4,2},{6,4},{1,7},{3,1},{5,3},{7,5},{8,14},{10,8},{12,... | collective-permute-start | bytes 184328 | tf_op jit(solution)/shard_map/ppermute | solution.py:210
  105.2 6.9 %collective-permute-start.32 = (f32[152,128]{1,0:T(8,128)S(1)}, f32[152,128]{1,0:T(8,128)S(1)}, u32[]{:S(2)}, u32[]{:S(2)}) collective-permute-start(f32[152,128]{1,0:T(8,128)S(1)} %get-tuple-element.210), channel_id=1, source_target_pairs={{0,8},{8,16},{16,24},{24,0},{1,9},{9,17},{17,25},{25,1},{2,10},{10... | collective-permute-start | bytes 233480 | tf_op jit(solution)/shard_map/ppermute | solution.py:210
  106.0 6.1 %collective-permute-start.33 = (f32[152,128]{1,0:T(8,128)S(1)}, f32[152,128]{1,0:T(8,128)S(1)}, u32[]{:S(2)}, u32[]{:S(2)}) collective-permute-start(f32[152,128]{1,0:T(8,128)S(1)} %get-tuple-element.211), channel_id=1, source_target_pairs={{0,24},{8,0},{16,8},{24,16},{1,25},{9,1},{17,9},{25,17},{2,26},{10... | collective-permute-start | bytes 233480 | tf_op jit(solution)/shard_map/ppermute | solution.py:210
  (18 other events, 55.4 us)

commit v4 on v3

--- a/solution.py
+++ b/solution.py
@@ -229,17 +229,21 @@
 
 
 def assemble(
-    layout, count, shares, rings, flats, function, keep, use=(), store=(), beside_y=None, beside_x=None
+    layout, count, shares, rings, flats, function, keep, use=(), store=(), beside_z=None, beside_y=None,
+    beside_x=None,
 ):
     ring_rows, flat_rows = layout.ring_rows, layout.rows - layout.ring_rows
     split = lambda value, size: [value[i * size : (i + 1) * size] for i in range(count)]
-    column, slab = shares
-
-    steps = steps_of("gz")
+    column, slab = shares or (0, 0)
+    far_steps = lambda axis: steps_of(axis)[2:] if shares else []
+    picked = lambda name: (name,) if column else ()
+
+    steps = [*steps_of("gz")[:2], *far_steps("gz")]
     sums = rings[count * ring_rows :] if len(steps) > 2 else None
     others = [shifted(rings, "gz", step) for step in steps[:2]]
     others += [shifted(sums, "gz", step) for step in steps[2:]]
-    near = min(2, len(steps))
+    ties = beside_z() if beside_z else ()
+    near = len(steps_of("gz")[:2])
 
     def after_z(rings, flats, *others):
         done, low, high = [], [], []
@@ -252,29 +256,33 @@
             done.append(ring)
             low.append(sides[0])
             high.append(sides[1])
+        if not shares:
+            return cat(low), cat(high), cat([*done, flats])
         own = rings[count * ring_rows :]
         for index, other in enumerate(others):
             own = own + (other[count * ring_rows :] if index < near else other)
         return cat([*low, own]), cat([*high, own]), own, cat([*done, flats])
 
     work = ("work", count * layout.rows)
-    low, high, own = run(after_z, rings, flats, *others, keep=keep, store=("work",))
+    low, high, *own = run(after_z, rings, flats, *others, after=ties, keep=keep, store=("work",))
+    far = [shifted(own[0], "gy", step) for step in far_steps("gy")]
     below, above = both_ways(low, high, "gy")
-    steps = steps_of("gy")
-    far = [shifted(own, "gy", step) for step in steps[2:]]
     ties = beside_y() if beside_y else ()
 
-    def all_parts(own, below, above, far, edge, steps):
+    def all_parts(own, below, above, far, edge, axis):
         parts = [own, below[edge:]]
-        return parts + ([above[edge:]] if len(steps) > 1 else []) + list(far)
+        return parts + ([above[edge:]] if len(steps_of(axis)) > 1 else []) + list(far)
 
     def merged(chosen, parts, size):
         plain = sum(part[size:] for part in parts)
+        if not size:
+            return (plain,)
         wide = cat([part[:size] for part in parts])
-        return pick(chosen[:, : wide.shape[0]].astype(jnp.bfloat16), wide), plain
-
-    def after_y(below, above, own, *rest):
-        far, (both, chosen) = rest[:-2], rest[-2:]
+        return pick(chosen[0][:, : wide.shape[0]].astype(jnp.bfloat16), wide), plain
+
+    def after_y(below, above, *rest):
+        own, rest = rest[: len(own_y)], rest[len(own_y) :]
+        far, both, chosen = rest[: len(far_y)], rest[len(far_y)], rest[len(far_y) + 1 :]
         done, low, high = [], [], []
         rings, flats = both[: count * ring_rows], both[count * ring_rows :]
         edge = count * layout.y_rows
@@ -288,30 +296,38 @@
             done.append(ring)
             low.append(sides[0])
             high.append(sides[1])
-        own = cat(merged(chosen, all_parts(own, below, above, far, edge, steps), column))
+        if not shares:
+            return cat(low), cat(high), cat([*done, flats])
+        own = cat(merged(chosen, all_parts(own[0], below, above, far, edge, "gy"), column))
         return cat([*low, own]), cat([*high, own]), own, cat([*done, flats])
 
-    low, high, own = run(
-        after_y, below, above, own, *far, after=ties, keep=keep, use=(work, "to_slab"), store=("work",)
-    )
+    own_y, far_y = own, far
+    low, high, *own = run(
+        after_y, below, above, *own, *far, after=ties, keep=keep, use=(work, *picked("to_slab")),
+        store=("work",),
+    )
+    far = [shifted(own[0], "gx", step) for step in far_steps("gx")]
     below, above = both_ways(low, high, "gx")
-    steps = steps_of("gx")
-    far = [shifted(own, "gx", step) for step in steps[2:]]
     ties = beside_x() if beside_x else ()
 
-    def after_x(below, above, own, *rest):
-        far, (both, chosen), rest = rest[: len(steps) - 2], rest[len(steps) - 2 : len(steps)], rest[len(steps) :]
+    def after_x(below, above, *rest):
+        own_x, rest = rest[: len(own)], rest[len(own) :]
+        far_x, both, rest = rest[: len(far)], rest[len(far)], rest[len(far) + 1 :]
+        chosen, rest = (rest[:1], rest[1:]) if column else ((), rest)
         rings, flats = both[: count * ring_rows], both[count * ring_rows :]
         edge = count * layout.x_rows
         parts = (
             split(rings, ring_rows), split(flats, flat_rows), split(below[:edge], layout.x_rows),
             split(above[:edge], layout.x_rows),
         )
-        sums = merged(chosen, all_parts(own, below, above, far, edge, steps), slab)
+        sums = ()
+        if shares:
+            sums = merged(chosen, all_parts(own_x[0], below, above, far_x, edge, "gx"), slab)
         return function(*[layout.fold_x(*values) for values in zip(*parts)], *sums, *rest)
 
     return run(
-        after_x, below, above, own, *far, after=ties, keep=keep, use=(work, "to_all", *use), store=store
+        after_x, below, above, *own, *far, after=ties, keep=keep,
+        use=(work, *picked("to_all"), *use), store=store,
     )
 
 
@@ -331,6 +347,37 @@
         pairs = [(part, right) for part in parts_of(left)]
     terms = [lax.dot_general(a, b, dims, preferred_element_type=jnp.float32) for a, b in pairs]
     return terms[0] + terms[1] + terms[2]
+
+
+def stacked(value):
+    return jnp.concatenate(parts_of(value), axis=0)
+
+
+def product(stack, right):
+    rows, lanes = stack.shape[0] // 3, right.shape[1]
+    high, middle, low = parts_of(right)
+    times = lambda a, b: jnp.dot(a, b, preferred_element_type=jnp.float32)
+    wide = times(stack[: 2 * rows], jnp.concatenate([high, middle], axis=1))
+    small = wide[rows:, lanes:] + times(stack[:rows], low) + times(stack[2 * rows :], high)
+    return wide[:rows, :lanes] + (wide[:rows, lanes:] + wide[rows:, :lanes] + small)
+
+
+def runs_of(places):
+    found, at = [], 0
+    while at < len(places):
+        if places[at] < 0:
+            at += 1
+            continue
+        size, stride = 1, 1
+        if at + 1 < len(places) and places[at + 1] > places[at]:
+            stride = int(places[at + 1] - places[at])
+            while at + size < len(places) and places[at + size] - places[at + size - 1] == stride:
+                size += 1
+            if size == 2 and stride > 1:
+                size = 1
+        found.append((at, int(places[at]), size, stride if size > 1 else 1))
+        at += size
+    return found
 
 
 def one_hot_rows(column, count):
@@ -399,12 +446,22 @@
     count = matrix.shape[0]
     rows = lax.broadcasted_iota(jnp.int32, (8, count), 0)
     lanes = lax.broadcasted_iota(jnp.int32, (1, count), 1)
-    for k in pivots:
-        tile = k // 8 * 8
-        column = jnp.take_along_axis(matrix, jnp.full(matrix.shape, k, jnp.int32), axis=1)
-        row = jnp.where(lanes == k, 1.0, matrix[k : k + 1, :]) / column[k : k + 1, :]
-        matrix = jnp.where(lanes == k, 0.0, matrix) - column * row
-        own = jnp.where(rows == k - tile, row, matrix[tile : tile + 8])
+    for k in pivots[::2]:
+        m, tile = k + 1, k // 8 * 8
+        spread = lambda lane: jnp.take_along_axis(
+            matrix, jnp.full(matrix.shape, lane, jnp.int32), axis=1
+        )
+        column0, column1 = spread(k), spread(m)
+        a, b, d = column0[k:m], column1[k:m], column1[m : m + 1]
+        scale = 1.0 / (a * d - b * b)
+        here = (lanes == k) | (lanes == m)
+        row0 = jnp.where(here, jnp.where(lanes == k, 1.0, 0.0), matrix[k:m, :])
+        row1 = jnp.where(here, jnp.where(lanes == m, 1.0, 0.0), matrix[m : m + 1, :])
+        new0 = (d * row0 - b * row1) * scale
+        new1 = (a * row1 - b * row0) * scale
+        matrix = jnp.where(here, 0.0, matrix) - column0 * new0 - column1 * new1
+        own = jnp.where(rows == k - tile, new0, matrix[tile : tile + 8])
+        own = jnp.where(rows == m - tile, new1, own)
         parts = [matrix[:tile], own, matrix[tile + 8 :]]
         matrix = jnp.concatenate([part for part in parts if part.shape[0]], axis=0)
     return matrix
@@ -432,10 +489,6 @@
     inner_pairs = [(i, j) for i in range(1, n - 1) for j in range(1, n - 1)]
     deep = n - 2
 
-    def part(loads, chosen, *extra):
-        mapped = pick(chosen[:, :chunk].astype(jnp.bfloat16), loads)
-        fill = jnp.zeros((PLAIN - sum(rows.shape[0] for rows in extra), lanes), jnp.float32)
-        return cat([mapped, *extra, fill])
 
     count = 1 + -(-coarse // lanes)
     ring_rows = layout.ring_rows
@@ -447,115 +500,149 @@
     )
     keep.plan("picks", [("to_column", column), ("to_slab", slab), ("to_all", coarse)])
     pick_lanes = up(max(sizes), 128)
-    keep.plan(
-        "matrices", [("schur", rows), ("scaled", rows), ("coupling", inside), ("weighted", chunk)]
-    )
-
-    def start(
-        load, matrix, inverse, basis_in, places, own_table,
-        bank, rings, flats, weighted, coarse_rows, picks,
-        natural, load_inside, begun, begun_natural,
+    loads_rows = up(rows + chunk, 16)
+
+    def prepare(
+        load, inverse, basis_in, places, own_table,
+        natural, right, tau, weighted, spread, own_hot, basis, picks, load_inside, begun,
     ):
         order = places[0:1, :]
-        surface = one_hot_rows(as_column(order), nodes)
         across = one_hot_columns(order, nodes)
         for i, j in pairs:
             natural[pl.ds((i * n + j) * n, n), :] = load[i, j]
         for index, (i, j) in enumerate(inner_pairs):
             load_inside[pl.ds(index * deep, deep), :] = load[i, j, pl.ds(1, deep), :]
         begun[...] = dot(inverse[0, 0, 0], load_inside[...])
-        tau = jnp.sum(load_inside[...] * begun[...], axis=0, keepdims=True)
-        begun_natural[...] = jnp.zeros_like(begun_natural)
+        tau[...] = jnp.broadcast_to(
+            jnp.sum(load_inside[...] * begun[...], axis=0, keepdims=True), (8, lanes)
+        )
+        right[:, pl.ds(0, lanes)] = jnp.zeros((nodes, lanes), jnp.float32)
         for index, (i, j) in enumerate(inner_pairs):
-            begun_natural[pl.ds((i * n + j) * n + 1, deep), :] = begun[pl.ds(index * deep, deep), :]
-        basis = jnp.concatenate(
+            right[pl.ds((i * n + j) * n + 1, deep), pl.ds(0, lanes)] = begun[
+                pl.ds(index * deep, deep), :
+            ]
+        basis[...] = jnp.concatenate(
             [basis_in[0, 0, 0], jnp.zeros((chunk - primal, nodes), jnp.float32)], axis=0
         )
-        weighted[...] = pick(basis, across) * places[1:2, :]
+        right[:, pl.ds(lanes, 128)] = jnp.concatenate(
+            [basis[...], jnp.zeros((128 - chunk, nodes), jnp.float32)], axis=0
+        ).T
+        weighted[...] = pick(basis[...], across) * places[1:2, :]
         me = own_table[pl.ds(lax.axis_index(AXES), 1), :]
         lists = [me[:, s : s + up(size, 128)] for s, size in zip(starts, sizes)]
         own = one_hot_rows(as_column(lists[0])[:chunk], coarse)
+        own_hot[...] = own.astype(jnp.float32)
+        spread[...] = pick(weighted[...], own, (0, 0))
 
         def match(name, targets, sources, size):
             found = jnp.where(targets == sources, 1.0, 0.0)
             lane = lax.broadcasted_iota(jnp.int32, found.shape, 1)
-            found = jnp.where(lane < size, found, 0.0)
-            picks[keep.place(name), pl.ds(0, found.shape[1])] = found
-            return found
-
-        to_column = match("to_column", as_column(lists[1])[:column], lists[0], chunk)
+            picks[keep.place(name), pl.ds(0, found.shape[1])] = jnp.where(lane < size, found, 0.0)
+
+        match("to_column", as_column(lists[1])[:column], lists[0], chunk)
         match("to_slab", as_column(lists[3])[:slab], lists[2], sizes[2])
         every = lax.broadcasted_iota(jnp.int32, (coarse, 1), 0).astype(jnp.float32)
         match("to_all", every, lists[4], sizes[4])
-        spread = pick(weighted[...], own, (0, 0))
-        wide = jnp.concatenate([basis, jnp.zeros((128 - chunk, nodes), jnp.float32)], axis=0).T
-        images = dot(matrix[0, 0, 0], jnp.concatenate([begun_natural[...], wide], axis=1))
-        both = jnp.concatenate([natural[...], natural[...] - images[:, :lanes]], axis=1)
-        both = pick(surface, both)
-        condensed = both[:, lanes:]
-        for name, value in (
-            ("load", both[:, :lanes]), ("condensed", condensed),
-            ("tau", jnp.broadcast_to(tau, (8, lanes))),
-        ):
-            bank[keep.place(name), :] = value
-        fields = [condensed] + [spread[:, s : s + lanes] for s in range(0, coarse, lanes)]
+
+    def part(loads, chosen, *extra):
+        mapped = pick(chosen[:, :chunk].astype(jnp.bfloat16), loads)
+        fill = jnp.zeros((PLAIN - sum(rows.shape[0] for rows in extra), lanes), jnp.float32)
+        return cat([mapped, *extra, fill])
+
+    moves = runs_of(list(layout.order))
+    empty = runs_of([row if node < 0 else -1 for row, node in enumerate(layout.order)])
+
+    def start(
+        matrix, right, natural, tau, spread, own_hot, basis, picks,
+        bank, rings, flats, coarse_rows, rest,
+    ):
+        images = dot(matrix[0, 0, 0], right[...])
+        coarse_local = dot(basis[...], images[:, lanes:])
+        rest[...] = natural[...] - images[:, :lanes]
+        bank[keep.place("tau"), :] = tau[...]
+        for name, source in (("load", natural), ("condensed", rest)):
+            first = keep.slots[name][1]
+            for _, row, size, _ in empty:
+                bank[pl.ds(first + row, size), :] = jnp.zeros((size, lanes), jnp.float32)
+            for at, row, size, stride in moves:
+                bank[pl.ds(first + at, size), :] = source[pl.ds(row, size, stride), :]
+        fields = [bank[keep.place("condensed"), :]]
+        fields += [spread[:, s : s + lanes] for s in range(0, coarse, lanes)]
         ringed, flats[...] = packed(layout, *fields)
-        coarse_local = dot(basis, images[:, lanes:])
-        spread_rows = pick(coarse_local[:, :chunk], own)
+        spread_rows = pick(coarse_local[:, :chunk], own_hot[...].astype(jnp.bfloat16))
         coarse_rows[...] = spread_rows
         if rides:
-            ridden = part(spread_rows, to_column)
+            ridden = part(spread_rows, picks[keep.place("to_column"), :])
         else:
             ridden = jnp.zeros((column + PLAIN, lanes), jnp.float32)
         rings[...] = cat([ringed, ridden])
 
+    def begin(
+        load, matrix, inverse, basis_in, places, own_table,
+        bank, rings, flats, weighted, coarse_rows, picks,
+        natural, right, tau, spread, own_hot, basis, load_inside, begun, rest,
+    ):
+        prepare(
+            load, inverse, basis_in, places, own_table, natural, right, tau, weighted, spread, own_hot,
+            basis, picks, load_inside, begun,
+        )
+        start(
+            matrix, right, natural, tau, spread, own_hot, basis, picks, bank, rings, flats,
+            coarse_rows, rest,
+        )
+
     bank, rings, flats, weighted, coarse_rows, picks = call(
-        start,
+        begin,
         (element_load, local_matrix, dirichlet_inverse, coarse_basis, places, own_table),
         (
             floats(keep.rows["bank"], lanes), floats(count * ring_rows + column + PLAIN, lanes),
-            floats(count * (rows - ring_rows), lanes), floats(chunk, rows),
-            floats(chunk, coarse), floats(keep.rows["picks"], pick_lanes),
+            floats(count * (rows - ring_rows), lanes), floats(chunk, rows), floats(chunk, coarse),
+            floats(keep.rows["picks"], pick_lanes),
         ),
         scratch=[
-            VMEM((nodes, lanes), jnp.float32), VMEM((inside, lanes), jnp.float32),
-            VMEM((inside, lanes), jnp.float32), VMEM((nodes, lanes), jnp.float32),
+            VMEM(shape, jnp.float32)
+            for shape in (
+                (nodes, lanes), (nodes, lanes + 128), (8, lanes), (rows, coarse), (chunk, coarse),
+                (chunk, nodes), (inside, lanes), (inside, lanes), (nodes, lanes),
+            )
         ],
     )
-    element_load, local_matrix, dirichlet_inverse = lax.optimization_barrier(
-        (element_load, local_matrix, dirichlet_inverse)
-    )
-
     keep.arrays.update(bank=bank, picks=picks)
 
-    def reorder(neumann, places):
+    def reorder(neumann, places, weighted):
         order, share = places[0:1, :], places[1:2, :]
         across = one_hot_columns(order, nodes)
         surface = one_hot_rows(as_column(order), nodes)
-        return pick(surface, pick(neumann[0, 0, 0], across)) * as_column(share) * share
-
-    def condense(matrix, inverse, places, weighted, out):
-        places = places[...]
-        order = places[0:1, :]
-        picked = pick(matrix[0, 0, 0], one_hot_columns(order, nodes))
-        surface = one_hot_rows(as_column(order), nodes)
+        scaled = pick(surface, pick(neumann[0, 0, 0], across)) * as_column(share) * share
+        fill = jnp.zeros((loads_rows - rows - chunk, rows), jnp.float32)
+        return stacked(jnp.concatenate([scaled, weighted, fill], axis=0))
+
+    def surface_columns(matrix, places):
+        return pick(matrix[0, 0, 0], one_hot_columns(places[0:1, :], nodes))
+
+    def condense(picked, inverse, places, schur, out):
+        picked, places = picked[...], places[...]
+        surface = one_hot_rows(as_column(places[0:1, :]), nodes)
         within = pick(surface, picked)
         coupling = jnp.concatenate(
             [picked[(i * n + j) * n + 1 : (i * n + j) * n + 1 + deep] for i, j in inner_pairs], axis=0
         )
-        out[keep.place("coupling"), :] = coupling
-        out[keep.place("weighted"), :] = weighted[...]
-        out[keep.place("schur"), :] = within - dot(coupling, dot(inverse[0, 0, 0], coupling), (0, 0))
+        out[...] = coupling
+        schur[...] = stacked(within - dot(coupling, dot(inverse[0, 0, 0], coupling), (0, 0)))
+
+    def make_columns():
+        keep.arrays["columns"] = run(surface_columns, local_matrix, places, flops=FILL)
+        return ()
 
     def make_schur():
-        (keep.arrays["matrices"],) = call(
-            condense, (local_matrix, dirichlet_inverse, places, weighted),
-            (floats(keep.rows["matrices"], rows),), flops=FILL,
+        keep.arrays["schur"], keep.arrays["coupling"] = call(
+            condense, (keep.arrays.pop("columns"), dirichlet_inverse, places),
+            (jax.ShapeDtypeStruct((3 * rows, rows), jnp.bfloat16), floats(inside, rows)), flops=FILL,
         )
         return ()
 
     def make_scaled():
-        run(reorder, neumann_inverse, places, flops=FILL, keep=keep, store=("scaled",))
+        keep.arrays["scaled"] = run(reorder, neumann_inverse, places, weighted, flops=FILL)
         return ()
 
     step = coarse // PIECES
@@ -568,15 +655,21 @@
 
             keep.arrays["coarse"] = run(eliminated, keep.arrays["coarse"], flops=FILL)
 
-    def invert_early():
+    def invert_first():
         if rides:
-            invert(0, PIECES - 1)
+            invert(0, 1)
+        return ()
+
+    def invert_more():
+        if rides:
+            invert(1, PIECES - 1)
         return ()
 
     def finish_inverse():
         if rides:
             invert(PIECES - 1, PIECES)
-        keep.arrays["lift"] = run(dot, keep.arrays.pop("spread"), keep.arrays.pop("coarse"))
+        lifted = lambda spread, inverse: stacked(dot(spread, inverse))
+        keep.arrays["lift"] = run(lifted, keep.arrays.pop("spread"), keep.arrays.pop("coarse"))
         return ()
 
     def other_inverse():
@@ -588,55 +681,54 @@
         eye = jnp.eye(coarse, dtype=jnp.float32)
         return jax.scipy.linalg.cho_solve((factor, True), eye)
 
-    def neumann_step(field, scaled, weighted):
-        return dot(scaled, field), dot(weighted, field)
+    def neumann_step(field, scaled):
+        both = product(scaled, field)
+        return both[:rows], both[rows : rows + chunk]
 
     def sent(field, loads, chosen, *extra):
         ringed, flats = packed(layout, field)
         return cat([ringed, part(loads, chosen, *extra)]), flats
 
     def first(field, *rest):
-        pieces, (summed, _, weighted, scaled, chosen) = rest[:-5], rest[-5:]
-        mapped, loads = neumann_step(field, scaled, weighted)
+        pieces, (summed, _, scaled, chosen) = rest[:-4], rest[-4:]
+        mapped, loads = neumann_step(field, scaled)
         spread = jnp.concatenate(pieces, axis=1) if len(pieces) > 1 else pieces[0]
         return (spread, summed, *sent(mapped, loads, chosen), field)
 
     keep.arrays["spread"], keep.arrays["coarse"], rings, flats = assemble(
-        layout, count, shares, rings, flats, first, keep, ("weighted", "scaled", "to_column"),
-        ("residual",), make_schur, make_scaled,
+        layout, count, shares, rings, flats, first, keep, ("scaled", "to_column"),
+        ("residual",), make_columns, make_schur, make_scaled,
     )
     if not rides:
         keep.arrays["coarse"] = other_inverse()
 
     def apply_first(mapped, summed, _, condensed, tau, load, schur, lift):
-        field = mapped + dot(lift, summed)
-        image = dot(schur, field)
+        field = mapped + product(lift, summed)
+        image = product(schur, field)
         energy = tau[:1] + jnp.sum(condensed * field, axis=0, keepdims=True)
         curvature = tau[:1] + jnp.sum(field * image, axis=0, keepdims=True)
         fill = jnp.zeros((6, lanes), jnp.float32)
-        ringed, flats = packed(layout, image, load)
-        ridden = jnp.zeros((column + PLAIN, lanes), jnp.float32)
         sums = jnp.concatenate([energy, curvature, fill], axis=0)
-        return cat([ringed, ridden]), flats, field, image, sums
+        return (*packed(layout, image, load), field, image, sums)
 
     rings, flats = assemble(
         layout, 1, shares, rings, flats, apply_first, keep,
-        ("condensed", "tau", "load", "schur", "lift"), ("field0", "image0", "totals"), invert_early,
-        finish_inverse,
-    )
-
-    def second(image, load, summed, _, sums, scaled, weighted, chosen):
-        mapped, loads = neumann_step(image, scaled, weighted)
+        ("condensed", "tau", "load", "schur", "lift"), ("field0", "image0", "totals"), invert_first,
+        invert_more, finish_inverse,
+    )
+
+    def second(image, load, sums, scaled, chosen):
+        mapped, loads = neumann_step(image, scaled)
         return (*sent(mapped, loads, chosen, sums[:2]), image, load)
 
     rings, flats = assemble(
-        layout, 2, shares, rings, flats, second, keep,
-        ("totals", "scaled", "weighted", "to_column"), ("image0_sum", "load_sum"),
+        layout, 2, None, rings, flats, second, keep,
+        ("totals", "scaled", "to_column"), ("image0_sum", "load_sum"),
     )
 
     def apply_second(mapped, summed, totals, schur, condensed, tau, field0, image0, lift):
-        field = mapped + dot(lift, summed)
-        image = dot(schur, field)
+        field = mapped + product(lift, summed)
+        image = product(schur, field)
         step = totals[:1] / totals[1:2]
         rest = 1.0 - step
         direction = field0 - step * field
@@ -649,9 +741,8 @@
         )
         cross = rest * tau[:1] + jnp.sum(direction * image0, axis=0, keepdims=True)
         ringed, flats = packed(layout, image)
-        ridden = jnp.zeros((column, lanes), jnp.float32)
         fill = jnp.zeros((PLAIN - 3, lanes), jnp.float32)
-        return cat([ringed, ridden, energy, curvature, cross, fill]), flats, field, totals
+        return cat([ringed, energy, curvature, cross, fill]), flats, field, totals
 
     rings, flats = assemble(
         layout, 1, shares, rings, flats, apply_second, keep,
@@ -676,22 +767,22 @@
                     at = ((i - 1) * deep + j - 1) * deep
                     out[i, j, pl.ds(1, deep), :] = deep_rows[pl.ds(at, deep), :]
 
-    def solve_inside(bank, matrices, inverse, load, out, inner_load):
+    def solve_inside(bank, coupling, inverse, load, out, inner_load):
         for index, (i, j) in enumerate(inner_pairs):
             inner_load[pl.ds(index * deep, deep), :] = load[i, j, pl.ds(1, deep), :]
         fields = jnp.concatenate([bank[keep.place("field0"), :], bank[keep.place("field1"), :]], axis=1)
         loads = jnp.concatenate([inner_load[...], inner_load[...]], axis=1)
-        right = loads - dot(matrices[keep.place("coupling"), :], fields)
+        right = loads - dot(coupling[...], fields)
         out[...] = dot(inverse[0, 0, 0], right)
 
     def finish_inside():
         (keep.arrays["deep"],) = call(
-            solve_inside, (keep.arrays["bank"], keep.arrays["matrices"], dirichlet_inverse, element_load),
+            solve_inside, (keep.arrays["bank"], keep.arrays["coupling"], dirichlet_inverse, element_load),
             (floats(inside, 2 * lanes),), scratch=[VMEM((inside, lanes), jnp.float32)], flops=FILL,
         )
         return ()
 
-    def leftover(image1, _, sums, totals, field0, field1, image0, residual, load_sum):
+    def leftover(image1, sums, totals, field0, field1, image0, residual, load_sum):
         energy, curvature = totals[:1], totals[1:2]
         step = energy / curvature
         energy_next, curvature_next, cross = sums[:1], sums[1:2], sums[2:3]
@@ -707,8 +798,9 @@
         return first * field0 + second * field1, residual_surface, weights
 
     solution_surface, residual_surface, weights = assemble(
-        layout, 1, shares, rings, flats, leftover, keep,
-        ("totals", "field0", "field1", "image0_sum", "residual", "load_sum"), (), finish_inside,
+        layout, 1, (0, 0), rings, flats, leftover, keep,
+        ("totals", "field0", "field1", "image0_sum", "residual", "load_sum"), (), None,
+        finish_inside,
     )
 
     def place(solution_surface, residual_surface, weights, both, load, one, two, deep_rows):

time: 114 us -> 104 us (0.912)
  Pallas kernels: 36.4 us -> 30.3 us
  waiting for transfers between devices: 30.6 us -> 26.6 us
  local copies, waits for them, and re-layouts: 2.29 us -> 3.93 us
  starting transfers between devices: 43.1 us -> 41.8 us
    pallas_call x25 -> x26, Pallas kernels: 36.4 us -> 30.3 us  [call(): pl.pallas_call(body, out_shape=[jax.ShapeDtypeStruct(x.shape, x.dtype) fo...]
    ppermute x35 -> x33, waiting for transfers between devices: 30.6 us -> 26.6 us  [shifted(): lax.ppermute(value, axis, [(i, (i + step) % size) for i in range(size)])]
    unnamed x18 -> x12, local copies, waits for them, and re-layouts: 2.11 us -> 3.93 us
    ppermute x35 -> x33, starting transfers between devices: 43.1 us -> 41.8 us  [shifted(): lax.ppermute(value, axis, [(i, (i + step) % size) for i in range(size)])]
  transfers between devices with their start and end apart: 35 -> 33, of which waited for: 14 -> 13; matrix products, arithmetic and copies ran while one was open for 0% -> 0% of each run, Pallas kernels for 20% -> 18%
where the time goes in v4:
time: 104 us
  starting transfers between devices  41.8 us (40%)
  Pallas kernels  30.3 us (29%)
  waiting for transfers between devices  26.6 us (26%)
  local copies, waits for them, and re-layouts  3.93 us (4%)
    ppermute x33, starting transfers between devices, shifted(): lax.ppermute(value, axis, [(i, (i + step) % size) for i in range(size)])  41.8 us
    pallas_call x26, Pallas kernels, call(): pl.pallas_call(body, out_shape=[jax.ShapeDtypeStruct(x.shape, x.dtype) fo...  30.3 us
    ppermute x33, waiting for transfers between devices, shifted(): lax.ppermute(value, axis, [(i, (i + step) % size) for i in range(size)])  26.6 us
    unnamed x12, local copies, waits for them, and re-layouts  3.93 us
  transfers between devices with their start and end apart: 33, of which 13 were waited for; matrix products, arithmetic and copies ran while one was open for 0% of the time, Pallas kernels for 18%

profile of v4, /device:TPU:0, one launch (start us, length us, event | category | flops | bytes accessed | tf_op | source)
XLA Modules:
  0.0 103.6 jit_solution(6603768677580269173)
XLA Ops:
  2.6 1.8 %copy.97.matrix.refs_0_ = f32[1,1,1,729,729]{4,3,2,1,0:T(8,128)S(1)} copy(f32[1,1,1,729,729]{4,2,3,1,0:T(1,128)} %param.8) | data formatting | bytes 4251528 | tf_op args[1]
  4.5 4.8 %shard_map.86 = (f32[4016,128]{1,0:T(8,128)S(1)}, f32[608,128]{1,0:T(8,128)S(1)}, f32[224,128]{1,0:T(8,128)S(1)}, f32[24,400]{1,0:T(8,128)S(1)}, f32[24,128]{1,0:T(8,128)}, /*index=5*/f32[208,256]{1,0:T(8,128)S(1)}) custom-call(f32[9,9,9,128]{3,2,1,0:T(8,128)S(1)} %copy-done, f32[1,1,1,729,729]{4,3,2,1,0:T(8,128)S(1)} %copy.97.matrix.refs_0_, ...), custom_call_target="tpu_custom_call" | custom-call | flops 1000000 | bytes 5884888 | tf_op jit(solution)/shard_map/pallas_call | solution.py:35
  9.8 2.0 %shard_map.87.refs_5_ = f32[729,400]{1,0:T(8,128)S(1)} custom-call(f32[1,1,1,729,729]{4,3,2,1,0:T(8,128)S(1)} %copy.97.matrix.refs_0_, f32[8,400]{1,0:T(8,128)S(1)} %copy-done.1), custom_call_target="tpu_custom_call" | custom-call | flops 100000000 | bytes 3304964 | tf_op jit(solution)/shard_map/pallas_call | solution.py:35
  11.8 2.6 %collective-permute-start.1 = (f32[208,128]{1,0:T(8,128)S(1)}, f32[208,128]{1,0:T(8,128)S(1)}, u32[]{:S(2)}, u32[]{:S(2)}) collective-permute-start(f32[208,128]{1,0:T(8,128)S(1)} %get-tuple-element.136), channel_id=1, source_target_pairs={{0,2},{2,4},{4,6},{6,0},{1,3},{3,5},{5,7},{7,1},{8,10},{10,12},{12... | collective-permute-start | bytes 319496 | tf_op jit(solution)/shard_map/ppermute | solution.py:210
  14.4 2.1 %collective-permute-start.2 = (f32[208,128]{1,0:T(8,128)S(1)}, f32[208,128]{1,0:T(8,128)S(1)}, u32[]{:S(2)}, u32[]{:S(2)}) collective-permute-start(f32[208,128]{1,0:T(8,128)S(1)} %get-tuple-element.137), channel_id=1, source_target_pairs={{0,6},{2,0},{4,2},{6,4},{1,7},{3,1},{5,3},{7,5},{8,14},{10,8},{12,... | collective-permute-start | bytes 319496 | tf_op jit(solution)/shard_map/ppermute | solution.py:210
  17.5 4.2 %shard_map.89 = (bf16[1200,400]{1,0:T(8,128)(2,1)S(1)}, f32[343,400]{1,0:T(8,128)S(1)}) custom-call(f32[729,400]{1,0:T(8,128)S(1)} %get-tuple-element.141.picked, f32[1,1,1,343,343]{4,3,2,1,0:T(8,128)S(1)} %copy.98.inverse, f32[8,400]{1,0:T(8,128)S(1)} %copy-done.1), custom_call_target="tpu_custom_call" | custom-call | flops 100000000 | bytes 4118596 | tf_op jit(solution)/shard_map/pallas_call | solution.py:35
  28.0 3.1 %shard_map.91.refs_8_ = bf16[1296,400]{1,0:T(8,128)(2,1)S(1)} custom-call(f32[1,1,1,729,729]{4,3,2,1,0:T(8,128)S(1)} %copy.102.refs_0_, f32[8,400]{1,0:T(8,128)S(1)} %copy-done.1, f32[24,400]{1,0:T(8,128)S(1)} %get-tuple-element.151.refs_2_), custom_call_target="tpu_custom_call" | custom-call | flops 100000000 | bytes 4250564 | tf_op jit(solution)/shard_map/pallas_call | solution.py:35
  34.9 3.8 %collective-permute-start.9 = (f32[120,128]{1,0:T(8,128)S(1)}, f32[120,128]{1,0:T(8,128)S(1)}, u32[]{:S(2)}, u32[]{:S(2)}) collective-permute-start(f32[120,128]{1,0:T(8,128)S(1)} %get-tuple-element.162), channel_id=1, source_target_pairs={{0,6},{2,0},{4,2},{6,4},{1,7},{3,1},{5,3},{7,5},{8,14},{10,8},{12,... | collective-permute-start | bytes 184328 | tf_op jit(solution)/shard_map/ppermute | solution.py:210
  40.4 1.8 %shard_map.96.refs_10_ = f32[128,128]{1,0:T(8,128)S(1)} custom-call(f32[128,128]{1,0:T(8,128)S(1)} %shard_map.95.refs_0_), custom_call_target="tpu_custom_call" | custom-call | flops 100000000 | bytes 131072 | tf_op jit(solution)/shard_map/pallas_call | solution.py:35
  47.0 1.8 %shard_map.98.refs_1_ = f32[128,128]{1,0:T(8,128)S(1)} custom-call(f32[128,128]{1,0:T(8,128)S(1)} %get-tuple-element.180.refs_0_), custom_call_target="tpu_custom_call" | custom-call | flops 100000000 | bytes 131072 | tf_op jit(solution)/shard_map/pallas_call | solution.py:35
  53.5 3.8 %collective-permute-start.16 = (f32[176,128]{1,0:T(8,128)S(1)}, f32[176,128]{1,0:T(8,128)S(1)}, u32[]{:S(2)}, u32[]{:S(2)}) collective-permute-start(f32[176,128]{1,0:T(8,128)S(1)} %get-tuple-element.190), channel_id=1, source_target_pairs={{0,6},{2,0},{4,2},{6,4},{1,7},{3,1},{5,3},{7,5},{8,14},{10,8},{12,... | collective-permute-start | bytes 270344 | tf_op jit(solution)/shard_map/ppermute | solution.py:210
  57.4 3.5 %collective-permute-done.15.refs_0_ = f32[176,128]{1,0:T(8,128)S(1)} collective-permute-done((f32[176,128]{1,0:T(8,128)S(1)}, f32[176,128]{1,0:T(8,128)S(1)}, u32[]{:S(2)}, u32[]{:S(2)}) %collective-permute-start.15) | collective-permute-done | bytes 90144 | tf_op jit(solution)/shard_map/ppermute | solution.py:210
  61.8 2.1 %collective-permute-start.18 = (f32[176,128]{1,0:T(8,128)S(1)}, f32[176,128]{1,0:T(8,128)S(1)}, u32[]{:S(2)}, u32[]{:S(2)}) collective-permute-start(f32[176,128]{1,0:T(8,128)S(1)} %get-tuple-element.198), channel_id=1, source_target_pairs={{0,24},{8,0},{16,8},{24,16},{1,25},{9,1},{17,9},{25,17},{2,26},{10... | collective-permute-start | bytes 270344 | tf_op jit(solution)/shard_map/ppermute | solution.py:210
  63.9 2.5 %collective-permute-done.17.refs_0_ = f32[176,128]{1,0:T(8,128)S(1)} collective-permute-done((f32[176,128]{1,0:T(8,128)S(1)}, f32[176,128]{1,0:T(8,128)S(1)}, u32[]{:S(2)}, u32[]{:S(2)}) %collective-permute-start.17) | collective-permute-done | bytes 90144 | tf_op jit(solution)/shard_map/ppermute | solution.py:210
  68.7 2.1 %collective-permute-start.20 = (f32[120,128]{1,0:T(8,128)S(1)}, f32[120,128]{1,0:T(8,128)S(1)}, u32[]{:S(2)}, u32[]{:S(2)}) collective-permute-start(f32[120,128]{1,0:T(8,128)S(1)} %get-tuple-element.213), channel_id=1, source_target_pairs={{0,2},{2,4},{4,6},{6,0},{1,3},{3,5},{5,7},{7,1},{8,10},{10,12},{12... | collective-permute-start | bytes 184328 | tf_op jit(solution)/shard_map/ppermute | solution.py:210
  70.8 1.8 %collective-permute-start.21 = (f32[120,128]{1,0:T(8,128)S(1)}, f32[120,128]{1,0:T(8,128)S(1)}, u32[]{:S(2)}, u32[]{:S(2)}) collective-permute-start(f32[120,128]{1,0:T(8,128)S(1)} %get-tuple-element.214), channel_id=1, source_target_pairs={{0,6},{2,0},{4,2},{6,4},{1,7},{3,1},{5,3},{7,5},{8,14},{10,8},{12,... | collective-permute-start | bytes 184328 | tf_op jit(solution)/shard_map/ppermute | solution.py:210
  72.7 4.5 %collective-permute-done.22.refs_3_ = f32[32,128]{1,0:T(8,128)S(1)} collective-permute-done((f32[32,128]{1,0:T(8,128)S(1)}, f32[32,128]{1,0:T(8,128)S(1)}, u32[]{:S(2)}, u32[]{:S(2)}) %collective-permute-start.22) | collective-permute-done | bytes 16416 | tf_op jit(solution)/shard_map/ppermute | solution.py:210
  77.4 2.0 %collective-permute-start.23 = (f32[152,128]{1,0:T(8,128)S(1)}, f32[152,128]{1,0:T(8,128)S(1)}, u32[]{:S(2)}, u32[]{:S(2)}) collective-permute-start(f32[152,128]{1,0:T(8,128)S(1)} %get-tuple-element.222), channel_id=1, source_target_pairs={{0,8},{8,16},{16,24},{24,0},{1,9},{9,17},{17,25},{25,1},{2,10},{10... | collective-permute-start | bytes 233480 | tf_op jit(solution)/shard_map/ppermute | solution.py:210
  81.9 2.5 %collective-permute-done.25.refs_3_ = f32[64,128]{1,0:T(8,128)S(1)} collective-permute-done((f32[64,128]{1,0:T(8,128)S(1)}, f32[64,128]{1,0:T(8,128)S(1)}, u32[]{:S(2)}, u32[]{:S(2)}) %collective-permute-start.25) | collective-permute-done | bytes 32800 | tf_op jit(solution)/shard_map/ppermute | solution.py:210
  87.4 3.6 %collective-permute-start.28 = (f32[96,128]{1,0:T(8,128)S(1)}, f32[96,128]{1,0:T(8,128)S(1)}, u32[]{:S(2)}, u32[]{:S(2)}) collective-permute-start(f32[96,128]{1,0:T(8,128)S(1)} %get-tuple-element.240), channel_id=1, source_target_pairs={{0,6},{2,0},{4,2},{6,4},{1,7},{3,1},{5,3},{7,5},{8,14},{10,8},{12,... | collective-permute-start | bytes 147464 | tf_op jit(solution)/shard_map/ppermute | solution.py:210
  91.1 2.4 %shard_map.108.refs_10_ = f32[343,256]{1,0:T(8,128)S(1)} custom-call(f32[4016,128]{1,0:T(8,128)S(1)} %get-tuple-element.242.bank.refs_4_, f32[343,400]{1,0:T(8,128)S(1)} %get-tuple-element.245.coupling.refs_7_, f32[1,1,1,343,343]{4,3,2,1,0:T(8,128)S(1)} %copy.98.inverse, f32[9,9,9,128]{3,2,1,0:T(8,128)S(1)} %copy-done), custom_call_target="tpu_custom_call" | custom-call | flops 100000000 | bytes 3800068 | tf_op jit(solution)/shard_map/pallas_call | solution.py:35
  93.5 2.1 %collective-permute-done.29.refs_3_ = f32[8,128]{1,0:T(8,128)S(1)} collective-permute-done((f32[8,128]{1,0:T(8,128)S(1)}, f32[8,128]{1,0:T(8,128)S(1)}, u32[]{:S(2)}, u32[]{:S(2)}) %collective-permute-start.29) | collective-permute-done | bytes 4128 | tf_op jit(solution)/shard_map/ppermute | solution.py:210
  95.6 1.8 %collective-permute-start.30 = (f32[96,128]{1,0:T(8,128)S(1)}, f32[96,128]{1,0:T(8,128)S(1)}, u32[]{:S(2)}, u32[]{:S(2)}) collective-permute-start(f32[96,128]{1,0:T(8,128)S(1)} %get-tuple-element.248), channel_id=1, source_target_pairs={{0,8},{8,16},{16,24},{24,0},{1,9},{9,17},{17,25},{25,1},{2,10},{10... | collective-permute-start | bytes 147464 | tf_op jit(solution)/shard_map/ppermute | solution.py:210
  100.1 2.1 %collective-permute-done.32.refs_3_ = f32[8,128]{1,0:T(8,128)S(1)} collective-permute-done((f32[8,128]{1,0:T(8,128)S(1)}, f32[8,128]{1,0:T(8,128)S(1)}, u32[]{:S(2)}, u32[]{:S(2)}) %collective-permute-start.32) | collective-permute-done | bytes 4128 | tf_op jit(solution)/shard_map/ppermute | solution.py:210
  (80 shorter events, 37.9 us)
Async XLA Ops:
  11.8 11.3 %collective-permute-start.1 = (f32[208,128]{1,0:T(8,128)S(1)}, f32[208,128]{1,0:T(8,128)S(1)}, u32[]{:S(2)}, u32[]{:S(2)}) collective-permute-start(f32[208,128]{1,0:T(8,128)S(1)} %get-tuple-element.136), channel_id=1, source_target_pairs={{0,2},{2,4},{4,6},{6,0},{1,3},{3,5},{5,7},{7,1},{8,10},{10,12},{12... | collective-permute-start | bytes 319496 | tf_op jit(solution)/shard_map/ppermute | solution.py:210
  14.4 8.7 %collective-permute-start.2 = (f32[208,128]{1,0:T(8,128)S(1)}, f32[208,128]{1,0:T(8,128)S(1)}, u32[]{:S(2)}, u32[]{:S(2)}) collective-permute-start(f32[208,128]{1,0:T(8,128)S(1)} %get-tuple-element.137), channel_id=1, source_target_pairs={{0,6},{2,0},{4,2},{6,4},{1,7},{3,1},{5,3},{7,5},{8,14},{10,8},{12,... | collective-permute-start | bytes 319496 | tf_op jit(solution)/shard_map/ppermute | solution.py:210
  16.5 6.6 %collective-permute-start.3 = (f32[32,128]{1,0:T(8,128)S(1)}, f32[32,128]{1,0:T(8,128)S(1)}, u32[]{:S(2)}, u32[]{:S(2)}) collective-permute-start(f32[32,128]{1,0:T(8,128)S(1)} %get-tuple-element.138.refs_2_), channel_id=1, source_target_pairs={{0,4},{2,6},{4,0},{6,2},{1,5},{3,7},{5,1},{7,3},{8,12},{10,14},{12... | collective-permute-start | bytes 49160 | tf_op jit(solution)/shard_map/ppermute | solution.py:210
  23.3 7.8 %collective-permute-start.4 = (f32[240,128]{1,0:T(8,128)S(1)}, f32[240,128]{1,0:T(8,128)S(1)}, u32[]{:S(2)}, u32[]{:S(2)}) collective-permute-start(f32[240,128]{1,0:T(8,128)S(1)} %get-tuple-element.144), channel_id=1, source_target_pairs={{0,8},{8,16},{16,24},{24,0},{1,9},{9,17},{17,25},{25,1},{2,10},{10... | collective-permute-start | bytes 368648 | tf_op jit(solution)/shard_map/ppermute | solution.py:210
  24.9 7.4 %collective-permute-start.5 = (f32[240,128]{1,0:T(8,128)S(1)}, f32[240,128]{1,0:T(8,128)S(1)}, u32[]{:S(2)}, u32[]{:S(2)}) collective-permute-start(f32[240,128]{1,0:T(8,128)S(1)} %get-tuple-element.145), channel_id=1, source_target_pairs={{0,24},{8,0},{16,8},{24,16},{1,25},{9,1},{17,9},{25,17},{2,26},{10... | collective-permute-start | bytes 368648 | tf_op jit(solution)/shard_map/ppermute | solution.py:210
  26.3 4.8 %collective-permute-start.6 = (f32[64,128]{1,0:T(8,128)S(1)}, f32[64,128]{1,0:T(8,128)S(1)}, u32[]{:S(2)}, u32[]{:S(2)}) collective-permute-start(f32[64,128]{1,0:T(8,128)S(1)} %get-tuple-element.146.refs_2_), channel_id=1, source_target_pairs={{0,16},{8,24},{16,0},{24,8},{1,17},{9,25},{17,1},{25,9},{2,18},{10... | collective-permute-start | bytes 98312 | tf_op jit(solution)/shard_map/ppermute | solution.py:210
  34.8 8.5 %collective-permute-start.8 = (f32[120,128]{1,0:T(8,128)S(1)}, f32[120,128]{1,0:T(8,128)S(1)}, u32[]{:S(2)}, u32[]{:S(2)}) collective-permute-start(f32[120,128]{1,0:T(8,128)S(1)} %get-tuple-element.161), channel_id=1, source_target_pairs={{0,2},{2,4},{4,6},{6,0},{1,3},{3,5},{5,7},{7,1},{8,10},{10,12},{12... | collective-permute-start | bytes 184328 | tf_op jit(solution)/shard_map/ppermute | solution.py:210
  34.9 8.4 %collective-permute-start.9 = (f32[120,128]{1,0:T(8,128)S(1)}, f32[120,128]{1,0:T(8,128)S(1)}, u32[]{:S(2)}, u32[]{:S(2)}) collective-permute-start(f32[120,128]{1,0:T(8,128)S(1)} %get-tuple-element.162), channel_id=1, source_target_pairs={{0,6},{2,0},{4,2},{6,4},{1,7},{3,1},{5,3},{7,5},{8,14},{10,8},{12,... | collective-permute-start | bytes 184328 | tf_op jit(solution)/shard_map/ppermute | solution.py:210
  38.7 4.6 %collective-permute-start.10 = (f32[32,128]{1,0:T(8,128)S(1)}, f32[32,128]{1,0:T(8,128)S(1)}, u32[]{:S(2)}, u32[]{:S(2)}) collective-permute-start(f32[32,128]{1,0:T(8,128)S(1)} %get-tuple-element.163.refs_2_), channel_id=1, source_target_pairs={{0,4},{2,6},{4,0},{6,2},{1,5},{3,7},{5,1},{7,3},{8,12},{10,14},{12... | collective-permute-start | bytes 49160 | tf_op jit(solution)/shard_map/ppermute | solution.py:210
  43.5 6.9 %collective-permute-start.11 = (f32[152,128]{1,0:T(8,128)S(1)}, f32[152,128]{1,0:T(8,128)S(1)}, u32[]{:S(2)}, u32[]{:S(2)}) collective-permute-start(f32[152,128]{1,0:T(8,128)S(1)} %get-tuple-element.171), channel_id=1, source_target_pairs={{0,8},{8,16},{16,24},{24,0},{1,9},{9,17},{17,25},{25,1},{2,10},{10... | collective-permute-start | bytes 233480 | tf_op jit(solution)/shard_map/ppermute | solution.py:210
  45.1 5.4 %collective-permute-start.12 = (f32[152,128]{1,0:T(8,128)S(1)}, f32[152,128]{1,0:T(8,128)S(1)}, u32[]{:S(2)}, u32[]{:S(2)}) collective-permute-start(f32[152,128]{1,0:T(8,128)S(1)} %get-tuple-element.172), channel_id=1, source_target_pairs={{0,24},{8,0},{16,8},{24,16},{1,25},{9,1},{17,9},{25,17},{2,26},{10... | collective-permute-start | bytes 233480 | tf_op jit(solution)/shard_map/ppermute | solution.py:210
  53.5 7.4 %collective-permute-start.15 = (f32[176,128]{1,0:T(8,128)S(1)}, f32[176,128]{1,0:T(8,128)S(1)}, u32[]{:S(2)}, u32[]{:S(2)}) collective-permute-start(f32[176,128]{1,0:T(8,128)S(1)} %get-tuple-element.189), channel_id=1, source_target_pairs={{0,2},{2,4},{4,6},{6,0},{1,3},{3,5},{5,7},{7,1},{8,10},{10,12},{12... | collective-permute-start | bytes 270344 | tf_op jit(solution)/shard_map/ppermute | solution.py:210
  53.5 7.3 %collective-permute-start.16 = (f32[176,128]{1,0:T(8,128)S(1)}, f32[176,128]{1,0:T(8,128)S(1)}, u32[]{:S(2)}, u32[]{:S(2)}) collective-permute-start(f32[176,128]{1,0:T(8,128)S(1)} %get-tuple-element.190), channel_id=1, source_target_pairs={{0,6},{2,0},{4,2},{6,4},{1,7},{3,1},{5,3},{7,5},{8,14},{10,8},{12,... | collective-permute-start | bytes 270344 | tf_op jit(solution)/shard_map/ppermute | solution.py:210
  61.0 5.5 %collective-permute-start.17 = (f32[176,128]{1,0:T(8,128)S(1)}, f32[176,128]{1,0:T(8,128)S(1)}, u32[]{:S(2)}, u32[]{:S(2)}) collective-permute-start(f32[176,128]{1,0:T(8,128)S(1)} %get-tuple-element.197), channel_id=1, source_target_pairs={{0,8},{8,16},{16,24},{24,0},{1,9},{9,17},{17,25},{25,1},{2,10},{10... | collective-permute-start | bytes 270344 | tf_op jit(solution)/shard_map/ppermute | solution.py:210
  61.8 4.7 %collective-permute-start.18 = (f32[176,128]{1,0:T(8,128)S(1)}, f32[176,128]{1,0:T(8,128)S(1)}, u32[]{:S(2)}, u32[]{:S(2)}) collective-permute-start(f32[176,128]{1,0:T(8,128)S(1)} %get-tuple-element.198), channel_id=1, source_target_pairs={{0,24},{8,0},{16,8},{24,16},{1,25},{9,1},{17,9},{25,17},{2,26},{10... | collective-permute-start | bytes 270344 | tf_op jit(solution)/shard_map/ppermute | solution.py:210
  68.7 8.5 %collective-permute-start.20 = (f32[120,128]{1,0:T(8,128)S(1)}, f32[120,128]{1,0:T(8,128)S(1)}, u32[]{:S(2)}, u32[]{:S(2)}) collective-permute-start(f32[120,128]{1,0:T(8,128)S(1)} %get-tuple-element.213), channel_id=1, source_target_pairs={{0,2},{2,4},{4,6},{6,0},{1,3},{3,5},{5,7},{7,1},{8,10},{10,12},{12... | collective-permute-start | bytes 184328 | tf_op jit(solution)/shard_map/ppermute | solution.py:210
  70.8 6.4 %collective-permute-start.21 = (f32[120,128]{1,0:T(8,128)S(1)}, f32[120,128]{1,0:T(8,128)S(1)}, u32[]{:S(2)}, u32[]{:S(2)}) collective-permute-start(f32[120,128]{1,0:T(8,128)S(1)} %get-tuple-element.214), channel_id=1, source_target_pairs={{0,6},{2,0},{4,2},{6,4},{1,7},{3,1},{5,3},{7,5},{8,14},{10,8},{12,... | collective-permute-start | bytes 184328 | tf_op jit(solution)/shard_map/ppermute | solution.py:210
  72.6 4.6 %collective-permute-start.22 = (f32[32,128]{1,0:T(8,128)S(1)}, f32[32,128]{1,0:T(8,128)S(1)}, u32[]{:S(2)}, u32[]{:S(2)}) collective-permute-start(f32[32,128]{1,0:T(8,128)S(1)} %get-tuple-element.215.refs_2_), channel_id=1, source_target_pairs={{0,4},{2,6},{4,0},{6,2},{1,5},{3,7},{5,1},{7,3},{8,12},{10,14},{12... | collective-permute-start | bytes 49160 | tf_op jit(solution)/shard_map/ppermute | solution.py:210
  77.4 7.0 %collective-permute-start.23 = (f32[152,128]{1,0:T(8,128)S(1)}, f32[152,128]{1,0:T(8,128)S(1)}, u32[]{:S(2)}, u32[]{:S(2)}) collective-permute-start(f32[152,128]{1,0:T(8,128)S(1)} %get-tuple-element.222), channel_id=1, source_target_pairs={{0,8},{8,16},{16,24},{24,0},{1,9},{9,17},{17,25},{25,1},{2,10},{10... | collective-permute-start | bytes 233480 | tf_op jit(solution)/shard_map/ppermute | solution.py:210
  79.4 4.9 %collective-permute-start.24 = (f32[152,128]{1,0:T(8,128)S(1)}, f32[152,128]{1,0:T(8,128)S(1)}, u32[]{:S(2)}, u32[]{:S(2)}) collective-permute-start(f32[152,128]{1,0:T(8,128)S(1)} %get-tuple-element.223), channel_id=1, source_target_pairs={{0,24},{8,0},{16,8},{24,16},{1,25},{9,1},{17,9},{25,17},{2,26},{10... | collective-permute-start | bytes 233480 | tf_op jit(solution)/shard_map/ppermute | solution.py:210
  87.2 8.4 %collective-permute-start.27 = (f32[96,128]{1,0:T(8,128)S(1)}, f32[96,128]{1,0:T(8,128)S(1)}, u32[]{:S(2)}, u32[]{:S(2)}) collective-permute-start(f32[96,128]{1,0:T(8,128)S(1)} %get-tuple-element.239), channel_id=1, source_target_pairs={{0,2},{2,4},{4,6},{6,0},{1,3},{3,5},{5,7},{7,1},{8,10},{10,12},{12... | collective-permute-start | bytes 147464 | tf_op jit(solution)/shard_map/ppermute | solution.py:210
  87.4 8.1 %collective-permute-start.28 = (f32[96,128]{1,0:T(8,128)S(1)}, f32[96,128]{1,0:T(8,128)S(1)}, u32[]{:S(2)}, u32[]{:S(2)}) collective-permute-start(f32[96,128]{1,0:T(8,128)S(1)} %get-tuple-element.240), channel_id=1, source_target_pairs={{0,6},{2,0},{4,2},{6,4},{1,7},{3,1},{5,3},{7,5},{8,14},{10,8},{12,... | collective-permute-start | bytes 147464 | tf_op jit(solution)/shard_map/ppermute | solution.py:210
  95.6 6.6 %collective-permute-start.30 = (f32[96,128]{1,0:T(8,128)S(1)}, f32[96,128]{1,0:T(8,128)S(1)}, u32[]{:S(2)}, u32[]{:S(2)}) collective-permute-start(f32[96,128]{1,0:T(8,128)S(1)} %get-tuple-element.248), channel_id=1, source_target_pairs={{0,8},{8,16},{16,24},{24,0},{1,9},{9,17},{17,25},{25,1},{2,10},{10... | collective-permute-start | bytes 147464 | tf_op jit(solution)/shard_map/ppermute | solution.py:210
  97.4 4.8 %collective-permute-start.31 = (f32[96,128]{1,0:T(8,128)S(1)}, f32[96,128]{1,0:T(8,128)S(1)}, u32[]{:S(2)}, u32[]{:S(2)}) collective-permute-start(f32[96,128]{1,0:T(8,128)S(1)} %get-tuple-element.249), channel_id=1, source_target_pairs={{0,24},{8,0},{16,8},{24,16},{1,25},{9,1},{17,9},{25,17},{2,26},{10... | collective-permute-start | bytes 147464 | tf_op jit(solution)/shard_map/ppermute | solution.py:210
  (13 other events, 35.0 us)

commit v5 on v4

--- a/solution.py
+++ b/solution.py
@@ -11,7 +11,7 @@
 PALLAS = True
 LIMIT = 24 * 2**20
 VMEM = pltpu.VMEM
-PIECES = 4
+PIECES = 8
 PLAIN = 8
 FILL = 10**8
 
@@ -662,12 +662,12 @@
 
     def invert_more():
         if rides:
-            invert(1, PIECES - 1)
+            invert(1, PIECES - 2)
         return ()
 
     def finish_inverse():
         if rides:
-            invert(PIECES - 1, PIECES)
+            invert(PIECES - 2, PIECES)
         lifted = lambda spread, inverse: stacked(dot(spread, inverse))
         keep.arrays["lift"] = run(lifted, keep.arrays.pop("spread"), keep.arrays.pop("coarse"))
         return ()

time: 104 us -> 104 us (level)
    pallas_call x26 -> x30, Pallas kernels: 30.3 us -> 30.3 us  [call(): pl.pallas_call(body, out_shape=[jax.ShapeDtypeStruct(x.shape, x.dtype) fo...]
  transfers between devices with their start and end apart: 33 -> 33, of which waited for: 13 -> 15; matrix products, arithmetic and copies ran while one was open for 0% -> 0% of each run, Pallas kernels for 18% -> 18%
where the time goes in v5:
time: 104 us
  starting transfers between devices  41.8 us (40%)
  Pallas kernels  30.3 us (29%)
  waiting for transfers between devices  27 us (26%)
  local copies, waits for them, and re-layouts  3.93 us (4%)
    ppermute x33, starting transfers between devices, shifted(): lax.ppermute(value, axis, [(i, (i + step) % size) for i in range(size)])  41.8 us
    pallas_call x30, Pallas kernels, call(): pl.pallas_call(body, out_shape=[jax.ShapeDtypeStruct(x.shape, x.dtype) fo...  30.3 us
    ppermute x33, waiting for transfers between devices, shifted(): lax.ppermute(value, axis, [(i, (i + step) % size) for i in range(size)])  27 us
    unnamed x12, local copies, waits for them, and re-layouts  3.93 us
  transfers between devices with their start and end apart: 33, of which 15 were waited for; matrix products, arithmetic and copies ran while one was open for 0% of the time, Pallas kernels for 18%

profile of v5, /device:TPU:0, one launch (start us, length us, event | category | flops | bytes accessed | tf_op | source)
XLA Modules:
  0.0 103.9 jit_solution(18065902246835916915)
XLA Ops:
  2.6 1.8 %copy.97.matrix.refs_0_ = f32[1,1,1,729,729]{4,3,2,1,0:T(8,128)S(1)} copy(f32[1,1,1,729,729]{4,2,3,1,0:T(1,128)} %param.8) | data formatting | bytes 4251528 | tf_op args[1]
  4.5 4.8 %shard_map.86 = (f32[4016,128]{1,0:T(8,128)S(1)}, f32[608,128]{1,0:T(8,128)S(1)}, f32[224,128]{1,0:T(8,128)S(1)}, f32[24,400]{1,0:T(8,128)S(1)}, f32[24,128]{1,0:T(8,128)}, /*index=5*/f32[208,256]{1,0:T(8,128)S(1)}) custom-call(f32[9,9,9,128]{3,2,1,0:T(8,128)S(1)} %copy-done, f32[1,1,1,729,729]{4,3,2,1,0:T(8,128)S(1)} %copy.97.matrix.refs_0_, ...), custom_call_target="tpu_custom_call" | custom-call | flops 1000000 | bytes 5884888 | tf_op jit(solution)/shard_map/pallas_call | solution.py:35
  9.8 2.0 %shard_map.87.refs_5_ = f32[729,400]{1,0:T(8,128)S(1)} custom-call(f32[1,1,1,729,729]{4,3,2,1,0:T(8,128)S(1)} %copy.97.matrix.refs_0_, f32[8,400]{1,0:T(8,128)S(1)} %copy-done.1), custom_call_target="tpu_custom_call" | custom-call | flops 100000000 | bytes 3304964 | tf_op jit(solution)/shard_map/pallas_call | solution.py:35
  11.8 2.6 %collective-permute-start.1 = (f32[208,128]{1,0:T(8,128)S(1)}, f32[208,128]{1,0:T(8,128)S(1)}, u32[]{:S(2)}, u32[]{:S(2)}) collective-permute-start(f32[208,128]{1,0:T(8,128)S(1)} %get-tuple-element.136), channel_id=1, source_target_pairs={{0,2},{2,4},{4,6},{6,0},{1,3},{3,5},{5,7},{7,1},{8,10},{10,12},{12... | collective-permute-start | bytes 319496 | tf_op jit(solution)/shard_map/ppermute | solution.py:210
  14.4 2.1 %collective-permute-start.2 = (f32[208,128]{1,0:T(8,128)S(1)}, f32[208,128]{1,0:T(8,128)S(1)}, u32[]{:S(2)}, u32[]{:S(2)}) collective-permute-start(f32[208,128]{1,0:T(8,128)S(1)} %get-tuple-element.137), channel_id=1, source_target_pairs={{0,6},{2,0},{4,2},{6,4},{1,7},{3,1},{5,3},{7,5},{8,14},{10,8},{12,... | collective-permute-start | bytes 319496 | tf_op jit(solution)/shard_map/ppermute | solution.py:210
  17.5 4.2 %shard_map.89 = (bf16[1200,400]{1,0:T(8,128)(2,1)S(1)}, f32[343,400]{1,0:T(8,128)S(1)}) custom-call(f32[729,400]{1,0:T(8,128)S(1)} %get-tuple-element.141.picked, f32[1,1,1,343,343]{4,3,2,1,0:T(8,128)S(1)} %copy.98.inverse, f32[8,400]{1,0:T(8,128)S(1)} %copy-done.1), custom_call_target="tpu_custom_call" | custom-call | flops 100000000 | bytes 4118596 | tf_op jit(solution)/shard_map/pallas_call | solution.py:35
  23.3 1.5 %collective-permute-start.4 = (f32[240,128]{1,0:T(8,128)S(1)}, f32[240,128]{1,0:T(8,128)S(1)}, u32[]{:S(2)}, u32[]{:S(2)}) collective-permute-start(f32[240,128]{1,0:T(8,128)S(1)} %get-tuple-element.144), channel_id=1, source_target_pairs={{0,8},{8,16},{16,24},{24,0},{1,9},{9,17},{17,25},{25,1},{2,10},{10... | collective-permute-start | bytes 368648 | tf_op jit(solution)/shard_map/ppermute | solution.py:210
  28.0 3.1 %shard_map.91.refs_8_ = bf16[1296,400]{1,0:T(8,128)(2,1)S(1)} custom-call(f32[1,1,1,729,729]{4,3,2,1,0:T(8,128)S(1)} %copy.102.refs_0_, f32[8,400]{1,0:T(8,128)S(1)} %copy-done.1, f32[24,400]{1,0:T(8,128)S(1)} %get-tuple-element.151.refs_2_), custom_call_target="tpu_custom_call" | custom-call | flops 100000000 | bytes 4250564 | tf_op jit(solution)/shard_map/pallas_call | solution.py:35
  34.6 3.8 %collective-permute-start.9 = (f32[120,128]{1,0:T(8,128)S(1)}, f32[120,128]{1,0:T(8,128)S(1)}, u32[]{:S(2)}, u32[]{:S(2)}) collective-permute-start(f32[120,128]{1,0:T(8,128)S(1)} %get-tuple-element.162), channel_id=1, source_target_pairs={{0,6},{2,0},{4,2},{6,4},{1,7},{3,1},{5,3},{7,5},{8,14},{10,8},{12,... | collective-permute-start | bytes 184328 | tf_op jit(solution)/shard_map/ppermute | solution.py:210
  51.5 1.6 %collective-permute-done.14.refs_2_ = f32[576,128]{1,0:T(8,128)S(1)} collective-permute-done((f32[576,128]{1,0:T(8,128)S(1)}, f32[576,128]{1,0:T(8,128)S(1)}, u32[]{:S(2)}, u32[]{:S(2)}) %collective-permute-start.14) | collective-permute-done | bytes 294944 | tf_op jit(solution)/shard_map/ppermute | solution.py:210
  53.5 3.5 %collective-permute-start.16 = (f32[176,128]{1,0:T(8,128)S(1)}, f32[176,128]{1,0:T(8,128)S(1)}, u32[]{:S(2)}, u32[]{:S(2)}) collective-permute-start(f32[176,128]{1,0:T(8,128)S(1)} %get-tuple-element.190), channel_id=1, source_target_pairs={{0,6},{2,0},{4,2},{6,4},{1,7},{3,1},{5,3},{7,5},{8,14},{10,8},{12,... | collective-permute-start | bytes 270344 | tf_op jit(solution)/shard_map/ppermute | solution.py:210
  57.0 3.5 %collective-permute-done.15.refs_0_ = f32[176,128]{1,0:T(8,128)S(1)} collective-permute-done((f32[176,128]{1,0:T(8,128)S(1)}, f32[176,128]{1,0:T(8,128)S(1)}, u32[]{:S(2)}, u32[]{:S(2)}) %collective-permute-start.15) | collective-permute-done | bytes 90144 | tf_op jit(solution)/shard_map/ppermute | solution.py:210
  62.0 2.2 %collective-permute-start.18 = (f32[176,128]{1,0:T(8,128)S(1)}, f32[176,128]{1,0:T(8,128)S(1)}, u32[]{:S(2)}, u32[]{:S(2)}) collective-permute-start(f32[176,128]{1,0:T(8,128)S(1)} %get-tuple-element.198), channel_id=1, source_target_pairs={{0,24},{8,0},{16,8},{24,16},{1,25},{9,1},{17,9},{25,17},{2,26},{10... | collective-permute-start | bytes 270344 | tf_op jit(solution)/shard_map/ppermute | solution.py:210
  64.1 2.7 %collective-permute-done.17.refs_0_ = f32[176,128]{1,0:T(8,128)S(1)} collective-permute-done((f32[176,128]{1,0:T(8,128)S(1)}, f32[176,128]{1,0:T(8,128)S(1)}, u32[]{:S(2)}, u32[]{:S(2)}) %collective-permute-start.17) | collective-permute-done | bytes 90144 | tf_op jit(solution)/shard_map/ppermute | solution.py:210
  69.1 1.8 %collective-permute-start.20 = (f32[120,128]{1,0:T(8,128)S(1)}, f32[120,128]{1,0:T(8,128)S(1)}, u32[]{:S(2)}, u32[]{:S(2)}) collective-permute-start(f32[120,128]{1,0:T(8,128)S(1)} %get-tuple-element.213), channel_id=1, source_target_pairs={{0,2},{2,4},{4,6},{6,0},{1,3},{3,5},{5,7},{7,1},{8,10},{10,12},{12... | collective-permute-start | bytes 184328 | tf_op jit(solution)/shard_map/ppermute | solution.py:210
  70.9 2.1 %collective-permute-start.21 = (f32[120,128]{1,0:T(8,128)S(1)}, f32[120,128]{1,0:T(8,128)S(1)}, u32[]{:S(2)}, u32[]{:S(2)}) collective-permute-start(f32[120,128]{1,0:T(8,128)S(1)} %get-tuple-element.214), channel_id=1, source_target_pairs={{0,6},{2,0},{4,2},{6,4},{1,7},{3,1},{5,3},{7,5},{8,14},{10,8},{12,... | collective-permute-start | bytes 184328 | tf_op jit(solution)/shard_map/ppermute | solution.py:210
  73.0 4.6 %collective-permute-done.22.refs_3_ = f32[32,128]{1,0:T(8,128)S(1)} collective-permute-done((f32[32,128]{1,0:T(8,128)S(1)}, f32[32,128]{1,0:T(8,128)S(1)}, u32[]{:S(2)}, u32[]{:S(2)}) %collective-permute-start.22) | collective-permute-done | bytes 16416 | tf_op jit(solution)/shard_map/ppermute | solution.py:210
  77.8 1.8 %collective-permute-start.23 = (f32[152,128]{1,0:T(8,128)S(1)}, f32[152,128]{1,0:T(8,128)S(1)}, u32[]{:S(2)}, u32[]{:S(2)}) collective-permute-start(f32[152,128]{1,0:T(8,128)S(1)} %get-tuple-element.222), channel_id=1, source_target_pairs={{0,8},{8,16},{16,24},{24,0},{1,9},{9,17},{17,25},{25,1},{2,10},{10... | collective-permute-start | bytes 233480 | tf_op jit(solution)/shard_map/ppermute | solution.py:210
  82.3 2.4 %collective-permute-done.25.refs_3_ = f32[64,128]{1,0:T(8,128)S(1)} collective-permute-done((f32[64,128]{1,0:T(8,128)S(1)}, f32[64,128]{1,0:T(8,128)S(1)}, u32[]{:S(2)}, u32[]{:S(2)}) %collective-permute-start.25) | collective-permute-done | bytes 32800 | tf_op jit(solution)/shard_map/ppermute | solution.py:210
  87.6 3.8 %collective-permute-start.28 = (f32[96,128]{1,0:T(8,128)S(1)}, f32[96,128]{1,0:T(8,128)S(1)}, u32[]{:S(2)}, u32[]{:S(2)}) collective-permute-start(f32[96,128]{1,0:T(8,128)S(1)} %get-tuple-element.240), channel_id=1, source_target_pairs={{0,6},{2,0},{4,2},{6,4},{1,7},{3,1},{5,3},{7,5},{8,14},{10,8},{12,... | collective-permute-start | bytes 147464 | tf_op jit(solution)/shard_map/ppermute | solution.py:210
  91.4 2.4 %shard_map.112.refs_10_ = f32[343,256]{1,0:T(8,128)S(1)} custom-call(f32[4016,128]{1,0:T(8,128)S(1)} %get-tuple-element.242.bank.refs_4_, f32[343,400]{1,0:T(8,128)S(1)} %get-tuple-element.245.coupling.refs_7_, f32[1,1,1,343,343]{4,3,2,1,0:T(8,128)S(1)} %copy.98.inverse, f32[9,9,9,128]{3,2,1,0:T(8,128)S(1)} %copy-done), custom_call_target="tpu_custom_call" | custom-call | flops 100000000 | bytes 3800068 | tf_op jit(solution)/shard_map/pallas_call | solution.py:35
  93.8 2.1 %collective-permute-done.29.refs_3_ = f32[8,128]{1,0:T(8,128)S(1)} collective-permute-done((f32[8,128]{1,0:T(8,128)S(1)}, f32[8,128]{1,0:T(8,128)S(1)}, u32[]{:S(2)}, u32[]{:S(2)}) %collective-permute-start.29) | collective-permute-done | bytes 4128 | tf_op jit(solution)/shard_map/ppermute | solution.py:210
  95.9 1.7 %collective-permute-start.30 = (f32[96,128]{1,0:T(8,128)S(1)}, f32[96,128]{1,0:T(8,128)S(1)}, u32[]{:S(2)}, u32[]{:S(2)}) collective-permute-start(f32[96,128]{1,0:T(8,128)S(1)} %get-tuple-element.248), channel_id=1, source_target_pairs={{0,8},{8,16},{16,24},{24,0},{1,9},{9,17},{17,25},{25,1},{2,10},{10... | collective-permute-start | bytes 147464 | tf_op jit(solution)/shard_map/ppermute | solution.py:210
  100.4 2.1 %collective-permute-done.32.refs_3_ = f32[8,128]{1,0:T(8,128)S(1)} collective-permute-done((f32[8,128]{1,0:T(8,128)S(1)}, f32[8,128]{1,0:T(8,128)S(1)}, u32[]{:S(2)}, u32[]{:S(2)}) %collective-permute-start.32) | collective-permute-done | bytes 4128 | tf_op jit(solution)/shard_map/ppermute | solution.py:210
  (84 shorter events, 38.8 us)
Async XLA Ops:
  11.8 11.3 %collective-permute-start.1 = (f32[208,128]{1,0:T(8,128)S(1)}, f32[208,128]{1,0:T(8,128)S(1)}, u32[]{:S(2)}, u32[]{:S(2)}) collective-permute-start(f32[208,128]{1,0:T(8,128)S(1)} %get-tuple-element.136), channel_id=1, source_target_pairs={{0,2},{2,4},{4,6},{6,0},{1,3},{3,5},{5,7},{7,1},{8,10},{10,12},{12... | collective-permute-start | bytes 319496 | tf_op jit(solution)/shard_map/ppermute | solution.py:210
  14.4 8.7 %collective-permute-start.2 = (f32[208,128]{1,0:T(8,128)S(1)}, f32[208,128]{1,0:T(8,128)S(1)}, u32[]{:S(2)}, u32[]{:S(2)}) collective-permute-start(f32[208,128]{1,0:T(8,128)S(1)} %get-tuple-element.137), channel_id=1, source_target_pairs={{0,6},{2,0},{4,2},{6,4},{1,7},{3,1},{5,3},{7,5},{8,14},{10,8},{12,... | collective-permute-start | bytes 319496 | tf_op jit(solution)/shard_map/ppermute | solution.py:210
  16.5 6.6 %collective-permute-start.3 = (f32[32,128]{1,0:T(8,128)S(1)}, f32[32,128]{1,0:T(8,128)S(1)}, u32[]{:S(2)}, u32[]{:S(2)}) collective-permute-start(f32[32,128]{1,0:T(8,128)S(1)} %get-tuple-element.138.refs_2_), channel_id=1, source_target_pairs={{0,4},{2,6},{4,0},{6,2},{1,5},{3,7},{5,1},{7,3},{8,12},{10,14},{12... | collective-permute-start | bytes 49160 | tf_op jit(solution)/shard_map/ppermute | solution.py:210
  23.3 7.8 %collective-permute-start.4 = (f32[240,128]{1,0:T(8,128)S(1)}, f32[240,128]{1,0:T(8,128)S(1)}, u32[]{:S(2)}, u32[]{:S(2)}) collective-permute-start(f32[240,128]{1,0:T(8,128)S(1)} %get-tuple-element.144), channel_id=1, source_target_pairs={{0,8},{8,16},{16,24},{24,0},{1,9},{9,17},{17,25},{25,1},{2,10},{10... | collective-permute-start | bytes 368648 | tf_op jit(solution)/shard_map/ppermute | solution.py:210
  24.9 7.4 %collective-permute-start.5 = (f32[240,128]{1,0:T(8,128)S(1)}, f32[240,128]{1,0:T(8,128)S(1)}, u32[]{:S(2)}, u32[]{:S(2)}) collective-permute-start(f32[240,128]{1,0:T(8,128)S(1)} %get-tuple-element.145), channel_id=1, source_target_pairs={{0,24},{8,0},{16,8},{24,16},{1,25},{9,1},{17,9},{25,17},{2,26},{10... | collective-permute-start | bytes 368648 | tf_op jit(solution)/shard_map/ppermute | solution.py:210
  26.3 4.8 %collective-permute-start.6 = (f32[64,128]{1,0:T(8,128)S(1)}, f32[64,128]{1,0:T(8,128)S(1)}, u32[]{:S(2)}, u32[]{:S(2)}) collective-permute-start(f32[64,128]{1,0:T(8,128)S(1)} %get-tuple-element.146.refs_2_), channel_id=1, source_target_pairs={{0,16},{8,24},{16,0},{24,8},{1,17},{9,25},{17,1},{25,9},{2,18},{10... | collective-permute-start | bytes 98312 | tf_op jit(solution)/shard_map/ppermute | solution.py:210
  34.5 8.5 %collective-permute-start.8 = (f32[120,128]{1,0:T(8,128)S(1)}, f32[120,128]{1,0:T(8,128)S(1)}, u32[]{:S(2)}, u32[]{:S(2)}) collective-permute-start(f32[120,128]{1,0:T(8,128)S(1)} %get-tuple-element.161), channel_id=1, source_target_pairs={{0,2},{2,4},{4,6},{6,0},{1,3},{3,5},{5,7},{7,1},{8,10},{10,12},{12... | collective-permute-start | bytes 184328 | tf_op jit(solution)/shard_map/ppermute | solution.py:210
  34.6 8.4 %collective-permute-start.9 = (f32[120,128]{1,0:T(8,128)S(1)}, f32[120,128]{1,0:T(8,128)S(1)}, u32[]{:S(2)}, u32[]{:S(2)}) collective-permute-start(f32[120,128]{1,0:T(8,128)S(1)} %get-tuple-element.162), channel_id=1, source_target_pairs={{0,6},{2,0},{4,2},{6,4},{1,7},{3,1},{5,3},{7,5},{8,14},{10,8},{12,... | collective-permute-start | bytes 184328 | tf_op jit(solution)/shard_map/ppermute | solution.py:210
  38.4 4.6 %collective-permute-start.10 = (f32[32,128]{1,0:T(8,128)S(1)}, f32[32,128]{1,0:T(8,128)S(1)}, u32[]{:S(2)}, u32[]{:S(2)}) collective-permute-start(f32[32,128]{1,0:T(8,128)S(1)} %get-tuple-element.163.refs_2_), channel_id=1, source_target_pairs={{0,4},{2,6},{4,0},{6,2},{1,5},{3,7},{5,1},{7,3},{8,12},{10,14},{12... | collective-permute-start | bytes 49160 | tf_op jit(solution)/shard_map/ppermute | solution.py:210
  43.3 6.9 %collective-permute-start.11 = (f32[152,128]{1,0:T(8,128)S(1)}, f32[152,128]{1,0:T(8,128)S(1)}, u32[]{:S(2)}, u32[]{:S(2)}) collective-permute-start(f32[152,128]{1,0:T(8,128)S(1)} %get-tuple-element.171), channel_id=1, source_target_pairs={{0,8},{8,16},{16,24},{24,0},{1,9},{9,17},{17,25},{25,1},{2,10},{10... | collective-permute-start | bytes 233480 | tf_op jit(solution)/shard_map/ppermute | solution.py:210
  44.8 5.4 %collective-permute-start.12 = (f32[152,128]{1,0:T(8,128)S(1)}, f32[152,128]{1,0:T(8,128)S(1)}, u32[]{:S(2)}, u32[]{:S(2)}) collective-permute-start(f32[152,128]{1,0:T(8,128)S(1)} %get-tuple-element.172), channel_id=1, source_target_pairs={{0,24},{8,0},{16,8},{24,16},{1,25},{9,1},{17,9},{25,17},{2,26},{10... | collective-permute-start | bytes 233480 | tf_op jit(solution)/shard_map/ppermute | solution.py:210
  53.2 7.3 %collective-permute-start.15 = (f32[176,128]{1,0:T(8,128)S(1)}, f32[176,128]{1,0:T(8,128)S(1)}, u32[]{:S(2)}, u32[]{:S(2)}) collective-permute-start(f32[176,128]{1,0:T(8,128)S(1)} %get-tuple-element.189), channel_id=1, source_target_pairs={{0,2},{2,4},{4,6},{6,0},{1,3},{3,5},{5,7},{7,1},{8,10},{10,12},{12... | collective-permute-start | bytes 270344 | tf_op jit(solution)/shard_map/ppermute | solution.py:210
  53.5 7.5 %collective-permute-start.16 = (f32[176,128]{1,0:T(8,128)S(1)}, f32[176,128]{1,0:T(8,128)S(1)}, u32[]{:S(2)}, u32[]{:S(2)}) collective-permute-start(f32[176,128]{1,0:T(8,128)S(1)} %get-tuple-element.190), channel_id=1, source_target_pairs={{0,6},{2,0},{4,2},{6,4},{1,7},{3,1},{5,3},{7,5},{8,14},{10,8},{12,... | collective-permute-start | bytes 270344 | tf_op jit(solution)/shard_map/ppermute | solution.py:210
  61.1 5.7 %collective-permute-start.17 = (f32[176,128]{1,0:T(8,128)S(1)}, f32[176,128]{1,0:T(8,128)S(1)}, u32[]{:S(2)}, u32[]{:S(2)}) collective-permute-start(f32[176,128]{1,0:T(8,128)S(1)} %get-tuple-element.197), channel_id=1, source_target_pairs={{0,8},{8,16},{16,24},{24,0},{1,9},{9,17},{17,25},{25,1},{2,10},{10... | collective-permute-start | bytes 270344 | tf_op jit(solution)/shard_map/ppermute | solution.py:210
  62.0 4.9 %collective-permute-start.18 = (f32[176,128]{1,0:T(8,128)S(1)}, f32[176,128]{1,0:T(8,128)S(1)}, u32[]{:S(2)}, u32[]{:S(2)}) collective-permute-start(f32[176,128]{1,0:T(8,128)S(1)} %get-tuple-element.198), channel_id=1, source_target_pairs={{0,24},{8,0},{16,8},{24,16},{1,25},{9,1},{17,9},{25,17},{2,26},{10... | collective-permute-start | bytes 270344 | tf_op jit(solution)/shard_map/ppermute | solution.py:210
  69.1 8.5 %collective-permute-start.20 = (f32[120,128]{1,0:T(8,128)S(1)}, f32[120,128]{1,0:T(8,128)S(1)}, u32[]{:S(2)}, u32[]{:S(2)}) collective-permute-start(f32[120,128]{1,0:T(8,128)S(1)} %get-tuple-element.213), channel_id=1, source_target_pairs={{0,2},{2,4},{4,6},{6,0},{1,3},{3,5},{5,7},{7,1},{8,10},{10,12},{12... | collective-permute-start | bytes 184328 | tf_op jit(solution)/shard_map/ppermute | solution.py:210
  70.9 6.7 %collective-permute-start.21 = (f32[120,128]{1,0:T(8,128)S(1)}, f32[120,128]{1,0:T(8,128)S(1)}, u32[]{:S(2)}, u32[]{:S(2)}) collective-permute-start(f32[120,128]{1,0:T(8,128)S(1)} %get-tuple-element.214), channel_id=1, source_target_pairs={{0,6},{2,0},{4,2},{6,4},{1,7},{3,1},{5,3},{7,5},{8,14},{10,8},{12,... | collective-permute-start | bytes 184328 | tf_op jit(solution)/shard_map/ppermute | solution.py:210
  73.0 4.6 %collective-permute-start.22 = (f32[32,128]{1,0:T(8,128)S(1)}, f32[32,128]{1,0:T(8,128)S(1)}, u32[]{:S(2)}, u32[]{:S(2)}) collective-permute-start(f32[32,128]{1,0:T(8,128)S(1)} %get-tuple-element.215.refs_2_), channel_id=1, source_target_pairs={{0,4},{2,6},{4,0},{6,2},{1,5},{3,7},{5,1},{7,3},{8,12},{10,14},{12... | collective-permute-start | bytes 49160 | tf_op jit(solution)/shard_map/ppermute | solution.py:210
  77.8 6.9 %collective-permute-start.23 = (f32[152,128]{1,0:T(8,128)S(1)}, f32[152,128]{1,0:T(8,128)S(1)}, u32[]{:S(2)}, u32[]{:S(2)}) collective-permute-start(f32[152,128]{1,0:T(8,128)S(1)} %get-tuple-element.222), channel_id=1, source_target_pairs={{0,8},{8,16},{16,24},{24,0},{1,9},{9,17},{17,25},{25,1},{2,10},{10... | collective-permute-start | bytes 233480 | tf_op jit(solution)/shard_map/ppermute | solution.py:210
  79.6 5.1 %collective-permute-start.24 = (f32[152,128]{1,0:T(8,128)S(1)}, f32[152,128]{1,0:T(8,128)S(1)}, u32[]{:S(2)}, u32[]{:S(2)}) collective-permute-start(f32[152,128]{1,0:T(8,128)S(1)} %get-tuple-element.223), channel_id=1, source_target_pairs={{0,24},{8,0},{16,8},{24,16},{1,25},{9,1},{17,9},{25,17},{2,26},{10... | collective-permute-start | bytes 233480 | tf_op jit(solution)/shard_map/ppermute | solution.py:210
  87.5 8.4 %collective-permute-start.27 = (f32[96,128]{1,0:T(8,128)S(1)}, f32[96,128]{1,0:T(8,128)S(1)}, u32[]{:S(2)}, u32[]{:S(2)}) collective-permute-start(f32[96,128]{1,0:T(8,128)S(1)} %get-tuple-element.239), channel_id=1, source_target_pairs={{0,2},{2,4},{4,6},{6,0},{1,3},{3,5},{5,7},{7,1},{8,10},{10,12},{12... | collective-permute-start | bytes 147464 | tf_op jit(solution)/shard_map/ppermute | solution.py:210
  87.6 8.3 %collective-permute-start.28 = (f32[96,128]{1,0:T(8,128)S(1)}, f32[96,128]{1,0:T(8,128)S(1)}, u32[]{:S(2)}, u32[]{:S(2)}) collective-permute-start(f32[96,128]{1,0:T(8,128)S(1)} %get-tuple-element.240), channel_id=1, source_target_pairs={{0,6},{2,0},{4,2},{6,4},{1,7},{3,1},{5,3},{7,5},{8,14},{10,8},{12,... | collective-permute-start | bytes 147464 | tf_op jit(solution)/shard_map/ppermute | solution.py:210
  95.9 6.6 %collective-permute-start.30 = (f32[96,128]{1,0:T(8,128)S(1)}, f32[96,128]{1,0:T(8,128)S(1)}, u32[]{:S(2)}, u32[]{:S(2)}) collective-permute-start(f32[96,128]{1,0:T(8,128)S(1)} %get-tuple-element.248), channel_id=1, source_target_pairs={{0,8},{8,16},{16,24},{24,0},{1,9},{9,17},{17,25},{25,1},{2,10},{10... | collective-permute-start | bytes 147464 | tf_op jit(solution)/shard_map/ppermute | solution.py:210
  97.7 4.8 %collective-permute-start.31 = (f32[96,128]{1,0:T(8,128)S(1)}, f32[96,128]{1,0:T(8,128)S(1)}, u32[]{:S(2)}, u32[]{:S(2)}) collective-permute-start(f32[96,128]{1,0:T(8,128)S(1)} %get-tuple-element.249), channel_id=1, source_target_pairs={{0,24},{8,0},{16,8},{24,16},{1,25},{9,1},{17,9},{25,17},{2,26},{10... | collective-permute-start | bytes 147464 | tf_op jit(solution)/shard_map/ppermute | solution.py:210
  (13 other events, 34.7 us)
